TPU v7x, 32 devices: a whole 2x2x4 slice. The times are simulated.
32 devices in a mesh: space: 8 (over z, y), level: 4 (over x, core).
Axes of the slice: x: 2, y: 2, z: 4, core: 2. Of those that a mesh axis runs over, the one named last changes fastest.
Arguments:
- grid_latent: bfloat16 [4096, 512], P('space'), may hold values from -6 to 6
- mesh_latent: bfloat16 [4, 64, 512], P('level', 'space'), may hold values from -6 to 6
- grid_output_cotangent: bfloat16 [4096, 512], P('space'), may hold values from -6 to 6
- w_send: bfloat16 [512, 512], replicated, may hold values from -0.25 to 0.25
- w_recv: bfloat16 [512, 512], replicated, may hold values from -0.25 to 0.25
- output_weight: bfloat16 [512, 512], replicated, may hold values from -0.25 to 0.25
- hidden_layer_bias: float32 [512], replicated, may hold values from -4 to 4
- output_norm_gain: float32 [512], replicated, may hold values from 0.1 to 1.9
- edge_sender: int32 [4, 16384], P('level', 'space'), may hold values from 0 to 23
- edge_receiver: int32 [4, 16384], P('level', 'space'), may hold values from 0 to 511
- edge_live: int32 [4, 16384], P('level', 'space'), may hold values 0 or 1
Outputs:
- d_grid: float32 [4096, 512], P(('space', 'level'))
- d_mesh: float32 [4, 64, 512], P('level', 'space')
- d_w_send: bfloat16 [512, 512], replicated
- d_w_recv: bfloat16 [512, 512], replicated
- d_w_out: bfloat16 [512, 512], replicated
- d_bias: float32 [512], replicated
- d_gain: float32 [512], replicated
All inputs are finite; a program needn't handle non-finite values. No bound on the sum of `edge_live` on one device may be relied on, other than what follows from the above.
Results may differ from a plain program's by a relative error of at most 0.012.
Values may be sent and summed in bfloat16 or wider, within the bound.
No kernel may reach another device: no remote copies, remote signals or barrier semaphores. Data moves between devices by JAX's collectives and lax.ppermute only.
A program may use at most 64 MiB of HBM per device.

v0:
```python
import jax
import jax.numpy as jnp
from jax import lax
from jax.sharding import PartitionSpec as P


def with_halo(cells, sides, width):
    for axis, dim in sides:
        count = lax.axis_size(axis)
        ends = count - 1
        head = lax.slice_in_dim(cells, 0, width, axis=dim)
        tail = lax.slice_in_dim(cells, cells.shape[dim] - width, cells.shape[dim], axis=dim)
        cells = jnp.concatenate(
            [
                lax.ppermute(tail, axis, [(i, (i + 1) % count) for i in range(ends)]),
                cells,
                lax.ppermute(head, axis, [((i + 1) % count, i) for i in range(ends)]),
            ],
            axis=dim,
        )
    return cells


def from_behind(block, axis, distance):
    devices = range(lax.axis_size(axis))
    route = [(i - distance, i) for i in devices if i - distance in devices]
    return lax.ppermute(block, axis, route)


def edge_reverse_step(
    sending_rows,
    receiver_rows,
    cotangent_lines,
    slot_active_flags,
    output_weight,
    hidden_layer_bias,
    output_norm_gain,
):
    preact = sending_rows + receiver_rows + hidden_layer_bias
    hidden = jax.nn.silu(preact).astype(jnp.bfloat16)
    outer = jnp.dot(hidden, output_weight, preferred_element_type=jnp.float32)
    center = outer - jnp.mean(outer, axis=-1, keepdims=True)
    inv_scale = lax.rsqrt(jnp.mean(center * center, axis=-1, keepdims=True) + 1e-05)
    normed = center * inv_scale
    incoming_gradient = cotangent_lines.astype(jnp.float32) * slot_active_flags[:, None].astype(
        jnp.float32
    )
    scaled = incoming_gradient * output_norm_gain
    d_outer = inv_scale * (
        scaled
        - jnp.mean(scaled, axis=-1, keepdims=True)
        - normed * jnp.mean(scaled * normed, axis=-1, keepdims=True)
    )
    d_outer_b = d_outer.astype(jnp.bfloat16)
    w_out_grad = jnp.dot(hidden.T, d_outer_b, preferred_element_type=jnp.float32)
    d_hidden = jnp.dot(d_outer_b, output_weight.T, preferred_element_type=jnp.float32)
    sigmoid = jax.nn.sigmoid(preact)
    preactivation_gradient = d_hidden * sigmoid * (1.0 + preact * (1.0 - sigmoid))
    return (
        preactivation_gradient,
        w_out_grad,
        jnp.sum(preactivation_gradient, axis=0),
        jnp.sum(incoming_gradient * normed, axis=0),
    )


def body(
    grid_latent,
    mesh_latent,
    grid_output_cotangent,
    w_send,
    w_recv,
    output_weight,
    hidden_layer_bias,
    output_norm_gain,
    edge_sender,
    edge_receiver,
    edge_live,
):
    shards = lax.axis_size("space")
    width = grid_latent.shape[1]
    grid_rows = grid_latent.shape[0]
    mesh_rows = mesh_latent.shape[1]
    slots = edge_sender.shape[1]
    sender_local = edge_sender[0]
    receiver_index = edge_receiver[0]
    band = lax.axis_index("space")
    window = sender_local // mesh_rows
    target = band + window - 1
    inside = (target >= 0) & (target < shards)
    window = jnp.where(inside, window, 1)
    table_row = window * mesh_rows + sender_local % mesh_rows
    proj_send = jnp.dot(mesh_latent[0], w_send, preferred_element_type=jnp.float32).astype(
        jnp.bfloat16
    )
    projected_receiver = jnp.dot(grid_latent, w_recv, preferred_element_type=jnp.float32)
    table = with_halo(proj_send, (("space", 0),), mesh_rows)
    sending_rows = table[table_row]
    block = 512
    blocks = slots // block

    def run_block(operands):
        rows_send, rows_recv, rows_cot, rows_live = operands
        return edge_reverse_step(
            rows_send.astype(jnp.float32),
            rows_recv,
            rows_cot,
            rows_live,
            output_weight,
            hidden_layer_bias,
            output_norm_gain,
        )

    operands = (
        sending_rows.reshape(blocks, block, width),
        projected_receiver[receiver_index].reshape(blocks, block, width),
        grid_output_cotangent[receiver_index].reshape(blocks, block, width),
        edge_live[0].reshape(blocks, block),
    )
    d_pre_blocks, wout_blocks, bias_blocks, gain_blocks = lax.map(run_block, operands)
    preactivation_gradient = d_pre_blocks.reshape(slots, width)
    output_weight_piece = jnp.sum(wout_blocks, axis=0)
    bias_piece = jnp.sum(bias_blocks, axis=0)
    gain_piece = jnp.sum(gain_blocks, axis=0)
    table_grads = jax.ops.segment_sum(preactivation_gradient, table_row, num_segments=3 * mesh_rows)
    below = table_grads[:mesh_rows]
    above = table_grads[2 * mesh_rows :]
    from_below = from_behind(above, "space", 1)
    from_above = from_behind(below, "space", -1)
    mesh_acc = table_grads[mesh_rows : 2 * mesh_rows] + from_below + from_above
    grid_local = jax.ops.segment_sum(preactivation_gradient, receiver_index, num_segments=grid_rows)
    share = grid_rows // lax.axis_size("level")
    offset = lax.axis_index("level") * share
    grid_acc = lax.psum_scatter(
        grid_local.astype(jnp.bfloat16), "level", scatter_dimension=0, tiled=True
    )
    grid_part = lax.dynamic_slice_in_dim(grid_latent, offset, share, 0)
    mesh_sum = mesh_acc.astype(jnp.bfloat16)
    d_mesh = jnp.dot(mesh_sum, w_send.T, preferred_element_type=jnp.float32)[None]
    d_grid = jnp.dot(grid_acc, w_recv.T, preferred_element_type=jnp.float32)
    wsend_part = jnp.dot(mesh_latent[0].T, mesh_sum, preferred_element_type=jnp.float32)
    wrecv_part = jnp.dot(grid_part.T, grid_acc, preferred_element_type=jnp.float32)
    totals = lax.psum(
        (wsend_part, wrecv_part, output_weight_piece, bias_piece, gain_piece), ("space", "level")
    )
    d_w_send = totals[0].astype(jnp.bfloat16)
    d_w_recv = totals[1].astype(jnp.bfloat16)
    d_w_out = totals[2].astype(jnp.bfloat16)
    d_bias = totals[3]
    d_gain = totals[4]
    return (d_grid, d_mesh, d_w_send, d_w_recv, d_w_out, d_bias, d_gain)


def solution(mesh):
    return jax.shard_map(
        body,
        mesh=mesh,
        in_specs=(
            P("space", None),
            P("level", "space", None),
            P("space", None),
            P(),
            P(),
            P(),
            P(),
            P(),
            P("level", "space"),
            P("level", "space"),
            P("level", "space"),
        ),
        out_specs=(P(("space", "level"), None), P("level", "space", None), P(), P(), P(), P(), P()),
        check_vma=False,
    )
```

profile of v0, /device:TPU:0, one launch (start us, length us, event | category | flops | bytes accessed | tf_op | source)
XLA Modules:
  0.0 218.6 jit_solution(9644242598406611209)
XLA Ops:
  7.2 1.3 convolution_convert_fusion
  8.5 1.3 collective-permute-start.1
  9.8 5.5 %collective-permute-start = (bf16[8,512]{1,0:T(8,128)(2,1)S(1)}, bf16[8,512]{1,0:T(8,128)(2,1)S(1)}, u32[]{:S(2)}, u32[]{:S(2)}) collective-permute-start(bf16[8,512]{1,0:T(8,128)(2,1)S(1)} %convolution_convert_fusion), channel_id=1, source_target_pairs={{0,4},{4,8},{8,12},{12,16},{16,20},{20,24},{24,28},{1,5},{5,9},{9,... | collective-permute-start | bytes 24584 | tf_op jit(solution)/shard_map/ppermute | solution.py:15
  15.3 0.7 compare_select_fusion
  16.1 0.8 compare_select_fusion.1
  16.9 1.6 fusion.27
  18.5 0.5 broadcast.290
  19.1 1.4 reduce.3
  20.5 9.2 %gather_fusion.2 = bf16[2048,512]{1,0:T(8,128)(2,1)} fusion(bf16[512,512]{1,0:T(8,128)(2,1)S(1)} %copy-done, s32[2048]{0:T(1024)S(1)} %broadcast_clamp_fusion), kind=kCustom, calls=%fused_computation.2 | custom fusion | bytes 4202496 | tf_op jit(solution)/shard_map/gather | solution.py:117
  29.6 8.9 %gather_fusion.1 = f32[2048,512]{1,0:T(8,128)} fusion(f32[512,512]{1,0:T(8,128)S(1)} %fusion.27, s32[2048]{0:T(1024)S(1)} %broadcast_clamp_fusion), kind=kCustom, calls=%fused_computation.1 | custom fusion | bytes 8396800 | tf_op jit(solution)/shard_map/gather | solution.py:116
  38.6 9.2 %gather_fusion = bf16[2048,512]{1,0:T(8,128)(2,1)} fusion(bf16[24,512]{1,0:T(8,128)(2,1)S(1)} %pad_maximum_fusion, s32[2048]{0:T(1024)S(1)} %broadcast_clamp_fusion.1), kind=kCustom, calls=%fused_computation | custom fusion | bytes 4202496 | tf_op jit(solution)/shard_map/gather | solution.py:98
  47.8 37.2 %while.16 = (s32[]{:T(128)}, f32[4,512,512]{2,1,0:T(8,128)}, f32[4,512,512]{2,1,0:T(8,128)}, f32[4,512]{1,0:T(4,128)S(1)}, f32[4,512]{1,0:T(4,128)S(1)}, /*index...) while((s32[]{:T(128)}, f32[4,512,512]{2,1,0:T(8,128)}, ...), condition=%wide.region_7.8_spmd, body=%wide.region_0.7_spmd.sunk | while | flops 816840704 | bytes 18942132 | solution.py:120
  47.8 1.7 multiply_convert_fusion.2
  49.5 1.1 constant_dynamic-slice_fusion.2
  50.8 0.5 fusion.60
  51.5 0.5 fusion.61
  51.9 0.3 fusion.62
  52.3 1.6 fusion.63
  53.9 3.0 %bitcast_dynamic-update-slice_fusion.2 = (f32[4,512,512]{2,1,0:T(8,128)}, f32[512,512]{1,0:T(8,128)S(1)}) fusion(f32[4,512,512]{2,1,0:T(8,128)} %get-tuple-element.263, s32[]{:T(128)S(6)} %copy.34, f32[512]{0:T(512)S(1)} %get-tuple-element.284, f32[4,512,512]{2,1,0:T(8,128)} %get-tuple-element.283, bf16[4,512,512]{2,1,0:T(8,128)(2,1)} %get-tuple-element.282, ...), kind=kOutput, calls=%fused_computation.20.clone.1 | convolution fusion | flops 271319040 | bytes 4720644 | tf_op jit(solution)/shard_map/while/body/eval_jaxpr/dot_general | solution.py:56
  57.1 1.7 multiply_convert_fusion.2
  58.8 1.1 constant_dynamic-slice_fusion.2
  60.1 0.5 fusion.60
  60.8 0.5 fusion.61
  61.7 1.5 fusion.63
  63.2 3.1 %bitcast_dynamic-update-slice_fusion.2 = (f32[4,512,512]{2,1,0:T(8,128)}, f32[512,512]{1,0:T(8,128)S(1)}) fusion(f32[4,512,512]{2,1,0:T(8,128)} %get-tuple-element.263, s32[]{:T(128)S(6)} %copy.34, f32[512]{0:T(512)S(1)} %get-tuple-element.284, f32[4,512,512]{2,1,0:T(8,128)} %get-tuple-element.283, bf16[4,512,512]{2,1,0:T(8,128)(2,1)} %get-tuple-element.282, ...), kind=kOutput, calls=%fused_computation.20.clone.1 | convolution fusion | flops 271319040 | bytes 4720644 | tf_op jit(solution)/shard_map/while/body/eval_jaxpr/dot_general | solution.py:56
  66.4 1.7 multiply_convert_fusion.2
  68.1 1.1 constant_dynamic-slice_fusion.2
  69.4 0.5 fusion.60
  70.1 0.5 fusion.61
  71.0 1.5 fusion.63
  72.5 3.1 %bitcast_dynamic-update-slice_fusion.2 = (f32[4,512,512]{2,1,0:T(8,128)}, f32[512,512]{1,0:T(8,128)S(1)}) fusion(f32[4,512,512]{2,1,0:T(8,128)} %get-tuple-element.263, s32[]{:T(128)S(6)} %copy.34, f32[512]{0:T(512)S(1)} %get-tuple-element.284, f32[4,512,512]{2,1,0:T(8,128)} %get-tuple-element.283, bf16[4,512,512]{2,1,0:T(8,128)(2,1)} %get-tuple-element.282, ...), kind=kOutput, calls=%fused_computation.20.clone.1 | convolution fusion | flops 271319040 | bytes 4720644 | tf_op jit(solution)/shard_map/while/body/eval_jaxpr/dot_general | solution.py:56
  75.7 1.7 multiply_convert_fusion.2
  77.4 1.1 constant_dynamic-slice_fusion.2
  78.7 0.5 fusion.60
  79.4 0.5 fusion.61
  80.3 1.5 fusion.63
  81.7 3.0 %bitcast_dynamic-update-slice_fusion.2 = (f32[4,512,512]{2,1,0:T(8,128)}, f32[512,512]{1,0:T(8,128)S(1)}) fusion(f32[4,512,512]{2,1,0:T(8,128)} %get-tuple-element.263, s32[]{:T(128)S(6)} %copy.34, f32[512]{0:T(512)S(1)} %get-tuple-element.284, f32[4,512,512]{2,1,0:T(8,128)} %get-tuple-element.283, bf16[4,512,512]{2,1,0:T(8,128)(2,1)} %get-tuple-element.282, ...), kind=kOutput, calls=%fused_computation.20.clone.1 | convolution fusion | flops 271319040 | bytes 4720644 | tf_op jit(solution)/shard_map/while/body/eval_jaxpr/dot_general | solution.py:56
  84.9 13.5 %scatter_custom_fusion = f32[512,512]{1,0:T(8,128)S(1)} fusion(s32[2048]{0:T(1024)} %bitcast.107, f32[2048,512]{1,0:T(8,128)} %bitcast.108, f32[]{:T(128)} %constant.75.clone.1), kind=kCustom, calls=%fused_computation.35 | custom fusion | flops 1048576 | bytes 1049088 | tf_op jit(solution)/shard_map/scatter-add | solution.py:131
  98.4 0.9 convert_element_type.46
  99.3 13.2 %scatter_custom_fusion.1 = f32[24,512]{1,0:T(8,128)S(1)} fusion(s32[2048]{0:T(1024)S(1)} %bitcast.106, f32[2048,512]{1,0:T(8,128)} %bitcast.109, f32[]{:T(128)} %constant.75.clone.1), kind=kCustom, calls=%fused_computation.45 | custom fusion | flops 1048576 | bytes 49664 | tf_op jit(solution)/shard_map/scatter-add | solution.py:125
  112.6 4.8 %collective-permute-start.2 = (f32[8,512]{1,0:T(8,128)S(1)}, f32[8,512]{1,0:T(8,128)S(1)}, u32[]{:S(2)}, u32[]{:S(2)}) collective-permute-start(f32[8,512]{1,0:T(8,128)S(1)} %get-tuple-element.154), channel_id=1, source_target_pairs={{0,4},{4,8},{8,12},{12,16},{16,20},{20,24},{24,28},{1,5},{5,9},{9,... | collective-permute-start | bytes 49160 | tf_op jit(solution)/shard_map/ppermute | solution.py:27
  117.4 1.5 collective-permute-start.3
  118.9 3.8 %reduce_sum.81 = f32[512,512]{1,0:T(8,128)} reduce(f32[4,512,512]{2,1,0:T(8,128)} %get-tuple-element.73, f32[]{:T(128)} %constant.75.clone.1), dimensions={0}, to_apply=%region_13.14 | reduce | flops 786432 | bytes 5242884 | tf_op jit(solution)/shard_map/reduce_sum | solution.py:122
  123.4 0.9 convolution_bitcast_fusion.2
  124.3 1.3 fusion.14
  125.6 83.1 %all-reduce.2 = (bf16[512,512]{0,1:T(8,128)(2,1)}, bf16[512,512]{1,0:T(8,128)(2,1)}, bf16[512,512]{1,0:T(8,128)(2,1)}, f32[512]{0:T(512)}, f32[512]{0:T(512)}) all-reduce(f32[512,512]{0,1:T(8,128)S(1)} %convolution_bitcast_fusion.1, f32[512,512]{1,0:T(8,128)S(1)} %fusion.14, ...), channel_id=1, replica_groups=mesh['space'=8,'level'=4] {'space','level'}, use_global_device_ids=true, to_apply=%region_11.12 | all-reduce | flops 787456 | bytes 4726784 | tf_op jit(solution)/shard_map/psum | solution.py:143
  208.7 2.0 copy.21
  210.7 1.0 fusion.28
  (75 shorter events, 4.4 us)
Async XLA Ops:
  7.2 13.3 %copy-start = (bf16[512,512]{1,0:T(8,128)(2,1)S(1)}, bf16[512,512]{1,0:T(8,128)(2,1)}, u32[]{:S(2)}) copy-start(bf16[512,512]{1,0:T(8,128)(2,1)} %param.15) | copy-start | bytes 1572868
  7.2 117.1 %reduce-scatter.2.cloned.1.call-start = ((), (), s32[]{:S(2)}) async-start(), calls=%async_computation.1 | async-start | bytes 655360 | tf_op jit(solution)/shard_map/reduce_scatter | solution.py:134
  8.5 30.0 %collective-permute-start.1 = (bf16[8,512]{1,0:T(8,128)(2,1)S(1)}, bf16[8,512]{1,0:T(8,128)(2,1)S(1)}, u32[]{:S(2)}, u32[]{:S(2)}) collective-permute-start(bf16[8,512]{1,0:T(8,128)(2,1)S(1)} %convolution_convert_fusion), channel_id=1, source_target_pairs={{4,0},{8,4},{12,8},{16,12},{20,16},{24,20},{28,24},{5,1},{9,5},{13... | collective-permute-start | bytes 24584 | tf_op jit(solution)/shard_map/ppermute | solution.py:17
  9.8 28.7 %collective-permute-start = (bf16[8,512]{1,0:T(8,128)(2,1)S(1)}, bf16[8,512]{1,0:T(8,128)(2,1)S(1)}, u32[]{:S(2)}, u32[]{:S(2)}) collective-permute-start(bf16[8,512]{1,0:T(8,128)(2,1)S(1)} %convolution_convert_fusion), channel_id=1, source_target_pairs={{0,4},{4,8},{8,12},{12,16},{16,20},{20,24},{24,28},{1,5},{5,9},{9,... | collective-permute-start | bytes 24584 | tf_op jit(solution)/shard_map/ppermute | solution.py:15
  38.5 9.2 %copy-start.1 = (bf16[512,512]{1,0:T(8,128)(2,1)S(1)}, bf16[512,512]{1,0:T(8,128)(2,1)}, u32[]{:S(2)}) copy-start(bf16[512,512]{1,0:T(8,128)(2,1)} %param.18) | copy-start | bytes 1572868
  38.5 9.2 %copy-start.5 = (f32[512]{0:T(512)S(1)}, f32[512]{0:T(512)}, u32[]{:S(2)}) copy-start(f32[512]{0:T(512)} %param.20) | copy-start | bytes 6148
  38.5 9.2 %copy-start.6 = (f32[512]{0:T(512)S(1)}, f32[512]{0:T(512)}, u32[]{:S(2)}) copy-start(f32[512]{0:T(512)} %param.19) | copy-start | bytes 6148
  84.9 38.1 %copy-start.7 = (bf16[1,8,512]{2,1,0:T(8,128)(2,1)S(1)}, bf16[1,8,512]{2,1,0:T(8,128)(2,1)}, u32[]{:S(2)}) copy-start(bf16[1,8,512]{2,1,0:T(8,128)(2,1)} %param.14) | copy-start | bytes 24580
  98.4 25.0 %copy-start.2 = (bf16[512,512]{1,0:T(8,128)(2,1)S(1)}, bf16[512,512]{1,0:T(8,128)(2,1)}, u32[]{:S(2)}) copy-start(bf16[512,512]{1,0:T(8,128)(2,1)} %param.16) | copy-start | bytes 1572868
  112.6 10.1 %collective-permute-start.2 = (f32[8,512]{1,0:T(8,128)S(1)}, f32[8,512]{1,0:T(8,128)S(1)}, u32[]{:S(2)}, u32[]{:S(2)}) collective-permute-start(f32[8,512]{1,0:T(8,128)S(1)} %get-tuple-element.154), channel_id=1, source_target_pairs={{0,4},{4,8},{8,12},{12,16},{16,20},{20,24},{24,28},{1,5},{5,9},{9,... | collective-permute-start | bytes 49160 | tf_op jit(solution)/shard_map/ppermute | solution.py:27
  117.4 5.6 %collective-permute-start.3 = (f32[8,512]{1,0:T(8,128)S(1)}, f32[8,512]{1,0:T(8,128)S(1)}, u32[]{:S(2)}, u32[]{:S(2)}) collective-permute-start(f32[8,512]{1,0:T(8,128)S(1)} %get-tuple-element.155), channel_id=1, source_target_pairs={{4,0},{8,4},{12,8},{16,12},{20,16},{24,20},{28,24},{5,1},{9,5},{13... | collective-permute-start | bytes 49160 | tf_op jit(solution)/shard_map/ppermute | solution.py:27
  122.7 88.0 %copy-start.3 = (bf16[512,512]{1,0:T(8,128)(2,1)S(1)}, bf16[512,512]{1,0:T(8,128)(2,1)}, u32[]{:S(2)}) copy-start(bf16[512,512]{1,0:T(8,128)(2,1)} %param.17) | copy-start | bytes 1572868
  124.3 86.5 %copy-start.4 = (bf16[128,512]{1,0:T(8,128)(2,1)S(1)}, bf16[128,512]{1,0:T(8,128)(2,1)}, u32[]{:S(2)}) copy-start(bf16[128,512]{1,0:T(8,128)(2,1)} %reduce-scatter.2.cloned.1.call-done) | copy-start | bytes 393220
Sparse Core Ops, SparseCore 0:
  99.4 23.2 reduce-scatter.1
where the time goes:
time: 220 us; the launch traced here: 219 us
  blocking collectives  83.1 us (38%)
  other arithmetic  45.5 us (21%)
  local copies, waits for them, and re-layouts  35.4 us (16%)
  matrix products  26.6 us (12%)
  between operations  14.3 us (6%)
  starting transfers between devices  13.2 us (6%)
    psum x1, blocking collectives, body(): lax.psum((wsend_part, wrecv_part, output_weight_piece, bias_piece, gain_p...  83.1 us
    scatter-add x1, other arithmetic, body(): jax.ops.segment_sum(preactivation_gradient, receiver_index, num_segments=...  13.5 us
    scatter-add x1, other arithmetic, body(): jax.ops.segment_sum(preactivation_gradient, table_row, num_segments=3 * m...  13.2 us
    dot_general x4, matrix products, edge_reverse_step(): jnp.dot(d_outer_b, output_weight.T, preferred_element_type=jnp.float32)  12.2 us
    gather x1, local copies, waits for them, and re-layouts, body(): sending_rows = table[table_row]  9.18 us
    gather x1, local copies, waits for them, and re-layouts, body(): grid_output_cotangent[receiver_index].reshape(blocks, block, width)  9.15 us
    gather x1, local copies, waits for them, and re-layouts, body(): projected_receiver[receiver_index].reshape(blocks, block, width)  8.9 us
    convert_element_type x4, other arithmetic, edge_reverse_step(): hidden = jax.nn.silu(preact).astype(jnp.bfloat16)  6.68 us
  transfers between devices with their start and end apart: 5, of which 1 were waited for; matrix products, arithmetic and copies ran while one was open for 19% of the time, Pallas kernels for 0%

commit v1 on v0

v1 whole, which is shorter than its diff:
```python
import functools

import jax
import jax.numpy as jnp
from jax import lax
from jax.experimental import pallas as pl
from jax.experimental.pallas import tpu as pltpu
from jax.sharding import PartitionSpec as P

F32 = jnp.float32
BF16 = jnp.bfloat16
ALL = ("space", "level")
LANES = 128
BLOCK = 512
SUB = 256
WINDOW_ROWS = 32
VMEM = 60 * 1024 * 1024


def sliced(width, parts):
    return width % (16 * parts) == 0


def chunk_of(width, parts):
    if not sliced(width, parts):
        return jax.ShapeDtypeStruct((width + 8, width), F32)
    rows = width * width // parts // LANES + 2 * width // LANES
    return jax.ShapeDtypeStruct((parts, rows, LANES), BF16)


def cost(flops, nbytes):
    return pl.CostEstimate(flops=flops, bytes_accessed=nbytes, transcendentals=0)


def mix(a, b, left, right):
    return lax.dot_general(a, b, (((left,), (right,)), ((), ())), preferred_element_type=F32)


def full(array):
    return pl.BlockSpec(array.shape, lambda *_: (0,) * array.ndim)


def rows_of(line, count):
    return [line[:, j * LANES : (j + 1) * LANES] for j in range(count)]


def columns_of(lines):
    used = jnp.concatenate([line.astype(F32) for line in lines], axis=0)
    pad = jnp.zeros((LANES - used.shape[0], LANES), F32)
    turned = jnp.concatenate([used, pad], axis=0).T
    return [turned[:, j : j + 1] for j in range(len(lines))]


def one_hot_rows(columns, width):
    lane = lax.broadcasted_iota(jnp.int32, (LANES, width), 1).astype(F32)
    hot = [jnp.where(lane == column, 1.0, 0.0).astype(BF16) for column in columns]
    return jnp.concatenate(hot, axis=0)


def one_hot_cols(lines, height):
    row = lax.broadcasted_iota(jnp.int32, (height, LANES), 0)
    hot = [jnp.where(row == line, 1.0, 0.0).astype(BF16) for line in lines]
    return jnp.concatenate(hot, axis=1)


def table_rows(sender, mesh_rows, band, shards):
    window = lax.div(sender, mesh_rows)
    target = band + window - 1
    window = jnp.where((target >= 0) & (target < shards), window, 1)
    return window * mesh_rows + lax.rem(sender, mesh_rows)


def groups(x):
    return jnp.sum(x.reshape(x.shape[0] // 8, 8, x.shape[1]), axis=0)


def split(x):
    hi = x.astype(BF16)
    return hi, (x - hi.astype(F32)).astype(BF16)


def store_slabs(out_ref, total, vector, parts):
    rows, width = total.shape
    if not sliced(width, parts):
        out_ref[:rows, :] = total
        out_ref[rows:, :] = jnp.broadcast_to(vector, (8, width))
        return
    own = rows // parts
    tiles = width // LANES
    for j in range(tiles):
        piece = total[:, j * LANES : (j + 1) * LANES].astype(BF16)
        out_ref[:, j * own : (j + 1) * own, :] = piece.reshape(parts, own, LANES)
    hi, lo = split(vector)
    extra = [v[:, j * LANES : (j + 1) * LANES] for v in (hi, lo) for j in range(tiles)]
    extra = jnp.concatenate([v.astype(F32) for v in extra], axis=0).astype(BF16)
    out_ref[:, own * tiles :, :] = jnp.broadcast_to(extra[None], (parts,) + extra.shape)


def gather_kernel(recv_ref, live_ref, lat_ref, cot_ref, w_ref, pre_ref, out_cot_ref, table):
    @pl.when(pl.program_id(0) == 0)
    def _():
        table[...] = jnp.dot(lat_ref[...], w_ref[...], preferred_element_type=F32).astype(BF16)

    pieces = BLOCK // LANES
    recv = recv_ref[...]
    kept = jnp.where(live_ref[...] == 1, recv, -1)
    cols = columns_of(rows_of(recv, pieces) + rows_of(kept, pieces))
    height = lat_ref.shape[0]
    pre = jnp.dot(one_hot_rows(cols[:pieces], height), table[...], preferred_element_type=F32)
    pre_ref[...] = pre.astype(BF16)
    cot = jnp.dot(one_hot_rows(cols[pieces:], height), cot_ref[...], preferred_element_type=F32)
    out_cot_ref[...] = cot.astype(BF16)


def gather(recv, live, lat, cot, w):
    slots = recv.shape[1]
    width = lat.shape[1]
    line = pl.BlockSpec((1, BLOCK), lambda i: (0, i))
    edge = pl.BlockSpec((BLOCK, width), lambda i: (i, 0))
    flops = 4 * slots * width * lat.shape[0]
    return pl.pallas_call(
        gather_kernel,
        grid=(slots // BLOCK,),
        in_specs=[line, line, full(lat), full(cot), full(w)],
        out_specs=[edge, edge],
        out_shape=[jax.ShapeDtypeStruct((slots, width), BF16)] * 2,
        scratch_shapes=[pltpu.VMEM(lat.shape, BF16)],
        compiler_params=pltpu.CompilerParams(vmem_limit_bytes=VMEM),
        cost_estimate=cost(flops, 6 * slots * width),
        name="edge_gather",
    )(recv, live, lat, cot, w)


def forward_kernel(
    shards, levels, parts,
    place_ref, send_ref, pre_ref, cot_ref, lat_ref, wsend_ref, wout_ref, bias_ref, gain_ref,
    wpart_ref, dout_ref, slope_ref, table, wsum, gsum,
):
    step = pl.program_id(0)
    band = place_ref[0]
    level = place_ref[1]
    mesh_rows = lat_ref.shape[1]

    @pl.when(step == 0)
    def _():
        near = [jnp.maximum(band - 1, 0), band, jnp.minimum(band + 1, shards - 1)]
        rows = [lat_ref[at * levels + level].astype(F32) for at in near]
        rows.append(jnp.zeros((WINDOW_ROWS - 3 * mesh_rows, lat_ref.shape[2]), F32))
        rows = jnp.concatenate(rows, axis=0).astype(BF16)
        proj = jnp.dot(rows, wsend_ref[...], preferred_element_type=F32).astype(BF16)
        table[...] = jnp.zeros_like(table)
        table[:WINDOW_ROWS, :] = proj
        wsum[...] = jnp.zeros_like(wsum)
        gsum[...] = jnp.zeros_like(gsum)

    width = wout_ref.shape[0]
    pieces = BLOCK // LANES
    near = table_rows(send_ref[...], mesh_rows, band, shards)
    cols = columns_of(rows_of(near, pieces))
    each = SUB // LANES
    for part in range(BLOCK // SUB):
        at = pl.ds(part * SUB, SUB)
        hot = one_hot_rows(cols[part * each : (part + 1) * each], LANES)
        pre = jnp.dot(hot, table[...], preferred_element_type=F32)
        pre = pre + pre_ref[at, :].astype(F32) + bias_ref[...]
        sig = 0.5 * jnp.tanh(0.5 * pre) + 0.5
        hidden = (pre * sig).astype(BF16)
        slope_ref[at, :] = (sig * (1.0 + pre * (1.0 - sig))).astype(BF16)
        outer = jnp.dot(hidden, wout_ref[...], preferred_element_type=F32)
        center = outer - jnp.sum(outer, axis=-1, keepdims=True) * (1.0 / width)
        var = jnp.sum(center * center, axis=-1, keepdims=True) * (1.0 / width)
        inv = lax.rsqrt(var + 1e-05)
        normed = center * inv
        upstream = cot_ref[at, :].astype(F32)
        scaled = upstream * gain_ref[...]
        mean_s = jnp.sum(scaled, axis=-1, keepdims=True) * (1.0 / width)
        mean_sn = jnp.sum(scaled * normed, axis=-1, keepdims=True) * (1.0 / width)
        d_outer = (inv * (scaled - mean_s - normed * mean_sn)).astype(BF16)
        dout_ref[at, :] = d_outer
        gsum[...] += groups(upstream * normed)
        wsum[...] += mix(hidden, d_outer, 0, 0)

    @pl.when(step == pl.num_programs(0) - 1)
    def _():
        store_slabs(wpart_ref, wsum[...], jnp.sum(gsum[...], axis=0, keepdims=True), parts)


def forward(shards, levels, place, send, pre, cot, lat, wsend, wout, bias, gain):
    slots, width = pre.shape
    parts = shards * levels
    line = pl.BlockSpec((1, BLOCK), lambda i: (0, i))
    edge = pl.BlockSpec((BLOCK, width), lambda i: (i, 0))
    chunk = chunk_of(width, parts)
    return pl.pallas_call(
        functools.partial(forward_kernel, shards, levels, parts),
        grid=(slots // BLOCK,),
        in_specs=[
            pl.BlockSpec(memory_space=pltpu.SMEM), line, edge, edge,
            full(lat), full(wsend), full(wout), full(bias), full(gain),
        ],
        out_specs=[full(chunk), edge, edge],
        out_shape=[
            chunk,
            jax.ShapeDtypeStruct((slots, width), BF16),
            jax.ShapeDtypeStruct((slots, width), BF16),
        ],
        scratch_shapes=[
            pltpu.VMEM((LANES, width), BF16),
            pltpu.VMEM((width, width), F32),
            pltpu.VMEM((8, width), F32),
        ],
        compiler_params=pltpu.CompilerParams(vmem_limit_bytes=VMEM),
        cost_estimate=cost(5 * slots * width * width, 8 * slots * width),
        name="edge_forward",
    )(place, send, pre, cot, lat, wsend, wout, bias, gain)


def backward_kernel(
    shards, mesh_rows, parts,
    place_ref, send_ref, recv_ref, dout_ref, slope_ref, wout_ref, lat_ref,
    vpart_ref, grid_ref, near_ref, gacc, tacc, bacc,
):
    step = pl.program_id(0)

    @pl.when(step == 0)
    def _():
        gacc[...] = jnp.zeros_like(gacc)
        tacc[...] = jnp.zeros_like(tacc)
        bacc[...] = jnp.zeros_like(bacc)

    pieces = BLOCK // LANES
    near = table_rows(send_ref[...], mesh_rows, place_ref[0], shards)
    d_hidden = mix(dout_ref[...], wout_ref[...], 1, 1)
    d_pre = d_hidden * slope_ref[...].astype(F32)
    bacc[...] += groups(d_pre)
    d_pre = d_pre.astype(BF16)
    hot = one_hot_cols(rows_of(recv_ref[...], pieces), lat_ref.shape[0])
    gacc[...] += jnp.dot(hot, d_pre, preferred_element_type=F32)
    hot = one_hot_cols(rows_of(near, pieces), WINDOW_ROWS)
    tacc[...] += jnp.dot(hot, d_pre, preferred_element_type=F32)

    @pl.when(step == pl.num_programs(0) - 1)
    def _():
        rows = gacc[...].astype(BF16)
        grid_ref[...] = rows
        near_ref[...] = tacc[...]
        total = mix(lat_ref[...], rows, 0, 0)
        store_slabs(vpart_ref, total, jnp.sum(bacc[...], axis=0, keepdims=True), parts)


def backward(shards, levels, mesh_rows, place, send, recv, dout, slope, wout, lat):
    slots, width = dout.shape
    parts = shards * levels
    line = pl.BlockSpec((1, BLOCK), lambda i: (0, i))
    edge = pl.BlockSpec((BLOCK, width), lambda i: (i, 0))
    chunk = chunk_of(width, parts)
    return pl.pallas_call(
        functools.partial(backward_kernel, shards, mesh_rows, parts),
        grid=(slots // BLOCK,),
        in_specs=[
            pl.BlockSpec(memory_space=pltpu.SMEM), line, line, edge, edge, full(wout), full(lat),
        ],
        out_specs=[
            full(chunk),
            pl.BlockSpec(lat.shape, lambda i: (0, 0)),
            pl.BlockSpec((WINDOW_ROWS, width), lambda i: (0, 0)),
        ],
        out_shape=[
            chunk,
            jax.ShapeDtypeStruct(lat.shape, BF16),
            jax.ShapeDtypeStruct((WINDOW_ROWS, width), F32),
        ],
        scratch_shapes=[
            pltpu.VMEM(lat.shape, F32),
            pltpu.VMEM((WINDOW_ROWS, width), F32),
            pltpu.VMEM((8, width), F32),
        ],
        compiler_params=pltpu.CompilerParams(vmem_limit_bytes=VMEM),
        cost_estimate=cost(5 * slots * width * width, 4 * slots * width),
        name="edge_backward",
    )(place, send, recv, dout, slope, wout, lat)


def reduce_kernel(
    mesh_rows, w_ref, v_ref, near_ref, below_ref, above_ref, wsend_ref,
    pay_ref, dmesh_ref, dbias_ref, dgain_ref,
):
    width = wsend_ref.shape[0]
    tiles = width // LANES
    copies = pay_ref.shape[0]
    slab = w_ref.shape[1] - 2 * tiles
    pieces = []
    for source, vector in ((w_ref, dgain_ref), (v_ref, dbias_ref)):
        total = jnp.sum(source[...].astype(F32), axis=0)
        pieces.append(total[:slab])
        both = total[slab : slab + tiles] + total[slab + tiles :]
        for j in range(tiles):
            vector[:, j * LANES : (j + 1) * LANES] = both[j : j + 1]
    mesh = near_ref[mesh_rows : 2 * mesh_rows, :] + below_ref[...] + above_ref[...]
    pieces += [mesh[:, j * LANES : (j + 1) * LANES] for j in range(tiles)]
    payload = jnp.concatenate(pieces, axis=0).astype(BF16)
    pay_ref[...] = jnp.broadcast_to(payload[None], (copies,) + payload.shape)
    dmesh_ref[...] = mix(mesh.astype(BF16), wsend_ref[...], 1, 1)


def reduce(shards, mesh_rows, w, v, near, below, above, wsend):
    width = wsend.shape[0]
    tiles = width // LANES
    rows = 2 * (w.shape[1] - 2 * tiles) + mesh_rows * tiles
    return pl.pallas_call(
        functools.partial(reduce_kernel, mesh_rows),
        out_shape=[
            jax.ShapeDtypeStruct((shards, rows, LANES), BF16),
            jax.ShapeDtypeStruct((mesh_rows, width), F32),
            jax.ShapeDtypeStruct((1, width), F32),
            jax.ShapeDtypeStruct((1, width), F32),
        ],
        compiler_params=pltpu.CompilerParams(vmem_limit_bytes=VMEM),
        cost_estimate=cost(2 * w.size, 4 * w.size),
        name="reduce_slabs",
    )(w, v, near, below, above, wsend)


def spread_kernel(levels, mesh_rows, place_ref, lat_ref, *refs):
    parts_refs = refs[:levels]
    dsend_ref, drecv_ref, dout_ref, mesh = refs[levels:]
    width = dsend_ref.shape[0]
    tiles = width // LANES
    shards = parts_refs[0].shape[0]
    own = width // (shards * levels)
    slab = own * tiles
    level = place_ref[1]
    for k, ref in enumerate(parts_refs):
        for s in range(shards):
            part = s * levels + (level ^ k)
            for j in range(tiles):
                cols = pl.ds(j * LANES, LANES)
                rows = pl.ds(pl.multiple_of(part * own, own), own)
                dout_ref[rows, cols] = ref[s, j * own : (j + 1) * own, :]
                drecv_ref[rows, cols] = ref[s, slab + j * own : slab + (j + 1) * own, :]
            tail = ref[s, 2 * slab :, :].astype(F32)
            for j in range(tiles):
                rows = pl.ds(pl.multiple_of(part * mesh_rows, mesh_rows), mesh_rows)
                cols = pl.ds(j * LANES, LANES)
                mesh[rows, cols] = tail[j * mesh_rows : (j + 1) * mesh_rows]
    dsend_ref[...] = mix(lat_ref[...], mesh[...].astype(BF16), 0, 0).astype(BF16)


def spread(levels, mesh_rows, place, lat, received):
    width = lat.shape[1]
    out = jax.ShapeDtypeStruct((width, width), BF16)
    return pl.pallas_call(
        functools.partial(spread_kernel, levels, mesh_rows),
        in_specs=[pl.BlockSpec(memory_space=pltpu.SMEM)]
        + [pl.BlockSpec(memory_space=pltpu.VMEM)] * (1 + levels),
        out_shape=[out, out, out],
        scratch_shapes=[pltpu.VMEM(lat.shape, F32)],
        compiler_params=pltpu.CompilerParams(vmem_limit_bytes=VMEM),
        cost_estimate=cost(2 * lat.size * width, 8 * width * width),
        name="spread_weights",
    )(place, lat, *received)


def to_all(x, axes, count):
    copies = jnp.broadcast_to(x[None], (count,) + x.shape)
    return lax.all_to_all(copies, axes, 0, 0, tiled=False)


def swap(x, axis, bit):
    return lax.ppermute(x, axis, [(i, i ^ bit) for i in range(lax.axis_size(axis))])


def shift(x, axis, step):
    count = lax.axis_size(axis)
    return lax.ppermute(
        x, axis, [(i, i + step) for i in range(count) if 0 <= i + step < count]
    )


def body(
    grid_latent, mesh_latent, grid_output_cotangent, w_send, w_recv, output_weight,
    hidden_layer_bias, output_norm_gain, edge_sender, edge_receiver, edge_live,
):
    shards, levels = lax.axis_size("space"), lax.axis_size("level")
    parts = shards * levels
    width = grid_latent.shape[1]
    grid_rows = grid_latent.shape[0]
    mesh_rows = mesh_latent.shape[1]
    place = jnp.stack([lax.axis_index("space"), lax.axis_index("level")]).astype(jnp.int32)

    lat_all = to_all(mesh_latent[0], ALL, parts)
    pre, cot = gather(edge_receiver, edge_live, grid_latent, grid_output_cotangent, w_recv)
    wpart, dout, slope = forward(
        shards, levels, place, edge_sender, pre, cot, lat_all, w_send, output_weight,
        hidden_layer_bias[None], output_norm_gain[None],
    )
    whole_slabs = sliced(width, parts)
    if whole_slabs:
        wrecv = lax.all_to_all(wpart, ALL, 0, 0, tiled=False)
    vpart, grid_local, near = backward(
        shards, levels, mesh_rows, place, edge_sender, edge_receiver, dout, slope,
        output_weight, grid_latent,
    )
    if whole_slabs:
        vrecv = lax.all_to_all(vpart, ALL, 0, 0, tiled=False)
    below = shift(near[2 * mesh_rows : 3 * mesh_rows], "space", 1)
    above = shift(near[:mesh_rows], "space", -1)
    share = grid_rows // levels
    levels_grid = lax.all_to_all(
        grid_local.reshape(levels, share, width), "level", 0, 0, tiled=False
    )
    grid_acc = jnp.sum(levels_grid.astype(F32), axis=0).astype(BF16)
    d_grid = jnp.dot(grid_acc, w_recv.T, preferred_element_type=F32)

    if not whole_slabs:
        mesh = near[mesh_rows : 2 * mesh_rows] + below + above
        mesh = mesh.astype(BF16)
        d_mesh = mix(mesh, w_send, 1, 1)
        totals = lax.psum((mix(mesh_latent[0], mesh, 0, 0), vpart, wpart), ALL)
        d_w = [total[:width].astype(BF16) for total in totals]
        return (d_grid, d_mesh[None], *d_w, totals[1][width], totals[2][width])

    payload, d_mesh, d_bias, d_gain = reduce(
        shards, mesh_rows, wrecv, vrecv, near, below, above, w_send
    )
    own = lax.all_to_all(payload, "space", 0, 0, tiled=False)
    received = {0: own}
    bit = levels // 2
    while bit:
        for k in list(received):
            received[k | bit] = swap(received[k], "level", bit)
        bit //= 2
    d_w_send, d_w_recv, d_w_out = spread(
        levels, mesh_rows, place, lat_all.reshape(parts * mesh_rows, width),
        [received[k] for k in range(levels)],
    )
    return (d_grid, d_mesh[None], d_w_send, d_w_recv, d_w_out, d_bias[0], d_gain[0])


def solution(mesh):
    return jax.shard_map(
        body,
        mesh=mesh,
        in_specs=(
            P("space", None), P("level", "space", None), P("space", None), P(), P(), P(), P(), P(),
            P("level", "space"), P("level", "space"), P("level", "space"),
        ),
        out_specs=(P(("space", "level"), None), P("level", "space", None), P(), P(), P(), P(), P()),
        check_vma=False,
    )
```

time: 220 us -> 118 us (0.54)
  blocking collectives: 83.1 us -> 34.9 us
  other arithmetic: 45.5 us -> 0.68 us
  local copies, waits for them, and re-layouts: 35.4 us -> 3.84 us
  Pallas kernels: 0 us -> 31.2 us
  matrix products: 26.6 us -> 1.01 us
  waiting for transfers between devices: 0.36 us -> 23 us
  between operations: 14.3 us -> 0.77 us
  starting transfers between devices: 13.2 us -> 21.8 us
    psum x1 -> x0, blocking collectives: 83.1 us -> none  [body(): lax.psum((wsend_part, wrecv_part, output_weight_piece, bias_piece, gain_p...]
    all_to_all x0 -> x2, blocking collectives: none -> 34.9 us  [the longest x1 20.3 us: body(): vrecv = lax.all_to_all(vpart, ALL, 0, 0, tiled=False)]
    pallas_call x0 -> x5, Pallas kernels: none -> 31.2 us  [the longest x1 12.8 us: forward(): pl.pallas_call(functools.partial(forward_kernel, shards, levels, parts),...]
    gather x3 -> x0, local copies, waits for them, and re-layouts: 27.2 us -> none  [the longest x1 9.18 us: body(): sending_rows = table[table_row]]
    scatter-add x2 -> x0, other arithmetic: 26.7 us -> none  [the longest x1 13.5 us: body(): jax.ops.segment_sum(preactivation_gradient, receiver_index, num_segments=...]
    dot_general x18 -> x1, matrix products: 26.6 us -> 1.01 us  [body(): d_grid = jnp.dot(grid_acc, w_recv.T, preferred_element_type=F32)]
    all_to_all x0 -> x3, waiting for transfers between devices: none -> 19 us  [the longest x1 9.35 us: body(): wrecv = lax.all_to_all(wpart, ALL, 0, 0, tiled=False)]
    all_to_all x0 -> x3, starting transfers between devices: none -> 13.9 us  [the longest x1 7.33 us: to_all(): return lax.all_to_all(copies, axes, 0, 0, tiled=False)]
  transfers between devices with their start and end apart: 5 -> 8, of which waited for: 1 -> 5; matrix products, arithmetic and copies ran while one was open for 19% -> 1% of each run, Pallas kernels for 0% -> 5%
where the time goes in v1:
time: 118 us; the launch traced here: 117 us
  blocking collectives  34.9 us (30%)
  Pallas kernels  31.2 us (26%)
  waiting for transfers between devices  23 us (19%)
  starting transfers between devices  21.8 us (18%)
  local copies, waits for them, and re-layouts  3.84 us (3%)
    all_to_all x1, blocking collectives, body(): vrecv = lax.all_to_all(vpart, ALL, 0, 0, tiled=False)  20.3 us
    all_to_all x1, blocking collectives, body(): own = lax.all_to_all(payload, 'space', 0, 0, tiled=False)  14.7 us
    pallas_call x1, Pallas kernels, forward(): pl.pallas_call(functools.partial(forward_kernel, shards, levels, parts),...  12.8 us
    all_to_all x1, waiting for transfers between devices, body(): wrecv = lax.all_to_all(wpart, ALL, 0, 0, tiled=False)  9.35 us
    all_to_all x1, starting transfers between devices, to_all(): return lax.all_to_all(copies, axes, 0, 0, tiled=False)  7.33 us
    pallas_call x1, Pallas kernels, backward(): pl.pallas_call(functools.partial(backward_kernel, shards, mesh_rows, part...  7.1 us
    pallas_call x1, Pallas kernels, gather(): pl.pallas_call(gather_kernel, grid=(slots // BLOCK,), in_specs=[line, lin...  6.06 us
    ppermute x2, starting transfers between devices, shift(): lax.ppermute(x, axis, [(i, i + step) for i in range(count) if 0 <= i + st...  5.97 us
  transfers between devices with their start and end apart: 8, of which 5 were waited for; matrix products, arithmetic and copies ran while one was open for 1% of the time, Pallas kernels for 5%

profile of v1, /device:TPU:0, one launch (start us, length us, event | category | flops | bytes accessed | tf_op | source)
XLA Modules:
  0.0 117.1 jit_solution(4182836058943315224)
XLA Ops:
  0.6 1.4 %broadcast_in_dim.17 = bf16[32,8,512]{2,1,0:T(8,128)(2,1)} broadcast(bf16[8,512]{1,0:T(8,128)(2,1)} %bitcast.13), dimensions={1,2} | broadcast | bytes 270336 | tf_op jit(solution)/shard_map/broadcast_in_dim | solution.py:365
  2.0 7.3 %all-to-all-start = ((bf16[32,8,512]{2,1,0:T(8,128)(2,1)}), bf16[32,8,512]{2,1,0:T(8,128)(2,1)S(1)}, u32[]{:S(2)}, u32[]{:S(2)}) async-start(bf16[32,8,512]{2,1,0:T(8,128)(2,1)} %broadcast_in_dim.17), calls=%async_computation | async-start | bytes 524288 | tf_op jit(solution)/shard_map/all_to_all | solution.py:366
  9.4 0.6 pad_add_fusion.place_ref
  10.0 6.1 %edge_gather.1 = (bf16[2048,512]{1,0:T(8,128)(2,1)}, bf16[2048,512]{1,0:T(8,128)(2,1)}) custom-call(s32[1,2048]{1,0:T(1,128)} %recv_ref.3, s32[1,2048]{1,0:T(1,128)} %live_ref.1, bf16[512,512]{1,0:T(8,128)(2,1)} %lat_ref.3, bf16[512,512]{1,0:T(8,128)(2,1)} %cot_ref.1, bf16[512,512]{1,0:T(8,128)(2,1)} %w_ref.1), custom_call_target="tpu_custom_call" | custom-call | flops 2147483648 | bytes 6291456 | tf_op jit(solution)/shard_map/edge_gather/pallas_call | solution.py:121
  16.0 3.9 %all-to-all-done.lat_ref = bf16[32,8,512]{2,1,0:T(8,128)(2,1)S(1)} async-done(((bf16[32,8,512]{2,1,0:T(8,128)(2,1)}), bf16[32,8,512]{2,1,0:T(8,128)(2,1)S(1)}, u32[]{:S(2)}, u32[]{:S(2)}) %all-to-all-start) | async-done | bytes 262176 | tf_op jit(solution)/shard_map/all_to_all | solution.py:366
  20.0 0.0 copy-start.2
  20.0 0.7 copy-done.2
  20.7 12.8 %edge_forward.1 = (bf16[32,72,128]{2,1,0:T(8,128)(2,1)}, bf16[2048,512]{1,0:T(8,128)(2,1)}, bf16[2048,512]{1,0:T(8,128)(2,1)}) custom-call(s32[2]{0:T(128)} %pad_add_fusion.place_ref, s32[1,2048]{1,0:T(1,128)} %send_ref.3, bf16[2048,512]{1,0:T(8,128)(2,1)} %get-tuple-element.22.pre_ref, bf16[2048,512]{1,0:T(8,128)(2,1)} %get-tuple-element.23.cot_ref, ...), custom_call_target="tpu_custom_call" | custom-call | flops 2684354560 | bytes 8388608 | tf_op jit(solution)/shard_map/edge_forward/pallas_call | solution.py:194
  33.5 7.1 %edge_backward.1 = (bf16[32,72,128]{2,1,0:T(8,128)(2,1)}, bf16[512,512]{1,0:T(8,128)(2,1)}, f32[32,512]{1,0:T(8,128)}) custom-call(s32[2]{0:T(128)} %pad_add_fusion.place_ref, s32[1,2048]{1,0:T(1,128)} %send_ref.3, s32[1,2048]{1,0:T(1,128)} %recv_ref.3, bf16[2048,512]{1,0:T(8,128)(2,1)} %get-tuple-element.24.dout_ref, ...), custom_call_target="tpu_custom_call" | custom-call | flops 2684354560 | bytes 4194304 | tf_op jit(solution)/shard_map/edge_backward/pallas_call | solution.py:257
  40.6 0.0 copy-start.7
  40.6 20.3 %all_to_all.25.v_ref = bf16[32,72,128]{2,1,0:T(8,128)(2,1)} all-to-all(bf16[32,72,128]{2,1,0:T(8,128)(2,1)} %get-tuple-element.28), channel_id=1, replica_groups=mesh['space'=8,'level'=4] {'space','level'}, dimensions={0} | all-to-all | bytes 1179648 | tf_op jit(solution)/shard_map/all_to_all | solution.py:405
  60.8 3.1 %all-to-all-start.2 = ((bf16[32,72,128]{2,1,0:T(8,128)(2,1)}), bf16[32,72,128]{2,1,0:T(8,128)(2,1)S(1)}, u32[]{:S(2)}, u32[]{:S(2)}) async-start(bf16[32,72,128]{2,1,0:T(8,128)(2,1)} %get-tuple-element.27), calls=%async_computation.2 | async-start | bytes 1179648 | tf_op jit(solution)/shard_map/all_to_all | solution.py:399
  64.0 0.0 copy-done.7
  64.0 0.0 copy-start.3
  64.0 1.4 %collective-permute-start.1 = (f32[8,512]{1,0:T(8,128)S(1)}, f32[8,512]{1,0:T(8,128)S(1)}, u32[]{:S(2)}, u32[]{:S(2)}) collective-permute-start(f32[8,512]{1,0:T(8,128)S(1)} %get-tuple-element.37), channel_id=1, source_target_pairs={{4,0},{8,4},{12,8},{16,12},{20,16},{24,20},{28,24},{5,1},{9,5},{13... | collective-permute-start | bytes 49160 | tf_op jit(solution)/shard_map/ppermute | solution.py:375
  65.4 4.5 %collective-permute-start = (f32[8,512]{1,0:T(8,128)S(1)}, f32[8,512]{1,0:T(8,128)S(1)}, u32[]{:S(2)}, u32[]{:S(2)}) collective-permute-start(f32[8,512]{1,0:T(8,128)S(1)} %get-tuple-element.38), channel_id=1, source_target_pairs={{0,4},{4,8},{8,12},{12,16},{16,20},{20,24},{24,28},{1,5},{5,9},{9,... | collective-permute-start | bytes 49160 | tf_op jit(solution)/shard_map/ppermute | solution.py:375
  70.0 0.0 collective-permute-done.1.above_ref
  70.0 0.0 copy-start.8
  70.0 1.4 %collective-permute-done.below_ref = f32[8,512]{1,0:T(8,128)S(1)} collective-permute-done((f32[8,512]{1,0:T(8,128)S(1)}, f32[8,512]{1,0:T(8,128)S(1)}, u32[]{:S(2)}, u32[]{:S(2)}) %collective-permute-start) | collective-permute-done | bytes 16416 | tf_op jit(solution)/shard_map/ppermute | solution.py:375
  71.4 0.0 copy-start.9
  71.4 9.3 %all-to-all-done.2.w_ref = bf16[32,72,128]{2,1,0:T(8,128)(2,1)S(1)} async-done(((bf16[32,72,128]{2,1,0:T(8,128)(2,1)}), bf16[32,72,128]{2,1,0:T(8,128)(2,1)S(1)}, u32[]{:S(2)}, u32[]{:S(2)}) %all-to-all-start.2) | async-done | bytes 589856 | tf_op jit(solution)/shard_map/all_to_all | solution.py:399
  80.8 0.0 copy-done.8
  80.8 0.0 copy-done.9
  80.8 0.0 copy-start
  80.8 0.8 copy-done
  81.6 2.5 %reduce_slabs.1 = (bf16[8,160,128]{2,1,0:T(8,128)(2,1)}, f32[8,512]{1,0:T(8,128)}, f32[1,512]{1,0:T(1,128)}, f32[1,512]{1,0:T(1,128)}) custom-call(bf16[32,72,128]{2,1,0:T(8,128)(2,1)} %copy-done, bf16[32,72,128]{2,1,0:T(8,128)(2,1)} %all_to_all.25.v_ref, f32[32,512]{1,0:T(8,128)} %get-tuple-element.29.near_ref, f32[8,512]{1,0:T(8,128)} %copy-done.9, ...), custom_call_target="tpu_custom_call" | custom-call | flops 589824 | bytes 1179648 | tf_op jit(solution)/shard_map/reduce_slabs/pallas_call | solution.py:310
  84.1 14.7 %all_to_all.26.refs_0_ = bf16[8,160,128]{2,1,0:T(8,128)(2,1)S(1)} all-to-all(bf16[8,160,128]{2,1,0:T(8,128)(2,1)} %get-tuple-element.31), channel_id=1, replica_groups=mesh['space'=8,'level'=4] {'space'}, dimensions={0} | all-to-all | bytes 655360 | tf_op jit(solution)/shard_map/all_to_all | solution.py:426
  98.8 0.0 copy-start.1
  98.8 1.4 %collective-permute-start.3 = (bf16[8,160,128]{2,1,0:T(8,128)(2,1)S(1)}, bf16[8,160,128]{2,1,0:T(8,128)(2,1)S(1)}, u32[]{:S(2)}, u32[]{:S(2)}) collective-permute-start(bf16[8,160,128]{2,1,0:T(8,128)(2,1)S(1)} %all_to_all.26.refs_0_), channel_id=1, source_target_pairs={{0,2},{1,3},{2,0},{3,1},{4,6},{5,7},{6,4},{7,5},{8,10},{9,11},{10,... | collective-permute-start | bytes 983048 | tf_op jit(solution)/shard_map/ppermute | solution.py:370
  100.2 3.5 %all-to-all-start.1 = ((bf16[4,128,512]{2,1,0:T(8,128)(2,1)}), bf16[4,128,512]{2,1,0:T(8,128)(2,1)S(1)}, u32[]{:S(2)}, u32[]{:S(2)}) async-start(bf16[4,128,512]{2,1,0:T(8,128)(2,1)} %bitcast.5), calls=%async_computation.1 | async-start | bytes 1048576 | tf_op jit(solution)/shard_map/all_to_all | solution.py:409
  103.7 0.5 collective-permute-start.2
  104.1 2.6 %collective-permute-done.3.refs_2_ = bf16[8,160,128]{2,1,0:T(8,128)(2,1)S(1)} collective-permute-done((bf16[8,160,128]{2,1,0:T(8,128)(2,1)S(1)}, bf16[8,160,128]{2,1,0:T(8,128)(2,1)S(1)}, u32[]{:S(2)}, u32[]{:S(2)}) %collective-permute-start.3) | collective-permute-done | bytes 327712 | tf_op jit(solution)/shard_map/ppermute | solution.py:370
  106.7 0.0 copy-start.4
  106.7 0.0 collective-permute-start.4
  106.7 5.7 %all-to-all-done.1 = bf16[4,128,512]{2,1,0:T(8,128)(2,1)S(1)} async-done(((bf16[4,128,512]{2,1,0:T(8,128)(2,1)}), bf16[4,128,512]{2,1,0:T(8,128)(2,1)S(1)}, u32[]{:S(2)}, u32[]{:S(2)}) %all-to-all-start.1) | async-done | bytes 524320 | tf_op jit(solution)/shard_map/all_to_all | solution.py:409
  112.4 0.1 reduce_sum.12
  112.5 0.0 copy-done.3
  112.5 1.0 fusion.1
  113.6 0.0 collective-permute-done.2.refs_1_
  113.6 0.0 copy-start.5
  113.6 0.0 collective-permute-done.4.refs_3_
  113.6 0.0 copy-start.6
  113.6 0.0 copy-done.1
  113.6 0.0 copy-done.4
  113.6 0.7 copy-done.5
  114.3 0.1 copy-done.6
  114.4 2.7 %spread_weights.1 = (bf16[512,512]{1,0:T(8,128)(2,1)}, bf16[512,512]{1,0:T(8,128)(2,1)}, bf16[512,512]{1,0:T(8,128)(2,1)}) custom-call(s32[2]{0:T(128)} %pad_add_fusion.place_ref, bf16[256,512]{1,0:T(8,128)(2,1)} %bitcast.12, bf16[8,160,128]{2,1,0:T(8,128)(2,1)} %copy-done.1, bf16[8,160,128]{2,1,0:T(8,128)(2,1)} %copy-done.5, ...), custom_call_target="tpu_custom_call" | custom-call | flops 134217728 | bytes 2097152 | tf_op jit(solution)/shard_map/spread_weights/pallas_call | solution.py:352
  (1 shorter events, 0.0 us)
Async XLA Ops:
  2.0 17.9 %all-to-all-start = ((bf16[32,8,512]{2,1,0:T(8,128)(2,1)}), bf16[32,8,512]{2,1,0:T(8,128)(2,1)S(1)}, u32[]{:S(2)}, u32[]{:S(2)}) async-start(bf16[32,8,512]{2,1,0:T(8,128)(2,1)} %broadcast_in_dim.17), calls=%async_computation | async-start | bytes 524288 | tf_op jit(solution)/shard_map/all_to_all | solution.py:366
  20.0 0.7 copy-start.2
  40.6 23.4 %copy-start.7 = (f32[32,512]{1,0:T(8,128)S(1)}, f32[32,512]{1,0:T(8,128)}, u32[]{:S(2)}) copy-start(f32[32,512]{1,0:T(8,128)} %get-tuple-element.29.near_ref) | copy-start | bytes 196612
  60.8 19.9 %all-to-all-start.2 = ((bf16[32,72,128]{2,1,0:T(8,128)(2,1)}), bf16[32,72,128]{2,1,0:T(8,128)(2,1)S(1)}, u32[]{:S(2)}, u32[]{:S(2)}) async-start(bf16[32,72,128]{2,1,0:T(8,128)(2,1)} %get-tuple-element.27), calls=%async_computation.2 | async-start | bytes 1179648 | tf_op jit(solution)/shard_map/all_to_all | solution.py:399
  64.0 48.6 %copy-start.3 = (bf16[512,512]{1,0:T(8,128)(2,1)S(1)}, bf16[512,512]{1,0:T(8,128)(2,1)}, u32[]{:S(2)}) copy-start(bf16[512,512]{1,0:T(8,128)(2,1)} %w_ref.1) | copy-start | bytes 1572868
  64.0 6.0 %collective-permute-start.1 = (f32[8,512]{1,0:T(8,128)S(1)}, f32[8,512]{1,0:T(8,128)S(1)}, u32[]{:S(2)}, u32[]{:S(2)}) collective-permute-start(f32[8,512]{1,0:T(8,128)S(1)} %get-tuple-element.37), channel_id=1, source_target_pairs={{4,0},{8,4},{12,8},{16,12},{20,16},{24,20},{28,24},{5,1},{9,5},{13... | collective-permute-start | bytes 49160 | tf_op jit(solution)/shard_map/ppermute | solution.py:375
  65.4 6.0 %collective-permute-start = (f32[8,512]{1,0:T(8,128)S(1)}, f32[8,512]{1,0:T(8,128)S(1)}, u32[]{:S(2)}, u32[]{:S(2)}) collective-permute-start(f32[8,512]{1,0:T(8,128)S(1)} %get-tuple-element.38), channel_id=1, source_target_pairs={{0,4},{4,8},{8,12},{12,16},{16,20},{20,24},{24,28},{1,5},{5,9},{9,... | collective-permute-start | bytes 49160 | tf_op jit(solution)/shard_map/ppermute | solution.py:375
  70.0 10.8 %copy-start.8 = (f32[8,512]{1,0:T(8,128)}, f32[8,512]{1,0:T(8,128)S(1)}, u32[]{:S(2)}) copy-start(f32[8,512]{1,0:T(8,128)S(1)} %collective-permute-done.1.above_ref) | copy-start | bytes 49156
  71.4 9.4 %copy-start.9 = (f32[8,512]{1,0:T(8,128)}, f32[8,512]{1,0:T(8,128)S(1)}, u32[]{:S(2)}) copy-start(f32[8,512]{1,0:T(8,128)S(1)} %collective-permute-done.below_ref) | copy-start | bytes 49156
  80.8 0.8 copy-start
  98.8 14.8 %copy-start.1 = (bf16[8,160,128]{2,1,0:T(8,128)(2,1)}, bf16[8,160,128]{2,1,0:T(8,128)(2,1)S(1)}, u32[]{:S(2)}) copy-start(bf16[8,160,128]{2,1,0:T(8,128)(2,1)S(1)} %all_to_all.26.refs_0_) | copy-start | bytes 983044
  98.8 7.9 %collective-permute-start.3 = (bf16[8,160,128]{2,1,0:T(8,128)(2,1)S(1)}, bf16[8,160,128]{2,1,0:T(8,128)(2,1)S(1)}, u32[]{:S(2)}, u32[]{:S(2)}) collective-permute-start(bf16[8,160,128]{2,1,0:T(8,128)(2,1)S(1)} %all_to_all.26.refs_0_), channel_id=1, source_target_pairs={{0,2},{1,3},{2,0},{3,1},{4,6},{5,7},{6,4},{7,5},{8,10},{9,11},{10,... | collective-permute-start | bytes 983048 | tf_op jit(solution)/shard_map/ppermute | solution.py:370
  100.2 12.3 %all-to-all-start.1 = ((bf16[4,128,512]{2,1,0:T(8,128)(2,1)}), bf16[4,128,512]{2,1,0:T(8,128)(2,1)S(1)}, u32[]{:S(2)}, u32[]{:S(2)}) async-start(bf16[4,128,512]{2,1,0:T(8,128)(2,1)} %bitcast.5), calls=%async_computation.1 | async-start | bytes 1048576 | tf_op jit(solution)/shard_map/all_to_all | solution.py:409
  103.7 9.9 %collective-permute-start.2 = (bf16[8,160,128]{2,1,0:T(8,128)(2,1)S(1)}, bf16[8,160,128]{2,1,0:T(8,128)(2,1)S(1)}, u32[]{:S(2)}, u32[]{:S(2)}) collective-permute-start(bf16[8,160,128]{2,1,0:T(8,128)(2,1)S(1)} %all_to_all.26.refs_0_), channel_id=1, source_target_pairs={{0,1},{1,0},{2,3},{3,2},{4,5},{5,4},{6,7},{7,6},{8,9},{9,8},{10,11... | collective-permute-start | bytes 983048 | tf_op jit(solution)/shard_map/ppermute | solution.py:370
  106.7 6.9 %copy-start.4 = (bf16[8,160,128]{2,1,0:T(8,128)(2,1)}, bf16[8,160,128]{2,1,0:T(8,128)(2,1)S(1)}, u32[]{:S(2)}) copy-start(bf16[8,160,128]{2,1,0:T(8,128)(2,1)S(1)} %collective-permute-done.3.refs_2_) | copy-start | bytes 983044
  106.7 6.8 %collective-permute-start.4 = (bf16[8,160,128]{2,1,0:T(8,128)(2,1)S(1)}, bf16[8,160,128]{2,1,0:T(8,128)(2,1)S(1)}, u32[]{:S(2)}, u32[]{:S(2)}) collective-permute-start(bf16[8,160,128]{2,1,0:T(8,128)(2,1)S(1)} %collective-permute-done.3.refs_2_), channel_id=1, source_target_pairs={{0,1},{1,0},{2,3},{3,2},{4,5},{5,4},{6,7},{7,6},{8,9},{9,8},{10,11... | collective-permute-start | bytes 983048 | tf_op jit(solution)/shard_map/ppermute | solution.py:370
  113.6 0.7 copy-start.5
  113.6 0.9 copy-start.6

commit v2 on v1

v2 whole, which is shorter than its diff:
```python
import functools

import jax
import jax.numpy as jnp
from jax import lax
from jax.experimental import pallas as pl
from jax.experimental.pallas import tpu as pltpu
from jax.sharding import Mesh, PartitionSpec as P


F32 = jnp.float32
BF16 = jnp.bfloat16
ALL = ("space", "high", "low")
MOST = ("space", "high")
LANES = 128
BLOCK = 512
SUB = 256
WINDOW_ROWS = 32
VMEM = 60 * 1024 * 1024


def sliced(width, parts):
    return width % (16 * parts) == 0


def chunk_of(width, parts):
    if not sliced(width, parts):
        return jax.ShapeDtypeStruct((width + 8, width), F32)
    rows = width * width // parts // LANES + 2 * width // LANES
    return jax.ShapeDtypeStruct((parts, rows, LANES), BF16)


def cost(flops, nbytes):
    return pl.CostEstimate(flops=flops, bytes_accessed=nbytes, transcendentals=0)


def mix(a, b, left, right):
    return lax.dot_general(a, b, (((left,), (right,)), ((), ())), preferred_element_type=F32)


def full(array):
    return pl.BlockSpec(array.shape, lambda *_: (0,) * array.ndim)


def rows_of(line, count):
    return [line[:, j * LANES : (j + 1) * LANES] for j in range(count)]


def columns_of(lines):
    used = jnp.concatenate([line.astype(F32) for line in lines], axis=0)
    pad = jnp.zeros((LANES - used.shape[0], LANES), F32)
    turned = jnp.concatenate([used, pad], axis=0).T
    return [turned[:, j : j + 1] for j in range(len(lines))]


def one_hot_rows(columns, width):
    lane = lax.broadcasted_iota(jnp.int32, (LANES, width), 1).astype(F32)
    hot = [jnp.where(lane == column, 1.0, 0.0).astype(BF16) for column in columns]
    return jnp.concatenate(hot, axis=0)


def one_hot_cols(lines, height):
    row = lax.broadcasted_iota(jnp.int32, (height, LANES), 0)
    hot = [jnp.where(row == line, 1.0, 0.0).astype(BF16) for line in lines]
    return jnp.concatenate(hot, axis=1)


def table_rows(sender, mesh_rows, band, shards):
    window = lax.div(sender, mesh_rows)
    target = band + window - 1
    window = jnp.where((target >= 0) & (target < shards), window, 1)
    return window * mesh_rows + lax.rem(sender, mesh_rows)


def groups(x):
    return jnp.sum(x.reshape(x.shape[0] // 8, 8, x.shape[1]), axis=0)


def split(x):
    hi = x.astype(BF16)
    return hi, (x - hi.astype(F32)).astype(BF16)


def store_slabs(out_ref, total, vector, parts):
    rows, width = total.shape
    if len(out_ref.shape) == 2:
        out_ref[:rows, :] = total
        out_ref[rows:, :] = jnp.broadcast_to(vector, (8, width))
        return
    own = rows // parts
    tiles = width // LANES
    for j in range(tiles):
        piece = total[:, j * LANES : (j + 1) * LANES].astype(BF16)
        out_ref[:, j * own : (j + 1) * own, :] = piece.reshape(parts, own, LANES)
    hi, lo = split(vector)
    extra = [v[:, j * LANES : (j + 1) * LANES] for v in (hi, lo) for j in range(tiles)]
    extra = jnp.concatenate([v.astype(F32) for v in extra], axis=0).astype(BF16)
    out_ref[:, own * tiles :, :] = jnp.broadcast_to(extra[None], (parts,) + extra.shape)


def gather_kernel(recv_ref, live_ref, lat_ref, cot_ref, w_ref, pre_ref, out_cot_ref, table):
    @pl.when(pl.program_id(0) == 0)
    def _():
        table[...] = jnp.dot(lat_ref[...], w_ref[...], preferred_element_type=F32).astype(BF16)

    pieces = BLOCK // LANES
    recv = recv_ref[...]
    kept = jnp.where(live_ref[...] == 1, recv, -1)
    cols = columns_of(rows_of(recv, pieces) + rows_of(kept, pieces))
    height = lat_ref.shape[0]
    pre = jnp.dot(one_hot_rows(cols[:pieces], height), table[...], preferred_element_type=F32)
    pre_ref[...] = pre.astype(BF16)
    cot = jnp.dot(one_hot_rows(cols[pieces:], height), cot_ref[...], preferred_element_type=F32)
    out_cot_ref[...] = cot.astype(BF16)


def gather(recv, live, lat, cot, w):
    slots = recv.shape[1]
    width = lat.shape[1]
    line = pl.BlockSpec((1, BLOCK), lambda i: (0, i))
    edge = pl.BlockSpec((BLOCK, width), lambda i: (i, 0))
    flops = 4 * slots * width * lat.shape[0]
    return pl.pallas_call(
        gather_kernel,
        grid=(slots // BLOCK,),
        in_specs=[line, line, full(lat), full(cot), full(w)],
        out_specs=[edge, edge],
        out_shape=[jax.ShapeDtypeStruct((slots, width), BF16)] * 2,
        scratch_shapes=[pltpu.VMEM(lat.shape, BF16)],
        compiler_params=pltpu.CompilerParams(vmem_limit_bytes=VMEM),
        cost_estimate=cost(flops, 6 * slots * width),
        name="edge_gather",
    )(recv, live, lat, cot, w)


def forward_kernel(
    shards, parts,
    place_ref, send_ref, pre_ref, cot_ref, lat_ref, pair_ref, other_ref, wsend_ref, wout_ref, bias_ref, gain_ref,
    wpart_ref, dout_ref, slope_ref, table, wsum, gsum,
):
    step = pl.program_id(0)
    band = place_ref[0]
    mesh_rows = lat_ref.shape[0]

    @pl.when(step == 0)
    def _():
        even = lax.rem(band, 2) == 0
        pair = pair_ref[...].astype(F32)
        other = other_ref[...].astype(F32)
        rows = [jnp.where(even, other, pair), lat_ref[...].astype(F32), jnp.where(even, pair, other)]
        rows.append(jnp.zeros((WINDOW_ROWS - 3 * mesh_rows, lat_ref.shape[1]), F32))
        rows = jnp.concatenate(rows, axis=0).astype(BF16)
        proj = jnp.dot(rows, wsend_ref[...], preferred_element_type=F32).astype(BF16)
        table[...] = jnp.zeros_like(table)
        table[:WINDOW_ROWS, :] = proj
        wsum[...] = jnp.zeros_like(wsum)
        gsum[...] = jnp.zeros_like(gsum)

    width = wout_ref.shape[0]
    pieces = BLOCK // LANES
    near = table_rows(send_ref[...], mesh_rows, band, shards)
    cols = columns_of(rows_of(near, pieces))
    each = SUB // LANES
    for part in range(BLOCK // SUB):
        at = pl.ds(part * SUB, SUB)
        hot = one_hot_rows(cols[part * each : (part + 1) * each], LANES)
        pre = jnp.dot(hot, table[...], preferred_element_type=F32)
        pre = pre + pre_ref[at, :].astype(F32) + bias_ref[...]
        sig = 0.5 * jnp.tanh(0.5 * pre) + 0.5
        hidden = (pre * sig).astype(BF16)
        slope_ref[at, :] = (sig * (1.0 + pre * (1.0 - sig))).astype(BF16)
        outer = jnp.dot(hidden, wout_ref[...], preferred_element_type=F32)
        center = outer - jnp.sum(outer, axis=-1, keepdims=True) * (1.0 / width)
        var = jnp.sum(center * center, axis=-1, keepdims=True) * (1.0 / width)
        inv = lax.rsqrt(var + 1e-05)
        normed = center * inv
        upstream = cot_ref[at, :].astype(F32)
        scaled = upstream * gain_ref[...]
        mean_s = jnp.sum(scaled, axis=-1, keepdims=True) * (1.0 / width)
        mean_sn = jnp.sum(scaled * normed, axis=-1, keepdims=True) * (1.0 / width)
        d_outer = (inv * (scaled - mean_s - normed * mean_sn)).astype(BF16)
        dout_ref[at, :] = d_outer
        gsum[...] += groups(upstream * normed)
        wsum[...] += mix(hidden, d_outer, 0, 0)

    @pl.when(step == pl.num_programs(0) - 1)
    def _():
        store_slabs(wpart_ref, wsum[...], jnp.sum(gsum[...], axis=0, keepdims=True), parts)


def forward(shards, levels, place, send, pre, cot, lat, pair, other, wsend, wout, bias, gain):
    slots, width = pre.shape
    parts = shards * levels
    line = pl.BlockSpec((1, BLOCK), lambda i: (0, i))
    edge = pl.BlockSpec((BLOCK, width), lambda i: (i, 0))
    chunk = chunk_of(width, parts)
    return pl.pallas_call(
        functools.partial(forward_kernel, shards, parts),
        grid=(slots // BLOCK,),
        in_specs=[
            pl.BlockSpec(memory_space=pltpu.SMEM), line, edge, edge,
            full(lat), full(pair), full(other), full(wsend), full(wout), full(bias), full(gain),
        ],
        out_specs=[full(chunk), edge, edge],
        out_shape=[
            chunk,
            jax.ShapeDtypeStruct((slots, width), BF16),
            jax.ShapeDtypeStruct((slots, width), BF16),
        ],
        scratch_shapes=[
            pltpu.VMEM((LANES, width), BF16),
            pltpu.VMEM((width, width), F32),
            pltpu.VMEM((8, width), F32),
        ],
        compiler_params=pltpu.CompilerParams(vmem_limit_bytes=VMEM),
        cost_estimate=cost(5 * slots * width * width, 8 * slots * width),
        name="edge_forward",
    )(place, send, pre, cot, lat, pair, other, wsend, wout, bias, gain)


def backward_kernel(
    shards, mesh_rows, sliced_rows,
    place_ref, send_ref, recv_ref, dout_ref, slope_ref, wout_ref, lat_ref,
    vsend_ref, vkeep_ref, gsend_ref, gkeep_ref, own_ref, pair_ref, other_ref,
    gacc, tacc, bacc, total,
):
    step = pl.program_id(0)

    @pl.when(step == 0)
    def _():
        gacc[...] = jnp.zeros_like(gacc)
        tacc[...] = jnp.zeros_like(tacc)
        bacc[...] = jnp.zeros_like(bacc)

    pieces = BLOCK // LANES
    near = table_rows(send_ref[...], mesh_rows, place_ref[0], shards)
    d_hidden = mix(dout_ref[...], wout_ref[...], 1, 1)
    d_pre = d_hidden * slope_ref[...].astype(F32)
    bacc[...] += groups(d_pre)
    d_pre = d_pre.astype(BF16)
    hot = one_hot_cols(rows_of(recv_ref[...], pieces), lat_ref.shape[0])
    gacc[...] += jnp.dot(hot, d_pre, preferred_element_type=F32)
    hot = one_hot_cols(rows_of(near, pieces), WINDOW_ROWS)
    tacc[...] += jnp.dot(hot, d_pre, preferred_element_type=F32)

    @pl.when(step == pl.num_programs(0) - 1)
    def _():
        high, low = place_ref[1], place_ref[2]
        even = lax.rem(place_ref[0], 2) == 0
        below = tacc[:mesh_rows, :]
        above = tacc[2 * mesh_rows : 3 * mesh_rows, :]
        own_ref[...] = tacc[mesh_rows : 2 * mesh_rows, :]
        pair_ref[...] = jnp.where(even, above, below)
        other_ref[...] = jnp.where(even, below, above)
        total[...] = mix(lat_ref[...], gacc[...].astype(BF16), 0, 0)
        bias = jnp.sum(bacc[...], axis=0, keepdims=True)
        half = vkeep_ref.shape[0] - 8
        if sliced_rows:
            mine = pl.multiple_of(low * half, half)
            theirs = pl.multiple_of((1 - low) * half, half)
            vkeep_ref[:half, :] = total[pl.ds(mine, half), :]
            vsend_ref[:half, :] = total[pl.ds(theirs, half), :].astype(BF16)
            hi, lo = split(bias)
            rest = jnp.zeros((6, bias.shape[1]), F32)
            vsend_ref[half:, :] = jnp.concatenate(
                [hi.astype(F32), lo.astype(F32), rest], axis=0
            ).astype(BF16)
        else:
            vkeep_ref[:half, :] = total[...]
            vsend_ref[...] = jnp.zeros_like(vsend_ref)
        vkeep_ref[half:, :] = jnp.broadcast_to(bias, (8, bias.shape[1]))
        share = gkeep_ref.shape[1]
        for k in range(gkeep_ref.shape[0]):
            base = (high ^ k) * 2
            mine = pl.multiple_of((base + low) * share, share)
            theirs = pl.multiple_of((base + 1 - low) * share, share)
            gkeep_ref[k] = gacc[pl.ds(mine, share), :]
            gsend_ref[k] = gacc[pl.ds(theirs, share), :].astype(BF16)


def backward(shards, levels, mesh_rows, place, send, recv, dout, slope, wout, lat):
    slots, width = dout.shape
    sliced_rows = sliced(width, shards * levels)
    line = pl.BlockSpec((1, BLOCK), lambda i: (0, i))
    edge = pl.BlockSpec((BLOCK, width), lambda i: (i, 0))
    half = width // 2 if sliced_rows else width
    grid = (levels // 2, lat.shape[0] // levels, width)
    near = jax.ShapeDtypeStruct((mesh_rows, width), F32)
    outs = [
        jax.ShapeDtypeStruct((width // 2 + 8, width), BF16),
        jax.ShapeDtypeStruct((half + 8, width), F32),
        jax.ShapeDtypeStruct(grid, BF16),
        jax.ShapeDtypeStruct(grid, F32),
        near, near, near,
    ]
    return pl.pallas_call(
        functools.partial(backward_kernel, shards, mesh_rows, sliced_rows),
        grid=(slots // BLOCK,),
        in_specs=[
            pl.BlockSpec(memory_space=pltpu.SMEM), line, line, edge, edge, full(wout), full(lat),
        ],
        out_specs=[full(out) for out in outs],
        out_shape=outs,
        scratch_shapes=[
            pltpu.VMEM(lat.shape, F32),
            pltpu.VMEM((WINDOW_ROWS, width), F32),
            pltpu.VMEM((8, width), F32),
            pltpu.VMEM((width, width), F32),
        ],
        compiler_params=pltpu.CompilerParams(vmem_limit_bytes=VMEM),
        cost_estimate=cost(5 * slots * width * width, 4 * slots * width),
        name="edge_backward",
    )(place, send, recv, dout, slope, wout, lat)


def combine_kernel(parts, vkeep_ref, vrecv_ref, gkeep_ref, grecv_ref, vpart_ref, gsend_ref, gown_ref):
    half = vkeep_ref.shape[0] - 8
    near = vrecv_ref[...].astype(F32)
    bias = vkeep_ref[half : half + 1, :] + near[half : half + 1] + near[half + 1 : half + 2]
    store_slabs(vpart_ref, vkeep_ref[:half, :] + near[:half], bias, parts)
    gown_ref[...] = gkeep_ref[0] + grecv_ref[0].astype(F32)
    gsend_ref[...] = (gkeep_ref[1] + grecv_ref[1].astype(F32)).astype(BF16)


def combine(parts, vkeep, vrecv, gkeep, grecv):
    width = vkeep.shape[1]
    chunk = chunk_of(width, 2 * parts)
    chunk = jax.ShapeDtypeStruct((parts,) + chunk.shape[1:], chunk.dtype)
    return pl.pallas_call(
        functools.partial(combine_kernel, parts),
        out_shape=[
            chunk,
            jax.ShapeDtypeStruct(gkeep.shape[1:], BF16),
            jax.ShapeDtypeStruct(gkeep.shape[1:], F32),
        ],
        compiler_params=pltpu.CompilerParams(vmem_limit_bytes=VMEM),
        cost_estimate=cost(2 * vkeep.size, 8 * vkeep.size),
        name="combine_halves",
    )(vkeep, vrecv, gkeep, grecv)


def sum_slabs(source_ref, vector_ref):
    tiles = vector_ref.shape[1] // LANES
    slab = source_ref.shape[1] - 2 * tiles
    total = jnp.sum(source_ref[...].astype(F32), axis=0)
    both = total[slab : slab + tiles] + total[slab + tiles :]
    for j in range(tiles):
        vector_ref[:, j * LANES : (j + 1) * LANES] = both[j : j + 1]
    return total[:slab]


def first_kernel(w_ref, slab_ref, dgain_ref):
    slab_ref[...] = sum_slabs(w_ref, dgain_ref)


def first_reduce(w, width):
    slab = w.shape[1] - 2 * width // LANES
    return pl.pallas_call(
        first_kernel,
        out_shape=[
            jax.ShapeDtypeStruct((slab, LANES), F32),
            jax.ShapeDtypeStruct((1, width), F32),
        ],
        compiler_params=pltpu.CompilerParams(vmem_limit_bytes=VMEM),
        cost_estimate=cost(2 * w.size, 2 * w.size),
        name="first_slabs",
    )(w)


def tiles_of(rows):
    return [rows[:, j : j + LANES] for j in range(0, rows.shape[1], LANES)]


def second_kernel(
    v_ref, first_ref, lat_ref, own_ref, pair_ref, other_ref, wsend_ref,
    pay_ref, dmesh_ref, dbias_ref,
):
    mesh = own_ref[...] + pair_ref[...] + other_ref[...]
    pieces = [first_ref[...], sum_slabs(v_ref, dbias_ref)]
    pieces += tiles_of(mesh) + tiles_of(lat_ref[...].astype(F32))
    payload = jnp.concatenate(pieces, axis=0).astype(BF16)
    pay_ref[...] = jnp.broadcast_to(payload[None], pay_ref.shape)
    dmesh_ref[...] = mix(mesh.astype(BF16), wsend_ref[...], 1, 1)


def second_reduce(shards, v, first, lat, own, pair, other, wsend):
    mesh_rows, width = lat.shape
    rows = 2 * first.shape[0] + 2 * mesh_rows * width // LANES
    return pl.pallas_call(
        second_kernel,
        out_shape=[
            jax.ShapeDtypeStruct((shards, rows, LANES), BF16),
            jax.ShapeDtypeStruct((mesh_rows, width), F32),
            jax.ShapeDtypeStruct((1, width), F32),
        ],
        compiler_params=pltpu.CompilerParams(vmem_limit_bytes=VMEM),
        cost_estimate=cost(2 * v.size, 4 * v.size),
        name="second_slabs",
    )(v, first, lat, own, pair, other, wsend)


def spread_kernel(levels, mesh_rows, place_ref, *refs):
    parts_refs = refs[:levels]
    dsend_ref, drecv_ref, dout_ref, mesh, lat = refs[levels:]
    width = dsend_ref.shape[0]
    tiles = width // LANES
    shards = parts_refs[0].shape[0]
    own = width // (shards * levels)
    slab = own * tiles
    level = place_ref[1] * 2 + place_ref[2]
    for k, ref in enumerate(parts_refs):
        for s in range(shards):
            at = level ^ k
            part = s * levels + at
            high, low = lax.shift_right_logical(at, 1), at & 1
            place = (low * shards + s) * (levels // 2) + high
            tail = ref[s, 2 * slab :, :].astype(F32)
            rows = pl.ds(pl.multiple_of(part * own, own), own)
            recv_rows = pl.ds(pl.multiple_of(place * own, own), own)
            near = pl.ds(pl.multiple_of(part * mesh_rows, mesh_rows), mesh_rows)
            for j in range(tiles):
                cols = pl.ds(j * LANES, LANES)
                dout_ref[rows, cols] = ref[s, j * own : (j + 1) * own, :]
                drecv_ref[recv_rows, cols] = ref[s, slab + j * own : slab + (j + 1) * own, :]
                mesh[near, cols] = tail[j * mesh_rows : (j + 1) * mesh_rows]
                lat[near, cols] = tail[(tiles + j) * mesh_rows : (tiles + j + 1) * mesh_rows]
    dsend_ref[...] = mix(lat[...].astype(BF16), mesh[...].astype(BF16), 0, 0).astype(BF16)


def spread(width, mesh_rows, place, received):
    levels = len(received)
    rows = received[0].shape[0] * levels * mesh_rows
    out = jax.ShapeDtypeStruct((width, width), BF16)
    return pl.pallas_call(
        functools.partial(spread_kernel, levels, mesh_rows),
        in_specs=[pl.BlockSpec(memory_space=pltpu.SMEM)]
        + [pl.BlockSpec(memory_space=pltpu.VMEM)] * levels,
        out_shape=[out, out, out],
        scratch_shapes=[pltpu.VMEM((rows, width), F32)] * 2,
        compiler_params=pltpu.CompilerParams(vmem_limit_bytes=VMEM),
        cost_estimate=cost(2 * rows * width * width, 8 * width * width),
        name="spread_weights",
    )(place, *received)


def swap(x, axis, bit):
    return lax.ppermute(x, axis, [(i, i ^ bit) for i in range(lax.axis_size(axis))])


def swap_between(x, axis):
    count = lax.axis_size(axis)
    pairs = [(i, i + 1) for i in range(1, count - 1, 2)]
    return lax.ppermute(x, axis, pairs + [(j, i) for i, j in pairs])


def body(
    grid_latent, mesh_latent, grid_output_cotangent, w_send, w_recv, output_weight,
    hidden_layer_bias, output_norm_gain, edge_sender, edge_receiver, edge_live,
):
    shards, levels = lax.axis_size("space"), lax.axis_size("high") * 2
    parts = shards * levels
    width = grid_latent.shape[1]
    mesh_rows = mesh_latent.shape[1]
    lat = mesh_latent[0]
    whole_slabs = sliced(width, parts)
    place = jnp.stack([lax.axis_index(axis) for axis in ALL]).astype(jnp.int32)

    lat_pair = swap(lat, "space", 1)
    lat_other = swap_between(lat, "space")
    pre, cot = gather(edge_receiver, edge_live, grid_latent, grid_output_cotangent, w_recv)
    wpart, dout, slope = forward(
        shards, levels, place, edge_sender, pre, cot, lat, lat_pair, lat_other, w_send,
        output_weight, hidden_layer_bias[None], output_norm_gain[None],
    )
    if whole_slabs:
        wrecv = lax.all_to_all(wpart, ALL, 0, 0, tiled=False)
    vsend, vkeep, gsend, gkeep, own, pair, other = backward(
        shards, levels, mesh_rows, place, edge_sender, edge_receiver, dout, slope,
        output_weight, grid_latent,
    )
    pair = swap(pair, "space", 1)
    other = swap_between(other, "space")

    if not whole_slabs:
        rows = jnp.stack([gkeep.astype(BF16), gsend])
        for k in range(1, levels):
            side = rows[k % 2, k // 2]
            for bit in (1, 2):
                if k & bit:
                    side = swap(side, ("low", "high")[bit // 2], 1)
            gkeep = gkeep.at[0].add(side.astype(F32))
        d_grid = mix(gkeep[0].astype(BF16), w_recv, 1, 1)
        mesh = (own + pair + other).astype(BF16)
        d_mesh = mix(mesh, w_send, 1, 1)
        totals = lax.psum((mix(lat, mesh, 0, 0), vkeep, wpart), ALL)
        d_w = [total[:width].astype(BF16) for total in totals]
        return (d_grid, d_mesh[None], *d_w, totals[1][width], totals[2][width])

    vnear = swap(vsend, "low", 1)
    gnear = swap(gsend, "low", 1)
    vpart, gsend, gown = combine(parts // 2, vkeep, vnear, gkeep, gnear)
    gfar = swap(gsend, "high", 1)
    vrecv = lax.all_to_all(vpart, MOST, 0, 0, tiled=False)
    d_grid = mix((gown + gfar.astype(F32)).astype(BF16), w_recv, 1, 1)
    first, d_gain = first_reduce(wrecv, width)
    payload, d_mesh, d_bias = second_reduce(
        shards, vrecv, first, lat, own, pair, other, w_send
    )
    received = {0: lax.all_to_all(payload, "space", 0, 0, tiled=False)}
    received[2] = swap(received[0], "high", 1)
    received[1] = swap(received[0], "low", 1)
    received[3] = swap(received[2], "low", 1)
    d_w_send, d_w_recv, d_w_out = spread(
        width, mesh_rows, place, [received[k] for k in range(levels)]
    )
    return (d_grid, d_mesh[None], d_w_send, d_w_recv, d_w_out, d_bias[0], d_gain[0])


def solution(mesh):
    shards, levels = mesh.devices.shape
    split_mesh = Mesh(mesh.devices.reshape(shards, levels // 2, 2), ALL)
    level = MOST[1:] + ALL[2:]

    return jax.shard_map(
        body,
        mesh=split_mesh,
        in_specs=(
            P("space", None), P(level, "space", None), P("space", None), P(), P(), P(), P(), P(),
            P(level, "space"), P(level, "space"), P(level, "space"),
        ),
        out_specs=(P(ALL, None), P(level, "space", None), P(), P(), P(), P(), P()),
        check_vma=False,
    )
```

time: 118 us -> 101 us (0.86)
  blocking collectives: 34.9 us -> 14.9 us
  Pallas kernels: 31.2 us -> 35.4 us
  starting transfers between devices: 21.8 us -> 19.8 us
  waiting for transfers between devices: 23 us -> 24.5 us
    all_to_all x2 -> x1, blocking collectives: 34.9 us -> 14.9 us  [body(): received = {0: lax.all_to_all(payload, 'space', 0, 0, tiled=False)}]
    ppermute x3 -> x8, waiting for transfers between devices: 2.59 us -> 14.1 us  [swap(): lax.ppermute(x, axis, [(i, i ^ bit) for i in range(lax.axis_size(axis))])]
    ppermute x3 -> x8, starting transfers between devices: 1.88 us -> 9.59 us  [swap(): lax.ppermute(x, axis, [(i, i ^ bit) for i in range(lax.axis_size(axis))])]
    all_to_all x2 -> x1, starting transfers between devices: 10.8 us -> 4.21 us  [body(): vrecv = lax.all_to_all(vpart, MOST, 0, 0, tiled=False)]
    all_to_all x1, waiting for transfers between devices: 9.35 us -> 4.1 us  [body(): wrecv = lax.all_to_all(wpart, ALL, 0, 0, tiled=False)]
    ppermute x2, starting transfers between devices: 5.97 us -> 1.31 us  [swap_between(): return lax.ppermute(x, axis, pairs + [(j, i) for i, j in pairs])]
    pallas_call x3 -> x5, Pallas kernels: 22.4 us -> 26.4 us  [the longest x1 12.8 us: forward(): pl.pallas_call(functools.partial(forward_kernel, shards, parts), grid=(sl...]
    all_to_all x2 -> x1, waiting for transfers between devices: 9.63 us -> 6.31 us  [body(): vrecv = lax.all_to_all(vpart, MOST, 0, 0, tiled=False)]
  transfers between devices with their start and end apart: 8 -> 12, of which waited for: 5 -> 5; matrix products, arithmetic and copies ran while one was open for 1% -> 2% of each run, Pallas kernels for 5% -> 17%
where the time goes in v2:
time: 101 us
  Pallas kernels  35.4 us (35%)
  waiting for transfers between devices  24.5 us (24%)
  starting transfers between devices  19.8 us (20%)
  blocking collectives  14.9 us (15%)
  local copies, waits for them, and re-layouts  3.61 us (4%)
  matrix products  1.01 us (1%)
    all_to_all x1, blocking collectives, body(): received = {0: lax.all_to_all(payload, 'space', 0, 0, tiled=False)}  14.9 us
    ppermute x8, waiting for transfers between devices, swap(): lax.ppermute(x, axis, [(i, i ^ bit) for i in range(lax.axis_size(axis))])  14.1 us
    pallas_call x1, Pallas kernels, forward(): pl.pallas_call(functools.partial(forward_kernel, shards, parts), grid=(sl...  12.8 us
    ppermute x8, starting transfers between devices, swap(): lax.ppermute(x, axis, [(i, i ^ bit) for i in range(lax.axis_size(axis))])  9.59 us
    pallas_call x1, Pallas kernels, backward(): pl.pallas_call(functools.partial(backward_kernel, shards, mesh_rows, slic...  7.37 us
    all_to_all x1, waiting for transfers between devices, body(): vrecv = lax.all_to_all(vpart, MOST, 0, 0, tiled=False)  6.31 us
    pallas_call x1, Pallas kernels, gather(): pl.pallas_call(gather_kernel, grid=(slots // BLOCK,), in_specs=[line, lin...  6.1 us
    all_to_all x1, starting transfers between devices, body(): wrecv = lax.all_to_all(wpart, ALL, 0, 0, tiled=False)  4.73 us
  transfers between devices with their start and end apart: 12, of which 5 were waited for; matrix products, arithmetic and copies ran while one was open for 2% of the time, Pallas kernels for 17%

profile of v2, /device:TPU:0, one launch (start us, length us, event | category | flops | bytes accessed | tf_op | source)
XLA Modules:
  0.0 100.6 jit_solution(8342160352297238559)
XLA Ops:
  0.6 0.7 collective-permute-start.1
  1.3 5.8 %collective-permute-start = (bf16[8,512]{1,0:T(8,128)(2,1)}, bf16[8,512]{1,0:T(8,128)(2,1)S(1)}, u32[]{:S(2)}, u32[]{:S(2)}) collective-permute-start(bf16[8,512]{1,0:T(8,128)(2,1)} %bitcast.11), channel_id=1, source_target_pairs={{0,4},{4,0},{8,12},{12,8},{16,20},{20,16},{24,28},{28,24},{1,5},{5... | collective-permute-start | bytes 24584 | tf_op jit(solution)/shard_map/ppermute | solution.py:447
  7.1 6.1 %edge_gather.1 = (bf16[2048,512]{1,0:T(8,128)(2,1)}, bf16[2048,512]{1,0:T(8,128)(2,1)}) custom-call(s32[1,2048]{1,0:T(1,128)} %recv_ref.3, s32[1,2048]{1,0:T(1,128)} %live_ref.1, bf16[512,512]{1,0:T(8,128)(2,1)} %lat_ref.3, bf16[512,512]{1,0:T(8,128)(2,1)} %cot_ref.1, bf16[512,512]{1,0:T(8,128)(2,1)} %w_ref.1), custom_call_target="tpu_custom_call" | custom-call | flops 2147483648 | bytes 6291456 | tf_op jit(solution)/shard_map/edge_gather/pallas_call | solution.py:123
  13.2 0.6 pad_add_fusion.place_ref
  13.8 0.0 collective-permute-done.1.other_ref
  13.8 0.0 collective-permute-done.pair_ref
  13.8 0.0 copy-start.16
  13.9 0.6 copy-done.15
  14.4 0.0 copy-done.16
  14.4 12.8 %edge_forward.1 = (bf16[32,72,128]{2,1,0:T(8,128)(2,1)}, bf16[2048,512]{1,0:T(8,128)(2,1)}, bf16[2048,512]{1,0:T(8,128)(2,1)}) custom-call(s32[3]{0:T(128)} %pad_add_fusion.place_ref, s32[1,2048]{1,0:T(1,128)} %send_ref.3, bf16[2048,512]{1,0:T(8,128)(2,1)} %get-tuple-element.30.pre_ref, bf16[2048,512]{1,0:T(8,128)(2,1)} %get-tuple-element.31.cot_ref, ...), custom_call_target="tpu_custom_call" | custom-call | flops 2684354560 | bytes 8388608 | tf_op jit(solution)/shard_map/edge_forward/pallas_call | solution.py:197
  27.3 4.7 %all-to-all-start.1 = ((bf16[32,72,128]{2,1,0:T(8,128)(2,1)}), bf16[32,72,128]{2,1,0:T(8,128)(2,1)S(1)}, u32[]{:S(2)}, u32[]{:S(2)}) async-start(bf16[32,72,128]{2,1,0:T(8,128)(2,1)} %get-tuple-element.41), calls=%async_computation.1 | async-start | bytes 1179648 | tf_op jit(solution)/shard_map/all_to_all | solution.py:476
  32.0 7.4 %edge_backward.1 = (bf16[264,512]{1,0:T(8,128)(2,1)}, f32[264,512]{1,0:T(8,128)}, bf16[2,128,512]{2,1,0:T(8,128)(2,1)}, f32[2,128,512]{2,1,0:T(8,128)}, f32[8,51...) custom-call(s32[3]{0:T(128)} %pad_add_fusion.place_ref, s32[1,2048]{1,0:T(1,128)} %send_ref.3, s32[1,2048]{1,0:T(1,128)} %recv_ref.3, ...), custom_call_target="tpu_custom_call" | custom-call | flops 2684354560 | bytes 4194304 | tf_op jit(solution)/shard_map/edge_backward/pallas_call | solution.py:296
  39.4 0.0 copy-start.14
  39.4 0.0 copy-start.13
  39.4 0.3 collective-permute-start.2
  39.7 0.3 collective-permute-start.3
  40.0 1.6 %collective-permute-done.3.grecv_ref = bf16[2,128,512]{2,1,0:T(8,128)(2,1)S(1)} collective-permute-done((bf16[2,128,512]{2,1,0:T(8,128)(2,1)}, bf16[2,128,512]{2,1,0:T(8,128)(2,1)S(1)}, u32[]{:S(2)}, u32[]{:S(2)}) %collective-permute-start.3) | collective-permute-done | bytes 262176 | tf_op jit(solution)/shard_map/ppermute | solution.py:447
  41.6 0.0 collective-permute-done.2.vrecv_ref
  41.6 0.7 copy-done.8
  42.3 0.1 copy-done.7
  42.4 2.3 %combine_halves.1 = (bf16[16,72,128]{2,1,0:T(8,128)(2,1)}, bf16[128,512]{1,0:T(8,128)(2,1)}, f32[128,512]{1,0:T(8,128)}) custom-call(f32[264,512]{1,0:T(8,128)} %get-tuple-element.34.vkeep_ref, bf16[264,512]{1,0:T(8,128)(2,1)} %copy-done.7, f32[2,128,512]{2,1,0:T(8,128)} %get-tuple-element.36.gkeep_ref, bf16[2,128,512]{2,1,0:T(8,128)(2,1)} %copy-done.8), custom_call_target="tpu_custom_call" | custom-call | flops 270336 | bytes 1081344 | tf_op jit(solution)/shard_map/combine_halves/pallas_call | solution.py:329
  44.7 4.1 %all-to-all-done.1.w_ref = bf16[32,72,128]{2,1,0:T(8,128)(2,1)S(1)} async-done(((bf16[32,72,128]{2,1,0:T(8,128)(2,1)}), bf16[32,72,128]{2,1,0:T(8,128)(2,1)S(1)}, u32[]{:S(2)}, u32[]{:S(2)}) %all-to-all-start.1) | async-done | bytes 589856 | tf_op jit(solution)/shard_map/all_to_all | solution.py:476
  48.8 4.2 %all-to-all-start = ((bf16[16,72,128]{2,1,0:T(8,128)(2,1)}), bf16[16,72,128]{2,1,0:T(8,128)(2,1)S(1)}, u32[]{:S(2)}, u32[]{:S(2)}) async-start(bf16[16,72,128]{2,1,0:T(8,128)(2,1)} %get-tuple-element.40), calls=%async_computation | async-start | bytes 589824 | tf_op jit(solution)/shard_map/all_to_all | solution.py:503
  53.0 0.0 copy-done.14
  53.1 2.0 %collective-permute-start.5 = (f32[8,512]{1,0:T(8,128)S(1)}, f32[8,512]{1,0:T(8,128)S(1)}, u32[]{:S(2)}, u32[]{:S(2)}) collective-permute-start(f32[8,512]{1,0:T(8,128)S(1)} %copy-done.14), channel_id=1, source_target_pairs={{0,4},{4,0},{8,12},{12,8},{16,20},{20,16},{24,28},{28,24},{1,5},{5... | collective-permute-start | bytes 49160 | tf_op jit(solution)/shard_map/ppermute | solution.py:447
  55.0 0.0 copy-done.13
  55.0 0.7 collective-permute-start.6
  55.7 1.8 %first_slabs.1 = (f32[64,128]{1,0:T(8,128)}, f32[1,512]{1,0:T(1,128)}) custom-call(bf16[32,72,128]{2,1,0:T(8,128)(2,1)} %copy-done), custom_call_target="tpu_custom_call" | custom-call | flops 589824 | bytes 589824 | tf_op jit(solution)/shard_map/first_slabs/pallas_call | solution.py:358
  57.5 0.0 collective-permute-done.5.pair_ref
  57.5 0.0 collective-permute-done.6.other_ref
  57.5 0.0 copy-start.11
  57.5 6.3 %all-to-all-done.v_ref = bf16[16,72,128]{2,1,0:T(8,128)(2,1)S(1)} async-done(((bf16[16,72,128]{2,1,0:T(8,128)(2,1)}), bf16[16,72,128]{2,1,0:T(8,128)(2,1)S(1)}, u32[]{:S(2)}, u32[]{:S(2)}) %all-to-all-start) | async-done | bytes 294944 | tf_op jit(solution)/shard_map/all_to_all | solution.py:503
  63.8 0.0 copy-done.10
  63.8 0.7 copy-done.2
  64.5 2.1 %second_slabs.1 = (bf16[8,192,128]{2,1,0:T(8,128)(2,1)}, f32[8,512]{1,0:T(8,128)}, f32[1,512]{1,0:T(1,128)}) custom-call(bf16[16,72,128]{2,1,0:T(8,128)(2,1)} %copy-done.2, f32[64,128]{1,0:T(8,128)} %get-tuple-element.42.first_ref, bf16[8,512]{1,0:T(8,128)(2,1)} %bitcast.13, f32[8,512]{1,0:T(8,128)} %get-tuple-element.43.own_ref, f32[8,512]{1,0:T(8,128)} %copy-done.10, ...), custom_call_target="tpu_custom_call" | custom-call | flops 294912 | bytes 589824 | tf_op jit(solution)/shard_map/second_slabs/pallas_call | solution.py:389
  66.7 14.9 %all_to_all.15.refs_0_ = bf16[8,192,128]{2,1,0:T(8,128)(2,1)S(1)} all-to-all(bf16[8,192,128]{2,1,0:T(8,128)(2,1)} %get-tuple-element.47), channel_id=1, replica_groups=mesh['space'=8,'high'=2,'low'=2] {'space'}, dimensions={0} | all-to-all | bytes 786432 | tf_op jit(solution)/shard_map/all_to_all | solution.py:509
  81.6 0.6 collective-permute-start.8
  82.1 0.0 collective-permute-start.7
  82.1 7.2 %collective-permute-done.8.refs_2_ = bf16[8,192,128]{2,1,0:T(8,128)(2,1)S(1)} collective-permute-done((bf16[8,192,128]{2,1,0:T(8,128)(2,1)S(1)}, bf16[8,192,128]{2,1,0:T(8,128)(2,1)S(1)}, u32[]{:S(2)}, u32[]{:S(2)}) %collective-permute-start.8) | collective-permute-done | bytes 393248 | tf_op jit(solution)/shard_map/ppermute | solution.py:447
  89.3 0.0 collective-permute-start.9
  89.4 0.6 collective-permute-start.4
  90.0 5.3 %collective-permute-done.4 = bf16[128,512]{1,0:T(8,128)(2,1)S(1)} collective-permute-done((bf16[128,512]{1,0:T(8,128)(2,1)S(1)}, bf16[128,512]{1,0:T(8,128)(2,1)S(1)}, u32[]{:S(2)}, u32[]{:S(2)}) %collective-permute-start.4) | collective-permute-done | bytes 131104 | tf_op jit(solution)/shard_map/ppermute | solution.py:447
  95.3 1.0 %fusion = f32[128,512]{1,0:T(8,128)} fusion(bf16[512,512]{1,0:T(8,128)(2,1)S(1)} %copy-done.3, f32[128,512]{1,0:T(8,128)S(1)} %copy-done.9, bf16[128,512]{1,0:T(8,128)(2,1)S(1)} %collective-permute-done.4), kind=kOutput, calls=%fused_computation.1 | convolution fusion | flops 67305472 | bytes 1179648 | tf_op jit(solution)/shard_map/dot_general | solution.py:38
  96.3 0.0 collective-permute-done.7.refs_1_
  96.3 0.0 collective-permute-done.9.refs_3_
  96.3 0.7 copy-done.5
  97.0 0.7 copy-done.6
  97.8 2.8 %spread_weights.1 = (bf16[512,512]{1,0:T(8,128)(2,1)}, bf16[512,512]{1,0:T(8,128)(2,1)}, bf16[512,512]{1,0:T(8,128)(2,1)}) custom-call(s32[3]{0:T(128)} %pad_add_fusion.place_ref, bf16[8,192,128]{2,1,0:T(8,128)(2,1)} %copy-done.1, bf16[8,192,128]{2,1,0:T(8,128)(2,1)} %copy-done.5, bf16[8,192,128]{2,1,0:T(8,128)(2,1)} %copy-done.4, bf16[8,192,128]{2,1,0:T(8,128)(2,1)} %copy-done.6), custom_call_target="tpu_custom_call" | custom-call | flops 134217728 | bytes 2097152 | tf_op jit(solution)/shard_map/spread_weights/pallas_call | solution.py:434
  (20 shorter events, 0.0 us)
Async XLA Ops:
  0.6 13.2 %collective-permute-start.1 = (bf16[8,512]{1,0:T(8,128)(2,1)}, bf16[8,512]{1,0:T(8,128)(2,1)S(1)}, u32[]{:S(2)}, u32[]{:S(2)}) collective-permute-start(bf16[8,512]{1,0:T(8,128)(2,1)} %bitcast.10), channel_id=1, source_target_pairs={{4,8},{12,16},{20,24},{8,4},{16,12},{24,20},{5,9},{13,17},{21,25},... | collective-permute-start | bytes 24584 | tf_op jit(solution)/shard_map/ppermute | solution.py:453
  1.3 12.5 %collective-permute-start = (bf16[8,512]{1,0:T(8,128)(2,1)}, bf16[8,512]{1,0:T(8,128)(2,1)S(1)}, u32[]{:S(2)}, u32[]{:S(2)}) collective-permute-start(bf16[8,512]{1,0:T(8,128)(2,1)} %bitcast.11), channel_id=1, source_target_pairs={{0,4},{4,0},{8,12},{12,8},{16,20},{20,16},{24,28},{28,24},{1,5},{5... | collective-permute-start | bytes 24584 | tf_op jit(solution)/shard_map/ppermute | solution.py:447
  13.8 0.6 copy-start.15
  13.8 0.6 copy-start.16
  27.3 21.5 %all-to-all-start.1 = ((bf16[32,72,128]{2,1,0:T(8,128)(2,1)}), bf16[32,72,128]{2,1,0:T(8,128)(2,1)S(1)}, u32[]{:S(2)}, u32[]{:S(2)}) async-start(bf16[32,72,128]{2,1,0:T(8,128)(2,1)} %get-tuple-element.41), calls=%async_computation.1 | async-start | bytes 1179648 | tf_op jit(solution)/shard_map/all_to_all | solution.py:476
  39.4 13.6 %copy-start.14 = (f32[8,512]{1,0:T(8,128)S(1)}, f32[8,512]{1,0:T(8,128)}, u32[]{:S(2)}) copy-start(f32[8,512]{1,0:T(8,128)} %get-tuple-element.44) | copy-start | bytes 49156
  39.4 15.6 %copy-start.13 = (f32[8,512]{1,0:T(8,128)S(1)}, f32[8,512]{1,0:T(8,128)}, u32[]{:S(2)}) copy-start(f32[8,512]{1,0:T(8,128)} %get-tuple-element.45) | copy-start | bytes 49156
  39.4 2.2 %collective-permute-start.2 = (bf16[264,512]{1,0:T(8,128)(2,1)}, bf16[264,512]{1,0:T(8,128)(2,1)S(1)}, u32[]{:S(2)}, u32[]{:S(2)}) collective-permute-start(bf16[264,512]{1,0:T(8,128)(2,1)} %get-tuple-element.35), channel_id=1, source_target_pairs={{0,1},{1,0},{2,3},{3,2},{4,5},{5,4},{6,7},{7,6},{8,9},{9,8},{10,11... | collective-permute-start | bytes 811016 | tf_op jit(solution)/shard_map/ppermute | solution.py:447
  39.7 1.9 %collective-permute-start.3 = (bf16[2,128,512]{2,1,0:T(8,128)(2,1)}, bf16[2,128,512]{2,1,0:T(8,128)(2,1)S(1)}, u32[]{:S(2)}, u32[]{:S(2)}) collective-permute-start(bf16[2,128,512]{2,1,0:T(8,128)(2,1)} %get-tuple-element.37), channel_id=1, source_target_pairs={{0,1},{1,0},{2,3},{3,2},{4,5},{5,4},{6,7},{7,6},{8,9},{9,8},{10,11... | collective-permute-start | bytes 786440 | tf_op jit(solution)/shard_map/ppermute | solution.py:447
  41.6 0.7 copy-start.8
  41.6 0.8 copy-start.7
  42.4 52.9 %copy-start.3 = (bf16[512,512]{1,0:T(8,128)(2,1)S(1)}, bf16[512,512]{1,0:T(8,128)(2,1)}, u32[]{:S(2)}) copy-start(bf16[512,512]{1,0:T(8,128)(2,1)} %w_ref.1) | copy-start | bytes 1572868
  44.7 44.6 %copy-start.12 = (bf16[128,512]{1,0:T(8,128)(2,1)S(1)}, bf16[128,512]{1,0:T(8,128)(2,1)}, u32[]{:S(2)}) copy-start(bf16[128,512]{1,0:T(8,128)(2,1)} %get-tuple-element.39) | copy-start | bytes 393220
  44.7 50.5 %copy-start.9 = (f32[128,512]{1,0:T(8,128)S(1)}, f32[128,512]{1,0:T(8,128)}, u32[]{:S(2)}) copy-start(f32[128,512]{1,0:T(8,128)} %get-tuple-element.38) | copy-start | bytes 786436
  48.8 6.9 %copy-start = (bf16[32,72,128]{2,1,0:T(8,128)(2,1)}, bf16[32,72,128]{2,1,0:T(8,128)(2,1)S(1)}, u32[]{:S(2)}) copy-start(bf16[32,72,128]{2,1,0:T(8,128)(2,1)S(1)} %all-to-all-done.1.w_ref) | copy-start | bytes 1769476
  48.8 15.0 %all-to-all-start = ((bf16[16,72,128]{2,1,0:T(8,128)(2,1)}), bf16[16,72,128]{2,1,0:T(8,128)(2,1)S(1)}, u32[]{:S(2)}, u32[]{:S(2)}) async-start(bf16[16,72,128]{2,1,0:T(8,128)(2,1)} %get-tuple-element.40), calls=%async_computation | async-start | bytes 589824 | tf_op jit(solution)/shard_map/all_to_all | solution.py:503
  53.1 4.4 %collective-permute-start.5 = (f32[8,512]{1,0:T(8,128)S(1)}, f32[8,512]{1,0:T(8,128)S(1)}, u32[]{:S(2)}, u32[]{:S(2)}) collective-permute-start(f32[8,512]{1,0:T(8,128)S(1)} %copy-done.14), channel_id=1, source_target_pairs={{0,4},{4,0},{8,12},{12,8},{16,20},{20,16},{24,28},{28,24},{1,5},{5... | collective-permute-start | bytes 49160 | tf_op jit(solution)/shard_map/ppermute | solution.py:447
  55.0 2.5 %collective-permute-start.6 = (f32[8,512]{1,0:T(8,128)S(1)}, f32[8,512]{1,0:T(8,128)S(1)}, u32[]{:S(2)}, u32[]{:S(2)}) collective-permute-start(f32[8,512]{1,0:T(8,128)S(1)} %copy-done.13), channel_id=1, source_target_pairs={{4,8},{12,16},{20,24},{8,4},{16,12},{24,20},{5,9},{13,17},{21,25},... | collective-permute-start | bytes 49160 | tf_op jit(solution)/shard_map/ppermute | solution.py:453
  57.5 6.3 %copy-start.10 = (f32[8,512]{1,0:T(8,128)}, f32[8,512]{1,0:T(8,128)S(1)}, u32[]{:S(2)}) copy-start(f32[8,512]{1,0:T(8,128)S(1)} %collective-permute-done.5.pair_ref) | copy-start | bytes 49156
  57.5 6.3 %copy-start.11 = (f32[8,512]{1,0:T(8,128)}, f32[8,512]{1,0:T(8,128)S(1)}, u32[]{:S(2)}) copy-start(f32[8,512]{1,0:T(8,128)S(1)} %collective-permute-done.6.other_ref) | copy-start | bytes 49156
  63.8 0.7 copy-start.2
  81.6 14.7 %copy-start.1 = (bf16[8,192,128]{2,1,0:T(8,128)(2,1)}, bf16[8,192,128]{2,1,0:T(8,128)(2,1)S(1)}, u32[]{:S(2)}) copy-start(bf16[8,192,128]{2,1,0:T(8,128)(2,1)S(1)} %all_to_all.15.refs_0_) | copy-start | bytes 1179652
  81.6 7.8 %collective-permute-start.8 = (bf16[8,192,128]{2,1,0:T(8,128)(2,1)S(1)}, bf16[8,192,128]{2,1,0:T(8,128)(2,1)S(1)}, u32[]{:S(2)}, u32[]{:S(2)}) collective-permute-start(bf16[8,192,128]{2,1,0:T(8,128)(2,1)S(1)} %all_to_all.15.refs_0_), channel_id=1, source_target_pairs={{0,2},{2,0},{1,3},{3,1},{4,6},{6,4},{5,7},{7,5},{8,10},{10,8},{9,1... | collective-permute-start | bytes 1179656 | tf_op jit(solution)/shard_map/ppermute | solution.py:447
  82.1 14.2 %collective-permute-start.7 = (bf16[8,192,128]{2,1,0:T(8,128)(2,1)S(1)}, bf16[8,192,128]{2,1,0:T(8,128)(2,1)S(1)}, u32[]{:S(2)}, u32[]{:S(2)}) collective-permute-start(bf16[8,192,128]{2,1,0:T(8,128)(2,1)S(1)} %all_to_all.15.refs_0_), channel_id=1, source_target_pairs={{0,1},{1,0},{2,3},{3,2},{4,5},{5,4},{6,7},{7,6},{8,9},{9,8},{10,11... | collective-permute-start | bytes 1179656 | tf_op jit(solution)/shard_map/ppermute | solution.py:447
  89.3 7.0 %copy-start.4 = (bf16[8,192,128]{2,1,0:T(8,128)(2,1)}, bf16[8,192,128]{2,1,0:T(8,128)(2,1)S(1)}, u32[]{:S(2)}) copy-start(bf16[8,192,128]{2,1,0:T(8,128)(2,1)S(1)} %collective-permute-done.8.refs_2_) | copy-start | bytes 1179652
  89.3 6.9 %collective-permute-start.9 = (bf16[8,192,128]{2,1,0:T(8,128)(2,1)S(1)}, bf16[8,192,128]{2,1,0:T(8,128)(2,1)S(1)}, u32[]{:S(2)}, u32[]{:S(2)}) collective-permute-start(bf16[8,192,128]{2,1,0:T(8,128)(2,1)S(1)} %collective-permute-done.8.refs_2_), channel_id=1, source_target_pairs={{0,1},{1,0},{2,3},{3,2},{4,5},{5,4},{6,7},{7,6},{8,9},{9,8},{10,11... | collective-permute-start | bytes 1179656 | tf_op jit(solution)/shard_map/ppermute | solution.py:447
  89.4 5.9 %collective-permute-start.4 = (bf16[128,512]{1,0:T(8,128)(2,1)S(1)}, bf16[128,512]{1,0:T(8,128)(2,1)S(1)}, u32[]{:S(2)}, u32[]{:S(2)}) collective-permute-start(bf16[128,512]{1,0:T(8,128)(2,1)S(1)} %copy-done.12), channel_id=1, source_target_pairs={{0,2},{2,0},{1,3},{3,1},{4,6},{6,4},{5,7},{7,5},{8,10},{10,8},{9,1... | collective-permute-start | bytes 393224 | tf_op jit(solution)/shard_map/ppermute | solution.py:447
  96.3 0.8 copy-start.5
  97.0 0.7 copy-start.6

commit v3 on v2

v3 whole, which is shorter than its diff:
```python
import functools

import jax
import jax.numpy as jnp
from jax import lax
from jax.experimental import pallas as pl
from jax.experimental.pallas import tpu as pltpu
from jax.sharding import Mesh, PartitionSpec as P


F32 = jnp.float32
BF16 = jnp.bfloat16
ALL = ("space", "high", "low")
MOST = ("space", "high")
LANES = 128
BLOCK = 1024
SUB = 512
WINDOW_ROWS = 32
VMEM = 16 * 1024 * 1024
EDGE_VMEM = 60 * 1024 * 1024


def sliced(width, parts):
    return width % (16 * parts) == 0


def cost(flops, nbytes):
    return pl.CostEstimate(flops=flops, bytes_accessed=nbytes, transcendentals=0)


def mix(a, b, left, right):
    return lax.dot_general(a, b, (((left,), (right,)), ((), ())), preferred_element_type=F32)


def full(array):
    return pl.BlockSpec(array.shape, lambda *_: (0,) * array.ndim)


def rows_of(line, count):
    return [line[:, j * LANES : (j + 1) * LANES] for j in range(count)]


def columns_of(lines):
    used = jnp.concatenate([line.astype(F32) for line in lines], axis=0)
    pad = jnp.zeros((LANES - used.shape[0], LANES), F32)
    turned = jnp.concatenate([used, pad], axis=0).T
    return [turned[:, j : j + 1] for j in range(len(lines))]


def one_hot_rows(columns, width, base=0.0):
    lane = lax.broadcasted_iota(jnp.int32, (LANES, width), 1).astype(F32)
    hot = [jnp.where(lane == column, 1.0, base).astype(BF16) for column in columns]
    return jnp.concatenate(hot, axis=0)


def one_hot_cols(lines, height):
    row = lax.broadcasted_iota(jnp.int32, (height, LANES), 0)
    hot = [jnp.where(row == line, 1.0, 0.0).astype(BF16) for line in lines]
    return jnp.concatenate(hot, axis=1)


def table_rows(sender, mesh_rows, band, shards):
    window = lax.div(sender, mesh_rows)
    target = band + window - 1
    window = jnp.where((target >= 0) & (target < shards), window, 1)
    return window * mesh_rows + lax.rem(sender, mesh_rows)


def groups(x):
    return jnp.sum(x.reshape(x.shape[0] // 8, 8, x.shape[1]), axis=0)


def split(x):
    hi = x.astype(BF16)
    return hi, (x - hi.astype(F32)).astype(BF16)


def store_pieces(out_ref, base, total):
    parts = out_ref.shape[0]
    own = total.shape[0] // parts
    for j, piece in enumerate(tiles_of(total)):
        at = pl.ds(base + j * own, own)
        out_ref[:, at, :] = piece.astype(BF16).reshape(parts, own, LANES)


def tiles_of(rows):
    return [rows[:, j : j + LANES] for j in range(0, rows.shape[1], LANES)]


def edge_kernel(
    shards, mesh_rows, halved,
    place_ref, send_ref, recv_ref, live_ref, grid_ref, cot_ref, lat_ref, pair_ref, other_ref,
    wsend_ref, wrecv_ref, wout_ref, bias_ref, gain_ref,
    dsend_ref, dkeep_ref, gsend_ref, gkeep_ref, own_ref, up_ref, down_ref,
    rows_tab, cot_tab, wsum, gacc, tacc, qacc, total,
):
    step = pl.program_id(0)
    band, high, low = place_ref[0], place_ref[1], place_ref[2]
    even = lax.rem(band, 2) == 0
    height, width = grid_ref.shape
    first_bias = 3 * mesh_rows

    @pl.when(step == 0)
    def _():
        proj = jnp.dot(grid_ref[...], wrecv_ref[...], preferred_element_type=F32)
        rows_tab[:height, :] = (0.5 * proj).astype(BF16)
        pair = pair_ref[...].astype(F32)
        other = other_ref[...].astype(F32)
        rows = [jnp.where(even, other, pair), lat_ref[...].astype(F32), jnp.where(even, pair, other)]
        rows.append(jnp.zeros((WINDOW_ROWS - first_bias, width), F32))
        rows = jnp.concatenate(rows, axis=0).astype(BF16)
        sent = 0.5 * jnp.dot(rows, wsend_ref[...], preferred_element_type=F32)
        hi, lo = split(0.5 * bias_ref[...])
        row = lax.broadcasted_iota(jnp.int32, (WINDOW_ROWS, 1), 0)
        sent = jnp.where(row == first_bias, hi.astype(F32), sent)
        sent = jnp.where(row == first_bias + 1, lo.astype(F32), sent)
        rows_tab[height:, :] = jnp.concatenate(
            [sent, jnp.zeros((LANES - WINDOW_ROWS, width), F32)], axis=0
        ).astype(BF16)
        cot_tab[...] = (cot_ref[...].astype(F32) * gain_ref[...]).astype(BF16)
        for ref in (wsum, gacc, tacc, qacc):
            ref[...] = jnp.zeros_like(ref)

    pieces = BLOCK // LANES
    each = SUB // LANES
    near = table_rows(send_ref[...], mesh_rows, band, shards)
    near_lines = rows_of(near, pieces)
    recv_lines = rows_of(recv_ref[...], pieces)
    cols = columns_of(recv_lines + near_lines + rows_of(live_ref[...], pieces))
    lane = lax.broadcasted_iota(jnp.int32, (1, LANES), 1)
    always = jnp.where((lane == first_bias) | (lane == first_bias + 1), 1.0, 0.0)
    scale = 1.0 / width
    for part in range(BLOCK // SUB):
        span = range(part * each, (part + 1) * each)
        hot = one_hot_rows([cols[i] for i in span], height)
        hot_near = one_hot_rows([cols[pieces + i] for i in span], LANES, always)
        live = jnp.concatenate([cols[2 * pieces + i] for i in span], axis=0)
        z = jnp.dot(
            jnp.concatenate([hot, hot_near], axis=1), rows_tab[...], preferred_element_type=F32
        )
        scaled = jnp.dot(hot, cot_tab[...], preferred_element_type=F32)
        t = jnp.tanh(z)
        u = t + 1.0
        h = z * u
        hidden = h.astype(BF16)
        slope = u + h * (1.0 - t)
        outer = jnp.dot(hidden, wout_ref[...], preferred_element_type=F32)
        center = outer - jnp.sum(outer, axis=-1, keepdims=True) * scale
        var = jnp.sum(center * center, axis=-1, keepdims=True) * scale
        inv = lax.rsqrt(var + 1e-05) * live
        normed = center * inv
        product = scaled * normed
        mean_s = jnp.sum(scaled, axis=-1, keepdims=True) * scale
        mean_sn = jnp.sum(product, axis=-1, keepdims=True) * scale
        d_outer = ((scaled - mean_s - normed * mean_sn) * inv).astype(BF16)
        qacc[...] += groups(product)
        wsum[...] += mix(hidden, d_outer, 0, 0)
        d_pre = (mix(d_outer, wout_ref[...], 1, 1) * slope).astype(BF16)
        hot = one_hot_cols([recv_lines[i] for i in span], height)
        gacc[...] += jnp.dot(hot, d_pre, preferred_element_type=F32)
        hot = one_hot_cols([near_lines[i] for i in span], WINDOW_ROWS)
        tacc[...] += jnp.dot(hot, d_pre, preferred_element_type=F32)

    @pl.when(step == pl.num_programs(0) - 1)
    def _():
        below = 0.5 * tacc[:mesh_rows, :]
        above = 0.5 * tacc[2 * mesh_rows : 3 * mesh_rows, :]
        own_ref[...] = 0.5 * tacc[mesh_rows : 2 * mesh_rows, :]
        up_ref[...] = jnp.where(even, above, below)
        edge = (band == 0) | (band == shards - 1)
        down_ref[...] = jnp.where(edge, 0.0, jnp.where(even, below, above))
        bias = 0.5 * jnp.sum(tacc[...], axis=0, keepdims=True)
        gain = jnp.sum(qacc[...], axis=0, keepdims=True) / gain_ref[...]
        gacc[...] = 0.5 * gacc[...]
        total[...] = mix(grid_ref[...], gacc[...].astype(BF16), 0, 0)
        half = (dkeep_ref.shape[0] - 8) // 2
        mine = pl.multiple_of(low * half, half) if halved else 0
        for k, whole in enumerate((wsum, total)):
            dkeep_ref[k * half : (k + 1) * half, :] = whole[pl.ds(mine, half), :]
            if halved:
                theirs = pl.multiple_of((1 - low) * half, half)
                dsend_ref[k * half : (k + 1) * half, :] = whole[pl.ds(theirs, half), :].astype(BF16)
        rest = jnp.zeros((4, width), F32)
        dkeep_ref[2 * half :, :] = jnp.concatenate([bias, gain, rest[:2], rest], axis=0)
        (bias_hi, bias_lo), (gain_hi, gain_lo) = split(bias), split(gain)
        sent = [v.astype(F32) for v in (bias_hi, gain_hi, bias_lo, gain_lo)]
        dsend_ref[dsend_ref.shape[0] - 8 :, :] = jnp.concatenate(sent + [rest], axis=0).astype(BF16)
        share = gkeep_ref.shape[1]
        for k in range(gkeep_ref.shape[0]):
            base = (high ^ k) * 2
            mine = pl.multiple_of((base + low) * share, share)
            theirs = pl.multiple_of((base + 1 - low) * share, share)
            gkeep_ref[k] = gacc[pl.ds(mine, share), :]
            gsend_ref[k] = gacc[pl.ds(theirs, share), :].astype(BF16)


def edges(shards, levels, place, send, recv, live, grid, cot, lat, pair, other, *weights):
    slots = send.shape[1]
    height, width = grid.shape
    mesh_rows = lat.shape[0]
    halved = sliced(width, shards * levels)
    line = pl.BlockSpec((1, BLOCK), lambda i: (0, i))
    half = width // 2 if halved else width
    share = (levels // 2, height // levels, width)
    near = jax.ShapeDtypeStruct((mesh_rows, width), F32)
    outs = [
        jax.ShapeDtypeStruct(((width if halved else 0) + 8, width), BF16),
        jax.ShapeDtypeStruct((2 * half + 8, width), F32),
        jax.ShapeDtypeStruct(share, BF16),
        jax.ShapeDtypeStruct(share, F32),
        near, near, near,
    ]
    whole = (grid, cot, lat, pair, other) + weights
    return pl.pallas_call(
        functools.partial(edge_kernel, shards, mesh_rows, halved),
        grid=(slots // BLOCK,),
        in_specs=[pl.BlockSpec(memory_space=pltpu.SMEM), line, line, line]
        + [full(array) for array in whole],
        out_specs=[full(out) for out in outs],
        out_shape=outs,
        scratch_shapes=[
            pltpu.VMEM((height + LANES, width), BF16),
            pltpu.VMEM((height, width), BF16),
            pltpu.VMEM((width, width), F32),
            pltpu.VMEM((height, width), F32),
            pltpu.VMEM((WINDOW_ROWS, width), F32),
            pltpu.VMEM((8, width), F32),
            pltpu.VMEM((width, width), F32),
        ],
        compiler_params=pltpu.CompilerParams(vmem_limit_bytes=EDGE_VMEM),
        cost_estimate=cost(14 * slots * width * width, 16 * width * width),
        name="edges",
    )(place, send, recv, live, *whole)


def combine_kernel(dkeep_ref, drecv_ref, gkeep_ref, grecv_ref, part_ref, gsend_ref, gown_ref):
    half = (dkeep_ref.shape[0] - 8) // 2
    width = dkeep_ref.shape[1]
    slab = half * width // LANES // part_ref.shape[0]
    for k in range(2):
        at = pl.ds(k * half, half)
        store_pieces(part_ref, k * slab, dkeep_ref[at, :] + drecv_ref[at, :].astype(F32))
    near = drecv_ref[2 * half :, :].astype(F32)
    vectors = dkeep_ref[2 * half : 2 * half + 2, :] + near[0:2] + near[2:4]
    hi, lo = split(vectors)
    extra = [v[k : k + 1] for v in (hi.astype(F32), lo.astype(F32)) for k in range(2)]
    extra = jnp.concatenate([tile for v in extra for tile in tiles_of(v)], axis=0).astype(BF16)
    part_ref[:, 2 * slab :, :] = jnp.broadcast_to(extra[None], (part_ref.shape[0],) + extra.shape)
    gown_ref[...] = gkeep_ref[0] + grecv_ref[0].astype(F32)
    gsend_ref[...] = (gkeep_ref[1] + grecv_ref[1].astype(F32)).astype(BF16)


def combine(parts, dkeep, drecv, gkeep, grecv):
    half, width = (dkeep.shape[0] - 8) // 2, dkeep.shape[1]
    rows = (2 * half // parts + 4) * (width // LANES)
    return pl.pallas_call(
        combine_kernel,
        out_shape=[
            jax.ShapeDtypeStruct((parts, rows, LANES), BF16),
            jax.ShapeDtypeStruct(gkeep.shape[1:], BF16),
            jax.ShapeDtypeStruct(gkeep.shape[1:], F32),
        ],
        compiler_params=pltpu.CompilerParams(vmem_limit_bytes=EDGE_VMEM),
        cost_estimate=cost(2 * dkeep.size, 8 * dkeep.size),
        name="combine_halves",
    )(dkeep, drecv, gkeep, grecv)


def sum_kernel(
    part_ref, lat_ref, own_ref, pair_ref, other_ref, wsend_ref,
    pay_ref, dmesh_ref, dbias_ref, dgain_ref,
):
    tiles = dbias_ref.shape[1] // LANES
    slabs = part_ref.shape[1] - 4 * tiles
    total = jnp.sum(part_ref[...].astype(F32), axis=0)
    for k, ref in enumerate((dbias_ref, dgain_ref)):
        base = slabs + k * tiles
        both = total[base : base + tiles] + total[base + 2 * tiles : base + 3 * tiles]
        for j in range(tiles):
            ref[:, j * LANES : (j + 1) * LANES] = both[j : j + 1]
    mesh = own_ref[...] + pair_ref[...] + other_ref[...]
    pieces = [total[:slabs]] + tiles_of(mesh) + tiles_of(lat_ref[...].astype(F32))
    payload = jnp.concatenate(pieces, axis=0).astype(BF16)
    pay_ref[...] = jnp.broadcast_to(payload[None], pay_ref.shape)
    dmesh_ref[...] = mix(mesh.astype(BF16), wsend_ref[...], 1, 1)


def sum_slabs(shards, part, lat, own, pair, other, wsend):
    mesh_rows, width = lat.shape
    tiles = width // LANES
    rows = part.shape[1] - 4 * tiles + 2 * mesh_rows * tiles
    vector = jax.ShapeDtypeStruct((1, width), F32)
    return pl.pallas_call(
        sum_kernel,
        out_shape=[
            jax.ShapeDtypeStruct((shards, rows, LANES), BF16),
            jax.ShapeDtypeStruct((mesh_rows, width), F32),
            vector, vector,
        ],
        compiler_params=pltpu.CompilerParams(vmem_limit_bytes=VMEM),
        cost_estimate=cost(2 * part.size, 4 * part.size),
        name="sum_slabs",
    )(part, lat, own, pair, other, wsend)


def spread_kernel(levels, mesh_rows, place_ref, *refs):
    parts_refs = refs[:levels]
    dsend_ref, drecv_ref, dout_ref, mesh, lat = refs[levels:]
    width = dsend_ref.shape[0]
    tiles = width // LANES
    shards = parts_refs[0].shape[0]
    own = width // (shards * levels)
    slab = own * tiles
    level = place_ref[1] * 2 + place_ref[2]
    for k, ref in enumerate(parts_refs):
        for s in range(shards):
            at = level ^ k
            high, low = lax.shift_right_logical(at, 1), at & 1
            place = (low * shards + s) * (levels // 2) + high
            tail = ref[s, 2 * slab :, :].astype(F32)
            rows = pl.ds(pl.multiple_of(place * own, own), own)
            near = pl.ds(pl.multiple_of(place * mesh_rows, mesh_rows), mesh_rows)
            for j in range(tiles):
                cols = pl.ds(j * LANES, LANES)
                dout_ref[rows, cols] = ref[s, j * own : (j + 1) * own, :]
                drecv_ref[rows, cols] = ref[s, slab + j * own : slab + (j + 1) * own, :]
                mesh[near, cols] = tail[j * mesh_rows : (j + 1) * mesh_rows]
                lat[near, cols] = tail[(tiles + j) * mesh_rows : (tiles + j + 1) * mesh_rows]
    dsend_ref[...] = mix(lat[...].astype(BF16), mesh[...].astype(BF16), 0, 0).astype(BF16)


def spread(width, mesh_rows, place, received):
    levels = len(received)
    rows = received[0].shape[0] * levels * mesh_rows
    out = jax.ShapeDtypeStruct((width, width), BF16)
    return pl.pallas_call(
        functools.partial(spread_kernel, levels, mesh_rows),
        in_specs=[pl.BlockSpec(memory_space=pltpu.SMEM)]
        + [pl.BlockSpec(memory_space=pltpu.VMEM)] * levels,
        out_shape=[out, out, out],
        scratch_shapes=[pltpu.VMEM((rows, width), F32)] * 2,
        compiler_params=pltpu.CompilerParams(vmem_limit_bytes=VMEM),
        cost_estimate=cost(2 * rows * width * width, 8 * width * width),
        name="spread_weights",
    )(place, *received)


def swap(x, axis, bit):
    return lax.ppermute(x, axis, [(i, i ^ bit) for i in range(lax.axis_size(axis))])


def swap_between(x, axis):
    count = lax.axis_size(axis)
    pairs = [(i, i + 1) for i in range(1, count - 1, 2)]
    ends = [(0, 0), (count - 1, count - 1)]
    return lax.ppermute(x, axis, pairs + [(j, i) for i, j in pairs] + ends)


def body(
    grid_latent, mesh_latent, grid_output_cotangent, w_send, w_recv, output_weight,
    hidden_layer_bias, output_norm_gain, edge_sender, edge_receiver, edge_live,
):
    shards, levels = lax.axis_size("space"), lax.axis_size("high") * 2
    parts = shards * levels
    width = grid_latent.shape[1]
    mesh_rows = mesh_latent.shape[1]
    lat = mesh_latent[0]
    whole_slabs = sliced(width, parts)
    place = jnp.stack([lax.axis_index(axis) for axis in ALL]).astype(jnp.int32)

    lat_pair = swap(lat, "space", 1)
    lat_other = swap_between(lat, "space")
    dsend, dkeep, gsend, gkeep, own, pair, other = edges(
        shards, levels, place, edge_sender, edge_receiver, edge_live,
        grid_latent, grid_output_cotangent, lat, lat_pair, lat_other,
        w_send, w_recv, output_weight, hidden_layer_bias[None], output_norm_gain[None],
    )
    pair = swap(pair, "space", 1)
    other = swap_between(other, "space")

    if not whole_slabs:
        rows = jnp.stack([gkeep.astype(BF16), gsend])
        for k in range(1, levels):
            side = rows[k % 2, k // 2]
            for bit in (1, 2):
                if k & bit:
                    side = swap(side, ("low", "high")[bit // 2], 1)
            gkeep = gkeep.at[0].add(side.astype(F32))
        d_grid = mix(gkeep[0].astype(BF16), w_recv, 1, 1)
        mesh = (own + pair + other).astype(BF16)
        d_mesh = mix(mesh, w_send, 1, 1)
        d_send, rest = lax.psum((mix(lat, mesh, 0, 0), dkeep), ALL)
        d_w_out, d_w_recv = rest[:width].astype(BF16), rest[width : 2 * width].astype(BF16)
        d_bias, d_gain = rest[2 * width], rest[2 * width + 1]
        return (d_grid, d_mesh[None], d_send.astype(BF16), d_w_recv, d_w_out, d_bias, d_gain)

    dnear = swap(dsend, "low", 1)
    gnear = swap(gsend, "low", 1)
    part, gsend, gown = combine(parts // 2, dkeep, dnear, gkeep, gnear)
    gfar = swap(gsend, "high", 1)
    part = lax.all_to_all(part, MOST, 0, 0, tiled=False)
    d_grid = mix((gown + gfar.astype(F32)).astype(BF16), w_recv, 1, 1)
    payload, d_mesh, d_bias, d_gain = sum_slabs(shards, part, lat, own, pair, other, w_send)
    received = {0: lax.all_to_all(payload, "space", 0, 0, tiled=False)}
    received[2] = swap(received[0], "high", 1)
    received[1] = swap(received[0], "low", 1)
    received[3] = swap(received[2], "low", 1)
    d_w_send, d_w_recv, d_w_out = spread(
        width, mesh_rows, place, [received[k] for k in range(levels)]
    )
    return (d_grid, d_mesh[None], d_w_send, d_w_recv, d_w_out, d_bias[0], d_gain[0])


def solution(mesh):
    shards, levels = mesh.devices.shape
    split_mesh = Mesh(mesh.devices.reshape(shards, levels // 2, 2), ALL)
    level = MOST[1:] + ALL[2:]

    return jax.shard_map(
        body,
        mesh=split_mesh,
        in_specs=(
            P("space", None), P(level, "space", None), P("space", None), P(), P(), P(), P(), P(),
            P(level, "space"), P(level, "space"), P(level, "space"),
        ),
        out_specs=(P(ALL, None), P(level, "space", None), P(), P(), P(), P(), P()),
        check_vma=False,
    )
```

time: 101 us -> 88.9 us (0.88)
  Pallas kernels: 35.4 us -> 22.5 us
  waiting for transfers between devices: 24.5 us -> 29.2 us
  local copies, waits for them, and re-layouts: 3.61 us -> 1.52 us
  starting transfers between devices: 19.8 us -> 17.8 us
    pallas_call x6 -> x3, Pallas kernels: 32.5 us -> 20.5 us  [the longest x1 16.9 us: edges(): pl.pallas_call(functools.partial(edge_kernel, shards, mesh_rows, halved),...]
    ppermute x8, waiting for transfers between devices: 14.1 us -> 18.6 us  [swap(): lax.ppermute(x, axis, [(i, i ^ bit) for i in range(lax.axis_size(axis))])]
    all_to_all x2 -> x1, starting transfers between devices: 8.94 us -> 6.51 us  [body(): part = lax.all_to_all(part, MOST, 0, 0, tiled=False)]
    unnamed x34 -> x26, local copies, waits for them, and re-layouts: 3.61 us -> 1.52 us
    all_to_all x2 -> x1, waiting for transfers between devices: 10.4 us -> 10.5 us  [body(): part = lax.all_to_all(part, MOST, 0, 0, tiled=False)]
  transfers between devices with their start and end apart: 12 -> 11, of which waited for: 5 -> 6; matrix products, arithmetic and copies ran while one was open for 2% -> 2% of each run, Pallas kernels for 17% -> 0%
where the time goes in v3:
time: 88.9 us; the launch traced here: 88.5 us
  waiting for transfers between devices  29.2 us (33%)
  Pallas kernels  22.5 us (25%)
  starting transfers between devices  17.8 us (20%)
  blocking collectives  15.2 us (17%)
  local copies, waits for them, and re-layouts  1.52 us (2%)
  matrix products  1.01 us (1%)
    ppermute x8, waiting for transfers between devices, swap(): lax.ppermute(x, axis, [(i, i ^ bit) for i in range(lax.axis_size(axis))])  18.6 us
    pallas_call x1, Pallas kernels, edges(): pl.pallas_call(functools.partial(edge_kernel, shards, mesh_rows, halved),...  16.9 us
    all_to_all x1, blocking collectives, body(): received = {0: lax.all_to_all(payload, 'space', 0, 0, tiled=False)}  15.2 us
    all_to_all x1, waiting for transfers between devices, body(): part = lax.all_to_all(part, MOST, 0, 0, tiled=False)  10.5 us
    ppermute x8, starting transfers between devices, swap(): lax.ppermute(x, axis, [(i, i ^ bit) for i in range(lax.axis_size(axis))])  9.23 us
    all_to_all x1, starting transfers between devices, body(): part = lax.all_to_all(part, MOST, 0, 0, tiled=False)  6.51 us
    pallas_call x1, Pallas kernels, combine(): pl.pallas_call(combine_kernel, out_shape=[jax.ShapeDtypeStruct((parts, ro...  2.63 us
    pallas_call x1, Pallas kernels, spread(): pl.pallas_call(functools.partial(spread_kernel, levels, mesh_rows), in_sp...  2.04 us
  transfers between devices with their start and end apart: 11, of which 6 were waited for; matrix products, arithmetic and copies ran while one was open for 2% of the time, Pallas kernels for 0%

profile of v3, /device:TPU:0, one launch (start us, length us, event | category | flops | bytes accessed | tf_op | source)
XLA Modules:
  0.0 88.5 jit_solution(3352253814416820994)
XLA Ops:
  0.6 1.4 %collective-permute-start.1 = (bf16[8,512]{1,0:T(8,128)(2,1)}, bf16[8,512]{1,0:T(8,128)(2,1)S(1)}, u32[]{:S(2)}, u32[]{:S(2)}) collective-permute-start(bf16[8,512]{1,0:T(8,128)(2,1)} %bitcast.10), channel_id=1, source_target_pairs={{4,8},{12,16},{20,24},{8,4},{16,12},{24,20},{0,0},{28,28},{5,9},{1... | collective-permute-start | bytes 24584 | tf_op jit(solution)/shard_map/ppermute | solution.py:356
  2.0 5.1 %collective-permute-start = (bf16[8,512]{1,0:T(8,128)(2,1)}, bf16[8,512]{1,0:T(8,128)(2,1)S(1)}, u32[]{:S(2)}, u32[]{:S(2)}) collective-permute-start(bf16[8,512]{1,0:T(8,128)(2,1)} %bitcast.11), channel_id=1, source_target_pairs={{0,4},{4,0},{8,12},{12,8},{16,20},{20,16},{24,28},{28,24},{1,5},{5... | collective-permute-start | bytes 24584 | tf_op jit(solution)/shard_map/ppermute | solution.py:349
  7.1 0.7 pad_add_fusion.place_ref
  7.8 0.0 collective-permute-done.1.other_ref
  7.8 0.0 copy-start.11
  7.8 1.2 %collective-permute-done.pair_ref = bf16[8,512]{1,0:T(8,128)(2,1)S(1)} collective-permute-done((bf16[8,512]{1,0:T(8,128)(2,1)}, bf16[8,512]{1,0:T(8,128)(2,1)S(1)}, u32[]{:S(2)}, u32[]{:S(2)}) %collective-permute-start) | collective-permute-done | bytes 8224 | tf_op jit(solution)/shard_map/ppermute | solution.py:349
  9.0 0.0 copy-done.11
  9.0 0.6 copy-done.12
  9.6 16.9 %edges.1 = (bf16[520,512]{1,0:T(8,128)(2,1)}, f32[520,512]{1,0:T(8,128)}, bf16[2,128,512]{2,1,0:T(8,128)(2,1)}, f32[2,128,512]{2,1,0:T(8,128)}, f32[8,512]{1,0:T...) custom-call(s32[3]{0:T(128)} %pad_add_fusion.place_ref, s32[1,2048]{1,0:T(1,128)} %send_ref.1, s32[1,2048]{1,0:T(1,128)} %recv_ref.1, ...), custom_call_target="tpu_custom_call" | custom-call | flops 7516192768 | bytes 4194304 | tf_op jit(solution)/shard_map/edges/pallas_call | solution.py:214
  26.5 0.1 collective-permute-start.2
  26.6 0.5 collective-permute-start.3
  27.1 2.0 %collective-permute-done.3.grecv_ref = bf16[2,128,512]{2,1,0:T(8,128)(2,1)S(1)} collective-permute-done((bf16[2,128,512]{2,1,0:T(8,128)(2,1)}, bf16[2,128,512]{2,1,0:T(8,128)(2,1)S(1)}, u32[]{:S(2)}, u32[]{:S(2)}) %collective-permute-start.3) | collective-permute-done | bytes 262176 | tf_op jit(solution)/shard_map/ppermute | solution.py:349
  29.1 0.0 collective-permute-done.2.drecv_ref
  29.1 0.7 copy-done.6
  29.8 0.2 copy-done.4
  30.0 2.6 %combine_halves.1 = (bf16[16,144,128]{2,1,0:T(8,128)(2,1)}, bf16[128,512]{1,0:T(8,128)(2,1)}, f32[128,512]{1,0:T(8,128)}) custom-call(f32[520,512]{1,0:T(8,128)} %get-tuple-element.24.dkeep_ref, bf16[520,512]{1,0:T(8,128)(2,1)} %copy-done.4, f32[2,128,512]{2,1,0:T(8,128)} %get-tuple-element.26.gkeep_ref, bf16[2,128,512]{2,1,0:T(8,128)(2,1)} %copy-done.6), custom_call_target="tpu_custom_call" | custom-call | flops 532480 | bytes 2129920 | tf_op jit(solution)/shard_map/combine_halves/pallas_call | solution.py:256
  32.6 0.0 copy-start.1
  32.6 0.0 copy-start.2
  32.6 6.5 %all-to-all-start = ((bf16[16,144,128]{2,1,0:T(8,128)(2,1)}), bf16[16,144,128]{2,1,0:T(8,128)(2,1)S(1)}, u32[]{:S(2)}, u32[]{:S(2)}) async-start(bf16[16,144,128]{2,1,0:T(8,128)(2,1)} %get-tuple-element.30), calls=%async_computation | async-start | bytes 1179648 | tf_op jit(solution)/shard_map/all_to_all | solution.py:401
  39.1 0.0 copy-start.8
  39.2 0.0 copy-start.5
  39.2 0.0 copy-start.7
  39.2 0.0 copy-done.10
  39.2 2.0 %collective-permute-start.5 = (f32[8,512]{1,0:T(8,128)S(1)}, f32[8,512]{1,0:T(8,128)S(1)}, u32[]{:S(2)}, u32[]{:S(2)}) collective-permute-start(f32[8,512]{1,0:T(8,128)S(1)} %copy-done.10), channel_id=1, source_target_pairs={{0,4},{4,0},{8,12},{12,8},{16,20},{20,16},{24,28},{28,24},{1,5},{5... | collective-permute-start | bytes 49160 | tf_op jit(solution)/shard_map/ppermute | solution.py:349
  41.2 0.0 copy-done.9
  41.2 0.7 collective-permute-start.6
  41.8 3.3 %collective-permute-done.5.pair_ref = f32[8,512]{1,0:T(8,128)S(1)} collective-permute-done((f32[8,512]{1,0:T(8,128)S(1)}, f32[8,512]{1,0:T(8,128)S(1)}, u32[]{:S(2)}, u32[]{:S(2)}) %collective-permute-start.5) | collective-permute-done | bytes 16416 | tf_op jit(solution)/shard_map/ppermute | solution.py:349
  45.1 0.0 collective-permute-done.6.other_ref
  45.1 10.5 %all-to-all-done.part_ref = bf16[16,144,128]{2,1,0:T(8,128)(2,1)S(1)} async-done(((bf16[16,144,128]{2,1,0:T(8,128)(2,1)}), bf16[16,144,128]{2,1,0:T(8,128)(2,1)S(1)}, u32[]{:S(2)}, u32[]{:S(2)}) %all-to-all-start) | async-done | bytes 589856 | tf_op jit(solution)/shard_map/all_to_all | solution.py:401
  55.7 0.0 copy-done
  55.7 0.0 copy-done.1
  55.7 0.0 copy-done.2
  55.7 0.9 %sum_slabs.1 = (bf16[8,192,128]{2,1,0:T(8,128)(2,1)S(1)}, f32[8,512]{1,0:T(8,128)}, f32[1,512]{1,0:T(1,128)}, f32[1,512]{1,0:T(1,128)}) custom-call(bf16[16,144,128]{2,1,0:T(8,128)(2,1)S(1)} %all-to-all-done.part_ref, bf16[8,512]{1,0:T(8,128)(2,1)S(1)} %bitcast.13, f32[8,512]{1,0:T(8,128)S(1)} %copy-done.1, f32[8,512]{1,0:T(8,128)S(1)} %collective-permute-done.5.pair_ref, ...), custom_call_target="tpu_custom_call" | custom-call | flops 589824 | bytes 1179648 | tf_op jit(solution)/shard_map/sum_slabs/pallas_call | solution.py:293
  56.6 15.2 %all_to_all.10.refs_0_ = bf16[8,192,128]{2,1,0:T(8,128)(2,1)S(1)} all-to-all(bf16[8,192,128]{2,1,0:T(8,128)(2,1)S(1)} %get-tuple-element.35), channel_id=1, replica_groups=mesh['space'=8,'high'=2,'low'=2] {'space'}, dimensions={0} | all-to-all | bytes 786432 | tf_op jit(solution)/shard_map/all_to_all | solution.py:404
  71.8 0.8 collective-permute-start.8
  72.5 0.0 collective-permute-start.7
  72.5 7.0 %collective-permute-done.8.refs_2_ = bf16[8,192,128]{2,1,0:T(8,128)(2,1)S(1)} collective-permute-done((bf16[8,192,128]{2,1,0:T(8,128)(2,1)S(1)}, bf16[8,192,128]{2,1,0:T(8,128)(2,1)S(1)}, u32[]{:S(2)}, u32[]{:S(2)}) %collective-permute-start.8) | collective-permute-done | bytes 393248 | tf_op jit(solution)/shard_map/ppermute | solution.py:349
  79.5 0.0 collective-permute-start.9
  79.5 0.0 copy-done.8
  79.6 0.8 collective-permute-start.4
  80.3 5.1 %collective-permute-done.4 = bf16[128,512]{1,0:T(8,128)(2,1)S(1)} collective-permute-done((bf16[128,512]{1,0:T(8,128)(2,1)S(1)}, bf16[128,512]{1,0:T(8,128)(2,1)S(1)}, u32[]{:S(2)}, u32[]{:S(2)}) %collective-permute-start.4) | collective-permute-done | bytes 131104 | tf_op jit(solution)/shard_map/ppermute | solution.py:349
  85.5 0.0 copy-done.5
  85.5 0.0 copy-done.7
  85.5 1.0 %fusion = f32[128,512]{1,0:T(8,128)} fusion(bf16[512,512]{1,0:T(8,128)(2,1)S(1)} %copy-done.5, f32[128,512]{1,0:T(8,128)S(1)} %copy-done.7, bf16[128,512]{1,0:T(8,128)(2,1)S(1)} %collective-permute-done.4), kind=kOutput, calls=%fused_computation.1 | convolution fusion | flops 67305472 | bytes 1179648 | tf_op jit(solution)/shard_map/dot_general | solution.py:32
  86.5 0.0 collective-permute-done.7.refs_1_
  86.5 0.0 collective-permute-done.9.refs_3_
  86.5 0.0 copy-done.3
  86.5 2.0 %spread_weights.1 = (bf16[512,512]{1,0:T(8,128)(2,1)}, bf16[512,512]{1,0:T(8,128)(2,1)}, bf16[512,512]{1,0:T(8,128)(2,1)}) custom-call(s32[3]{0:T(128)S(1)} %copy-done.3, bf16[8,192,128]{2,1,0:T(8,128)(2,1)S(1)} %all_to_all.10.refs_0_, bf16[8,192,128]{2,1,0:T(8,128)(2,1)S(1)} %collective-permute-done.7.refs_1_, ...), custom_call_target="tpu_custom_call" | custom-call | flops 134217728 | bytes 2097152 | tf_op jit(solution)/shard_map/spread_weights/pallas_call | solution.py:336
  (7 shorter events, 0.0 us)
Async XLA Ops:
  0.6 7.2 %collective-permute-start.1 = (bf16[8,512]{1,0:T(8,128)(2,1)}, bf16[8,512]{1,0:T(8,128)(2,1)S(1)}, u32[]{:S(2)}, u32[]{:S(2)}) collective-permute-start(bf16[8,512]{1,0:T(8,128)(2,1)} %bitcast.10), channel_id=1, source_target_pairs={{4,8},{12,16},{20,24},{8,4},{16,12},{24,20},{0,0},{28,28},{5,9},{1... | collective-permute-start | bytes 24584 | tf_op jit(solution)/shard_map/ppermute | solution.py:356
  2.0 7.0 %collective-permute-start = (bf16[8,512]{1,0:T(8,128)(2,1)}, bf16[8,512]{1,0:T(8,128)(2,1)S(1)}, u32[]{:S(2)}, u32[]{:S(2)}) collective-permute-start(bf16[8,512]{1,0:T(8,128)(2,1)} %bitcast.11), channel_id=1, source_target_pairs={{0,4},{4,0},{8,12},{12,8},{16,20},{20,16},{24,28},{28,24},{1,5},{5... | collective-permute-start | bytes 24584 | tf_op jit(solution)/shard_map/ppermute | solution.py:349
  7.8 1.2 %copy-start.11 = (bf16[8,512]{1,0:T(8,128)(2,1)}, bf16[8,512]{1,0:T(8,128)(2,1)S(1)}, u32[]{:S(2)}) copy-start(bf16[8,512]{1,0:T(8,128)(2,1)S(1)} %collective-permute-done.1.other_ref) | copy-start | bytes 24580
  9.0 0.6 copy-start.12
  26.5 2.6 %collective-permute-start.2 = (bf16[520,512]{1,0:T(8,128)(2,1)}, bf16[520,512]{1,0:T(8,128)(2,1)S(1)}, u32[]{:S(2)}, u32[]{:S(2)}) collective-permute-start(bf16[520,512]{1,0:T(8,128)(2,1)} %get-tuple-element.25), channel_id=1, source_target_pairs={{0,1},{1,0},{2,3},{3,2},{4,5},{5,4},{6,7},{7,6},{8,9},{9,8},{10,11... | collective-permute-start | bytes 1597448 | tf_op jit(solution)/shard_map/ppermute | solution.py:349
  26.6 2.5 %collective-permute-start.3 = (bf16[2,128,512]{2,1,0:T(8,128)(2,1)}, bf16[2,128,512]{2,1,0:T(8,128)(2,1)S(1)}, u32[]{:S(2)}, u32[]{:S(2)}) collective-permute-start(bf16[2,128,512]{2,1,0:T(8,128)(2,1)} %get-tuple-element.27), channel_id=1, source_target_pairs={{0,1},{1,0},{2,3},{3,2},{4,5},{5,4},{6,7},{7,6},{8,9},{9,8},{10,11... | collective-permute-start | bytes 786440 | tf_op jit(solution)/shard_map/ppermute | solution.py:349
  29.1 0.7 copy-start.6
  29.1 0.9 copy-start.4
  32.6 6.6 %copy-start.10 = (f32[8,512]{1,0:T(8,128)S(1)}, f32[8,512]{1,0:T(8,128)}, u32[]{:S(2)}) copy-start(f32[8,512]{1,0:T(8,128)} %get-tuple-element.32) | copy-start | bytes 49156
  32.6 8.6 %copy-start.9 = (f32[8,512]{1,0:T(8,128)S(1)}, f32[8,512]{1,0:T(8,128)}, u32[]{:S(2)}) copy-start(f32[8,512]{1,0:T(8,128)} %get-tuple-element.33) | copy-start | bytes 49156
  32.6 23.1 %copy-start = (bf16[512,512]{1,0:T(8,128)(2,1)S(1)}, bf16[512,512]{1,0:T(8,128)(2,1)}, u32[]{:S(2)}) copy-start(bf16[512,512]{1,0:T(8,128)(2,1)} %wsend_ref.3) | copy-start | bytes 1572868
  32.6 23.1 %copy-start.1 = (f32[8,512]{1,0:T(8,128)S(1)}, f32[8,512]{1,0:T(8,128)}, u32[]{:S(2)}) copy-start(f32[8,512]{1,0:T(8,128)} %get-tuple-element.31.own_ref) | copy-start | bytes 49156
  32.6 23.1 %copy-start.2 = (bf16[1,8,512]{2,1,0:T(8,128)(2,1)S(1)}, bf16[1,8,512]{2,1,0:T(8,128)(2,1)}, u32[]{:S(2)}) copy-start(bf16[1,8,512]{2,1,0:T(8,128)(2,1)} %param.12) | copy-start | bytes 24580
  32.6 23.0 %all-to-all-start = ((bf16[16,144,128]{2,1,0:T(8,128)(2,1)}), bf16[16,144,128]{2,1,0:T(8,128)(2,1)S(1)}, u32[]{:S(2)}, u32[]{:S(2)}) async-start(bf16[16,144,128]{2,1,0:T(8,128)(2,1)} %get-tuple-element.30), calls=%async_computation | async-start | bytes 1179648 | tf_op jit(solution)/shard_map/all_to_all | solution.py:401
  39.1 40.4 %copy-start.8 = (bf16[128,512]{1,0:T(8,128)(2,1)S(1)}, bf16[128,512]{1,0:T(8,128)(2,1)}, u32[]{:S(2)}) copy-start(bf16[128,512]{1,0:T(8,128)(2,1)} %get-tuple-element.29) | copy-start | bytes 393220
  39.2 46.3 %copy-start.5 = (bf16[512,512]{1,0:T(8,128)(2,1)S(1)}, bf16[512,512]{1,0:T(8,128)(2,1)}, u32[]{:S(2)}) copy-start(bf16[512,512]{1,0:T(8,128)(2,1)} %wrecv_ref.1) | copy-start | bytes 1572868
  39.2 46.3 %copy-start.7 = (f32[128,512]{1,0:T(8,128)S(1)}, f32[128,512]{1,0:T(8,128)}, u32[]{:S(2)}) copy-start(f32[128,512]{1,0:T(8,128)} %get-tuple-element.28) | copy-start | bytes 786436
  39.2 5.9 %collective-permute-start.5 = (f32[8,512]{1,0:T(8,128)S(1)}, f32[8,512]{1,0:T(8,128)S(1)}, u32[]{:S(2)}, u32[]{:S(2)}) collective-permute-start(f32[8,512]{1,0:T(8,128)S(1)} %copy-done.10), channel_id=1, source_target_pairs={{0,4},{4,0},{8,12},{12,8},{16,20},{20,16},{24,28},{28,24},{1,5},{5... | collective-permute-start | bytes 49160 | tf_op jit(solution)/shard_map/ppermute | solution.py:349
  41.2 4.0 %collective-permute-start.6 = (f32[8,512]{1,0:T(8,128)S(1)}, f32[8,512]{1,0:T(8,128)S(1)}, u32[]{:S(2)}, u32[]{:S(2)}) collective-permute-start(f32[8,512]{1,0:T(8,128)S(1)} %copy-done.9), channel_id=1, source_target_pairs={{4,8},{12,16},{20,24},{8,4},{16,12},{24,20},{0,0},{28,28},{5,9},{1... | collective-permute-start | bytes 49160 | tf_op jit(solution)/shard_map/ppermute | solution.py:356
  56.6 29.9 %copy-start.3 = (s32[3]{0:T(128)S(1)}, s32[3]{0:T(128)}, u32[]{:S(2)}) copy-start(s32[3]{0:T(128)} %pad_add_fusion.place_ref) | copy-start | bytes 40
  71.8 7.8 %collective-permute-start.8 = (bf16[8,192,128]{2,1,0:T(8,128)(2,1)S(1)}, bf16[8,192,128]{2,1,0:T(8,128)(2,1)S(1)}, u32[]{:S(2)}, u32[]{:S(2)}) collective-permute-start(bf16[8,192,128]{2,1,0:T(8,128)(2,1)S(1)} %all_to_all.10.refs_0_), channel_id=1, source_target_pairs={{0,2},{2,0},{1,3},{3,1},{4,6},{6,4},{5,7},{7,5},{8,10},{10,8},{9,1... | collective-permute-start | bytes 1179656 | tf_op jit(solution)/shard_map/ppermute | solution.py:349
  72.5 14.0 %collective-permute-start.7 = (bf16[8,192,128]{2,1,0:T(8,128)(2,1)S(1)}, bf16[8,192,128]{2,1,0:T(8,128)(2,1)S(1)}, u32[]{:S(2)}, u32[]{:S(2)}) collective-permute-start(bf16[8,192,128]{2,1,0:T(8,128)(2,1)S(1)} %all_to_all.10.refs_0_), channel_id=1, source_target_pairs={{0,1},{1,0},{2,3},{3,2},{4,5},{5,4},{6,7},{7,6},{8,9},{9,8},{10,11... | collective-permute-start | bytes 1179656 | tf_op jit(solution)/shard_map/ppermute | solution.py:349
  79.5 6.9 %collective-permute-start.9 = (bf16[8,192,128]{2,1,0:T(8,128)(2,1)S(1)}, bf16[8,192,128]{2,1,0:T(8,128)(2,1)S(1)}, u32[]{:S(2)}, u32[]{:S(2)}) collective-permute-start(bf16[8,192,128]{2,1,0:T(8,128)(2,1)S(1)} %collective-permute-done.8.refs_2_), channel_id=1, source_target_pairs={{0,1},{1,0},{2,3},{3,2},{4,5},{5,4},{6,7},{7,6},{8,9},{9,8},{10,11... | collective-permute-start | bytes 1179656 | tf_op jit(solution)/shard_map/ppermute | solution.py:349
  79.6 5.9 %collective-permute-start.4 = (bf16[128,512]{1,0:T(8,128)(2,1)S(1)}, bf16[128,512]{1,0:T(8,128)(2,1)S(1)}, u32[]{:S(2)}, u32[]{:S(2)}) collective-permute-start(bf16[128,512]{1,0:T(8,128)(2,1)S(1)} %copy-done.8), channel_id=1, source_target_pairs={{0,2},{2,0},{1,3},{3,1},{4,6},{6,4},{5,7},{7,5},{8,10},{10,8},{9,1... | collective-permute-start | bytes 393224 | tf_op jit(solution)/shard_map/ppermute | solution.py:349

commit v4 on v3

--- a/solution.py
+++ b/solution.py
@@ -13,11 +13,12 @@
 ALL = ("space", "high", "low")
 MOST = ("space", "high")
 LANES = 128
-BLOCK = 1024
-SUB = 512
+BLOCK = 2048
+SUB = 256
 WINDOW_ROWS = 32
 VMEM = 16 * 1024 * 1024
-EDGE_VMEM = 60 * 1024 * 1024
+EDGE_VMEM = 40 * 1024 * 1024
+COMBINE_VMEM = 16 * 1024 * 1024
 
 
 def sliced(width, parts):
@@ -87,23 +88,39 @@
     return [rows[:, j : j + LANES] for j in range(0, rows.shape[1], LANES)]
 
 
-def edge_kernel(
-    shards, mesh_rows, halved,
-    place_ref, send_ref, recv_ref, live_ref, grid_ref, cot_ref, lat_ref, pair_ref, other_ref,
-    wsend_ref, wrecv_ref, wout_ref, bias_ref, gain_ref,
-    dsend_ref, dkeep_ref, gsend_ref, gkeep_ref, own_ref, up_ref, down_ref,
-    rows_tab, cot_tab, wsum, gacc, tacc, qacc, total,
-):
+def edge_kernel(shards, mesh_rows, halved, fetched, place_ref, pair_ref, other_ref, *refs):
+    sources, refs = refs[:fetched], refs[fetched:]
+    dsend_ref, dkeep_ref, gsend_ref, gkeep_ref, own_ref, up_ref, down_ref = refs[:7]
+    copies, refs = refs[7 : 7 + fetched], refs[7 + fetched :]
+    rows_tab, cot_tab, wsum, gacc, tacc, qacc, total, sems = refs
+    grid_ref, wrecv_ref, lat_ref, wsend_ref, bias_ref, gain_ref, cot_ref = copies[:7]
+    send_ref, recv_ref, live_ref, wout_ref = copies[7:]
     step = pl.program_id(0)
     band, high, low = place_ref[0], place_ref[1], place_ref[2]
     even = lax.rem(band, 2) == 0
     height, width = grid_ref.shape
     first_bias = 3 * mesh_rows
 
+    def fetch(k):
+        return pltpu.make_async_copy(sources[k], copies[k], sems.at[k])
+
     @pl.when(step == 0)
     def _():
+        for k in range(fetched):
+            fetch(k).start()
+
+    def arrived(first, last):
+        for k in range(first, last):
+            fetch(k).wait()
+
+    @pl.when(step == 0)
+    def _():
+        for ref in (wsum, gacc, tacc, qacc):
+            ref[...] = jnp.zeros_like(ref)
+        arrived(0, 2)
         proj = jnp.dot(grid_ref[...], wrecv_ref[...], preferred_element_type=F32)
         rows_tab[:height, :] = (0.5 * proj).astype(BF16)
+        arrived(2, 5)
         pair = pair_ref[...].astype(F32)
         other = other_ref[...].astype(F32)
         rows = [jnp.where(even, other, pair), lat_ref[...].astype(F32), jnp.where(even, pair, other)]
@@ -117,49 +134,65 @@
         rows_tab[height:, :] = jnp.concatenate(
             [sent, jnp.zeros((LANES - WINDOW_ROWS, width), F32)], axis=0
         ).astype(BF16)
+        arrived(5, 7)
         cot_tab[...] = (cot_ref[...].astype(F32) * gain_ref[...]).astype(BF16)
-        for ref in (wsum, gacc, tacc, qacc):
-            ref[...] = jnp.zeros_like(ref)
+        arrived(7, fetched)
 
     pieces = BLOCK // LANES
     each = SUB // LANES
-    near = table_rows(send_ref[...], mesh_rows, band, shards)
+    block = pl.ds(pl.multiple_of(step * BLOCK, BLOCK), BLOCK)
+    near = table_rows(send_ref[:, block], mesh_rows, band, shards)
     near_lines = rows_of(near, pieces)
-    recv_lines = rows_of(recv_ref[...], pieces)
-    cols = columns_of(recv_lines + near_lines + rows_of(live_ref[...], pieces))
+    recv_lines = rows_of(recv_ref[:, block], pieces)
+    cols = columns_of(recv_lines + near_lines + rows_of(live_ref[:, block], pieces))
     lane = lax.broadcasted_iota(jnp.int32, (1, LANES), 1)
     always = jnp.where((lane == first_bias) | (lane == first_bias + 1), 1.0, 0.0)
     scale = 1.0 / width
-    for part in range(BLOCK // SUB):
-        span = range(part * each, (part + 1) * each)
+    count = BLOCK // SUB
+    spans = [range(part * each, (part + 1) * each) for part in range(count)]
+
+    def hot_rows(span):
         hot = one_hot_rows([cols[i] for i in span], height)
-        hot_near = one_hot_rows([cols[pieces + i] for i in span], LANES, always)
-        live = jnp.concatenate([cols[2 * pieces + i] for i in span], axis=0)
-        z = jnp.dot(
-            jnp.concatenate([hot, hot_near], axis=1), rows_tab[...], preferred_element_type=F32
-        )
-        scaled = jnp.dot(hot, cot_tab[...], preferred_element_type=F32)
-        t = jnp.tanh(z)
-        u = t + 1.0
-        h = z * u
-        hidden = h.astype(BF16)
-        slope = u + h * (1.0 - t)
-        outer = jnp.dot(hidden, wout_ref[...], preferred_element_type=F32)
-        center = outer - jnp.sum(outer, axis=-1, keepdims=True) * scale
-        var = jnp.sum(center * center, axis=-1, keepdims=True) * scale
-        inv = lax.rsqrt(var + 1e-05) * live
-        normed = center * inv
-        product = scaled * normed
-        mean_s = jnp.sum(scaled, axis=-1, keepdims=True) * scale
-        mean_sn = jnp.sum(product, axis=-1, keepdims=True) * scale
-        d_outer = ((scaled - mean_s - normed * mean_sn) * inv).astype(BF16)
-        qacc[...] += groups(product)
-        wsum[...] += mix(hidden, d_outer, 0, 0)
-        d_pre = (mix(d_outer, wout_ref[...], 1, 1) * slope).astype(BF16)
-        hot = one_hot_cols([recv_lines[i] for i in span], height)
-        gacc[...] += jnp.dot(hot, d_pre, preferred_element_type=F32)
-        hot = one_hot_cols([near_lines[i] for i in span], WINDOW_ROWS)
-        tacc[...] += jnp.dot(hot, d_pre, preferred_element_type=F32)
+        near = one_hot_rows([cols[pieces + i] for i in span], LANES, always)
+        return hot, jnp.concatenate([hot, near], axis=1)
+
+    def row_mean(x):
+        return jnp.sum(x, axis=-1, keepdims=True) * scale
+
+    ahead, behind = hot_rows(spans[0]), None
+    for part in range(count + 1):
+        if part < count:
+            z = jnp.dot(ahead[1], rows_tab[...], preferred_element_type=F32)
+            scaled = jnp.dot(ahead[0], cot_tab[...], preferred_element_type=F32)
+        if behind is not None:
+            span, hidden_b, slope_b, scaled_b, outer = behind
+            live = jnp.concatenate([cols[2 * pieces + i] for i in span], axis=0)
+            center = outer - row_mean(outer)
+            inv = lax.rsqrt(row_mean(center * center) + 1e-05) * live
+            normed = center * inv
+            product = scaled_b * normed
+            d_outer = scaled_b - row_mean(scaled_b) - normed * row_mean(product)
+            d_outer = (d_outer * inv).astype(BF16)
+            qacc[...] += groups(product)
+            wsum[...] += mix(hidden_b, d_outer, 0, 0)
+            d_hidden = mix(d_outer, wout_ref[...], 1, 1)
+        if part < count:
+            t = jnp.tanh(z)
+            u = t + 1.0
+            h = z * u
+            hidden = h.astype(BF16)
+            slope = u + h * (1.0 - t)
+            outer = jnp.dot(hidden, wout_ref[...], preferred_element_type=F32)
+        if behind is not None:
+            d_pre = (d_hidden * slope_b).astype(BF16)
+            hot = one_hot_cols([recv_lines[i] for i in span], height)
+            gacc[...] += jnp.dot(hot, d_pre, preferred_element_type=F32)
+            hot = one_hot_cols([near_lines[i] for i in span], WINDOW_ROWS)
+            tacc[...] += jnp.dot(hot, d_pre, preferred_element_type=F32)
+        if part < count:
+            behind = (spans[part], hidden, slope, scaled, outer)
+        if part + 1 < count:
+            ahead = hot_rows(spans[part + 1])
 
     @pl.when(step == pl.num_programs(0) - 1)
     def _():
@@ -194,12 +227,12 @@
             gsend_ref[k] = gacc[pl.ds(theirs, share), :].astype(BF16)
 
 
-def edges(shards, levels, place, send, recv, live, grid, cot, lat, pair, other, *weights):
+def edges(shards, levels, place, pair, other, *fetched):
+    grid, send = fetched[0], fetched[7]
     slots = send.shape[1]
     height, width = grid.shape
-    mesh_rows = lat.shape[0]
+    mesh_rows = pair.shape[0]
     halved = sliced(width, shards * levels)
-    line = pl.BlockSpec((1, BLOCK), lambda i: (0, i))
     half = width // 2 if halved else width
     share = (levels // 2, height // levels, width)
     near = jax.ShapeDtypeStruct((mesh_rows, width), F32)
@@ -210,15 +243,15 @@
         jax.ShapeDtypeStruct(share, F32),
         near, near, near,
     ]
-    whole = (grid, cot, lat, pair, other) + weights
     return pl.pallas_call(
-        functools.partial(edge_kernel, shards, mesh_rows, halved),
+        functools.partial(edge_kernel, shards, mesh_rows, halved, len(fetched)),
         grid=(slots // BLOCK,),
-        in_specs=[pl.BlockSpec(memory_space=pltpu.SMEM), line, line, line]
-        + [full(array) for array in whole],
+        in_specs=[pl.BlockSpec(memory_space=pltpu.SMEM), full(pair), full(other)]
+        + [pl.BlockSpec(memory_space=pltpu.HBM)] * len(fetched),
         out_specs=[full(out) for out in outs],
         out_shape=outs,
-        scratch_shapes=[
+        scratch_shapes=[pltpu.VMEM(array.shape, array.dtype) for array in fetched]
+        + [
             pltpu.VMEM((height + LANES, width), BF16),
             pltpu.VMEM((height, width), BF16),
             pltpu.VMEM((width, width), F32),
@@ -226,11 +259,12 @@
             pltpu.VMEM((WINDOW_ROWS, width), F32),
             pltpu.VMEM((8, width), F32),
             pltpu.VMEM((width, width), F32),
+            pltpu.SemaphoreType.DMA((len(fetched),)),
         ],
         compiler_params=pltpu.CompilerParams(vmem_limit_bytes=EDGE_VMEM),
         cost_estimate=cost(14 * slots * width * width, 16 * width * width),
         name="edges",
-    )(place, send, recv, live, *whole)
+    )(place, pair, other, *[pltpu.with_memory_space_constraint(x, pltpu.HBM) for x in fetched])
 
 
 def combine_kernel(dkeep_ref, drecv_ref, gkeep_ref, grecv_ref, part_ref, gsend_ref, gown_ref):
@@ -260,7 +294,7 @@
             jax.ShapeDtypeStruct(gkeep.shape[1:], BF16),
             jax.ShapeDtypeStruct(gkeep.shape[1:], F32),
         ],
-        compiler_params=pltpu.CompilerParams(vmem_limit_bytes=EDGE_VMEM),
+        compiler_params=pltpu.CompilerParams(vmem_limit_bytes=COMBINE_VMEM),
         cost_estimate=cost(2 * dkeep.size, 8 * dkeep.size),
         name="combine_halves",
     )(dkeep, drecv, gkeep, grecv)
@@ -371,9 +405,9 @@
     lat_pair = swap(lat, "space", 1)
     lat_other = swap_between(lat, "space")
     dsend, dkeep, gsend, gkeep, own, pair, other = edges(
-        shards, levels, place, edge_sender, edge_receiver, edge_live,
-        grid_latent, grid_output_cotangent, lat, lat_pair, lat_other,
-        w_send, w_recv, output_weight, hidden_layer_bias[None], output_norm_gain[None],
+        shards, levels, place, lat_pair, lat_other,
+        grid_latent, w_recv, lat, w_send, hidden_layer_bias[None], output_norm_gain[None],
+        grid_output_cotangent, edge_sender, edge_receiver, edge_live, output_weight,
     )
     pair = swap(pair, "space", 1)
     other = swap_between(other, "space")

time: 88.9 us -> 80.6 us (0.907)
  Pallas kernels: 22.5 us -> 16.2 us
  local copies, waits for them, and re-layouts: 1.52 us -> 0.01 us
    pallas_call x1, Pallas kernels: 16.9 us -> 12.2 us  [edges(): pl.pallas_call(functools.partial(edge_kernel, shards, mesh_rows, halved,...]
    pallas_call x1, Pallas kernels: 2.63 us -> 0.98 us  [combine(): pl.pallas_call(combine_kernel, out_shape=[jax.ShapeDtypeStruct((parts, ro...]
    unnamed x26 -> x6, local copies, waits for them, and re-layouts: 1.52 us -> 0.01 us
  transfers between devices with their start and end apart: 11 -> 11, of which waited for: 6 -> 6; matrix products, arithmetic and copies ran while one was open for 2% -> 1% of each run, Pallas kernels for 0% -> 0%
where the time goes in v4:
time: 80.6 us; the launch traced here: 80.3 us
  waiting for transfers between devices  29.6 us (37%)
  starting transfers between devices  17.7 us (22%)
  Pallas kernels  16.2 us (20%)
  blocking collectives  15 us (19%)
  matrix products  1.02 us (1%)
    ppermute x8, waiting for transfers between devices, swap(): lax.ppermute(x, axis, [(i, i ^ bit) for i in range(lax.axis_size(axis))])  19.1 us
    all_to_all x1, blocking collectives, body(): received = {0: lax.all_to_all(payload, 'space', 0, 0, tiled=False)}  15 us
    pallas_call x1, Pallas kernels, edges(): pl.pallas_call(functools.partial(edge_kernel, shards, mesh_rows, halved,...  12.2 us
    all_to_all x1, waiting for transfers between devices, body(): part = lax.all_to_all(part, MOST, 0, 0, tiled=False)  10.5 us
    ppermute x8, starting transfers between devices, swap(): lax.ppermute(x, axis, [(i, i ^ bit) for i in range(lax.axis_size(axis))])  9.22 us
    all_to_all x1, starting transfers between devices, body(): part = lax.all_to_all(part, MOST, 0, 0, tiled=False)  6.48 us
    pallas_call x1, Pallas kernels, spread(): pl.pallas_call(functools.partial(spread_kernel, levels, mesh_rows), in_sp...  2.03 us
    ppermute x2, starting transfers between devices, swap_between(): return lax.ppermute(x, axis, pairs + [(j, i) for i, j in pairs] + ends)  2.01 us
  transfers between devices with their start and end apart: 11, of which 6 were waited for; matrix products, arithmetic and copies ran while one was open for 1% of the time, Pallas kernels for 0%

profile of v4, /device:TPU:0, one launch (start us, length us, event | category | flops | bytes accessed | tf_op | source)
XLA Modules:
  0.0 80.3 jit_solution(12955249009222021895)
XLA Ops:
  0.6 1.4 %collective-permute-start.1 = (bf16[8,512]{1,0:T(8,128)(2,1)}, bf16[8,512]{1,0:T(8,128)(2,1)S(1)}, u32[]{:S(2)}, u32[]{:S(2)}) collective-permute-start(bf16[8,512]{1,0:T(8,128)(2,1)} %bitcast.10), channel_id=1, source_target_pairs={{4,8},{12,16},{20,24},{8,4},{16,12},{24,20},{0,0},{28,28},{5,9},{1... | collective-permute-start | bytes 24584 | tf_op jit(solution)/shard_map/ppermute | solution.py:390
  2.0 5.1 %collective-permute-start = (bf16[8,512]{1,0:T(8,128)(2,1)}, bf16[8,512]{1,0:T(8,128)(2,1)S(1)}, u32[]{:S(2)}, u32[]{:S(2)}) collective-permute-start(bf16[8,512]{1,0:T(8,128)(2,1)} %bitcast.11), channel_id=1, source_target_pairs={{0,4},{4,0},{8,12},{12,8},{16,20},{20,16},{24,28},{28,24},{1,5},{5... | collective-permute-start | bytes 24584 | tf_op jit(solution)/shard_map/ppermute | solution.py:383
  7.1 0.1 pad_add_fusion.place_ref
  7.2 0.0 collective-permute-done.1.other_ref
  7.2 1.8 %collective-permute-done.pair_ref = bf16[8,512]{1,0:T(8,128)(2,1)S(1)} collective-permute-done((bf16[8,512]{1,0:T(8,128)(2,1)}, bf16[8,512]{1,0:T(8,128)(2,1)S(1)}, u32[]{:S(2)}, u32[]{:S(2)}) %collective-permute-start) | collective-permute-done | bytes 8224 | tf_op jit(solution)/shard_map/ppermute | solution.py:383
  9.0 12.2 %edges.1 = (bf16[520,512]{1,0:T(8,128)(2,1)S(1)}, f32[520,512]{1,0:T(8,128)S(1)}, bf16[2,128,512]{2,1,0:T(8,128)(2,1)S(1)}, f32[2,128,512]{2,1,0:T(8,128)S(1)}, ...) custom-call(s32[3]{0:T(128)S(1)} %pad_add_fusion.place_ref, ...), custom_call_target="tpu_custom_call" | custom-call | flops 7516192768 | bytes 4194304 | tf_op jit(solution)/shard_map/edges/pallas_call | solution.py:246
  21.2 0.1 collective-permute-start.2
  21.3 0.5 collective-permute-start.3
  21.8 1.8 %collective-permute-done.3.grecv_ref = bf16[2,128,512]{2,1,0:T(8,128)(2,1)S(1)} collective-permute-done((bf16[2,128,512]{2,1,0:T(8,128)(2,1)S(1)}, bf16[2,128,512]{2,1,0:T(8,128)(2,1)S(1)}, u32[]{:S(2)}, u32[]{:S(2)}) %collective-permute-start.3) | collective-permute-done | bytes 262176 | tf_op jit(solution)/shard_map/ppermute | solution.py:383
  23.6 0.0 collective-permute-done.2.drecv_ref
  23.6 1.0 %combine_halves.1 = (bf16[16,144,128]{2,1,0:T(8,128)(2,1)}, bf16[128,512]{1,0:T(8,128)(2,1)S(1)}, f32[128,512]{1,0:T(8,128)S(1)}) custom-call(f32[520,512]{1,0:T(8,128)S(1)} %get-tuple-element.24.dkeep_ref, bf16[520,512]{1,0:T(8,128)(2,1)S(1)} %collective-permute-done.2.drecv_ref, f32[2,128,512]{2,1,0:T(8,128)S(1)} %get-tuple-element.26.gkeep_ref, ...), custom_call_target="tpu_custom_call" | custom-call | flops 532480 | bytes 2129920 | tf_op jit(solution)/shard_map/combine_halves/pallas_call | solution.py:290
  24.6 0.0 copy-start
  24.6 0.0 copy-start.1
  24.6 6.5 %all-to-all-start = ((bf16[16,144,128]{2,1,0:T(8,128)(2,1)}), bf16[16,144,128]{2,1,0:T(8,128)(2,1)S(1)}, u32[]{:S(2)}, u32[]{:S(2)}) async-start(bf16[16,144,128]{2,1,0:T(8,128)(2,1)} %get-tuple-element.30), calls=%async_computation | async-start | bytes 1179648 | tf_op jit(solution)/shard_map/all_to_all | solution.py:435
  31.1 0.0 copy-start.2
  31.1 2.0 %collective-permute-start.5 = (f32[8,512]{1,0:T(8,128)S(1)}, f32[8,512]{1,0:T(8,128)S(1)}, u32[]{:S(2)}, u32[]{:S(2)}) collective-permute-start(f32[8,512]{1,0:T(8,128)S(1)} %get-tuple-element.32), channel_id=1, source_target_pairs={{0,4},{4,0},{8,12},{12,8},{16,20},{20,16},{24,28},{28,24},{1,5},{5... | collective-permute-start | bytes 49160 | tf_op jit(solution)/shard_map/ppermute | solution.py:383
  33.1 0.7 collective-permute-start.6
  33.7 3.3 %collective-permute-done.5.pair_ref = f32[8,512]{1,0:T(8,128)S(1)} collective-permute-done((f32[8,512]{1,0:T(8,128)S(1)}, f32[8,512]{1,0:T(8,128)S(1)}, u32[]{:S(2)}, u32[]{:S(2)}) %collective-permute-start.5) | collective-permute-done | bytes 16416 | tf_op jit(solution)/shard_map/ppermute | solution.py:383
  37.1 0.0 collective-permute-done.6.other_ref
  37.1 10.5 %all-to-all-done.part_ref = bf16[16,144,128]{2,1,0:T(8,128)(2,1)S(1)} async-done(((bf16[16,144,128]{2,1,0:T(8,128)(2,1)}), bf16[16,144,128]{2,1,0:T(8,128)(2,1)S(1)}, u32[]{:S(2)}, u32[]{:S(2)}) %all-to-all-start) | async-done | bytes 589856 | tf_op jit(solution)/shard_map/all_to_all | solution.py:435
  47.6 0.0 copy-done
  47.6 0.0 copy-done.1
  47.6 0.9 %sum_slabs.1 = (bf16[8,192,128]{2,1,0:T(8,128)(2,1)S(1)}, f32[8,512]{1,0:T(8,128)}, f32[1,512]{1,0:T(1,128)}, f32[1,512]{1,0:T(1,128)}) custom-call(bf16[16,144,128]{2,1,0:T(8,128)(2,1)S(1)} %all-to-all-done.part_ref, bf16[8,512]{1,0:T(8,128)(2,1)S(1)} %bitcast.13, f32[8,512]{1,0:T(8,128)S(1)} %get-tuple-element.31.own_ref, ...), custom_call_target="tpu_custom_call" | custom-call | flops 589824 | bytes 1179648 | tf_op jit(solution)/shard_map/sum_slabs/pallas_call | solution.py:327
  48.5 15.0 %all_to_all.10.refs_0_ = bf16[8,192,128]{2,1,0:T(8,128)(2,1)S(1)} all-to-all(bf16[8,192,128]{2,1,0:T(8,128)(2,1)S(1)} %get-tuple-element.35), channel_id=1, replica_groups=mesh['space'=8,'high'=2,'low'=2] {'space'}, dimensions={0} | all-to-all | bytes 786432 | tf_op jit(solution)/shard_map/all_to_all | solution.py:438
  63.5 0.8 collective-permute-start.8
  64.3 0.0 collective-permute-start.7
  64.3 7.0 %collective-permute-done.8.refs_2_ = bf16[8,192,128]{2,1,0:T(8,128)(2,1)S(1)} collective-permute-done((bf16[8,192,128]{2,1,0:T(8,128)(2,1)S(1)}, bf16[8,192,128]{2,1,0:T(8,128)(2,1)S(1)}, u32[]{:S(2)}, u32[]{:S(2)}) %collective-permute-start.8) | collective-permute-done | bytes 393248 | tf_op jit(solution)/shard_map/ppermute | solution.py:383
  71.3 0.0 collective-permute-start.9
  71.3 0.8 collective-permute-start.4
  72.1 5.2 %collective-permute-done.4 = bf16[128,512]{1,0:T(8,128)(2,1)S(1)} collective-permute-done((bf16[128,512]{1,0:T(8,128)(2,1)S(1)}, bf16[128,512]{1,0:T(8,128)(2,1)S(1)}, u32[]{:S(2)}, u32[]{:S(2)}) %collective-permute-start.4) | collective-permute-done | bytes 131104 | tf_op jit(solution)/shard_map/ppermute | solution.py:383
  77.2 0.0 copy-done.2
  77.2 1.0 %fusion = f32[128,512]{1,0:T(8,128)} fusion(bf16[512,512]{1,0:T(8,128)(2,1)S(1)} %copy-done.2, f32[128,512]{1,0:T(8,128)S(1)} %get-tuple-element.28, bf16[128,512]{1,0:T(8,128)(2,1)S(1)} %collective-permute-done.4), kind=kOutput, calls=%fused_computation.1 | convolution fusion | flops 67305472 | bytes 1179648 | tf_op jit(solution)/shard_map/dot_general | solution.py:33
  78.3 0.0 collective-permute-done.7.refs_1_
  78.3 0.0 collective-permute-done.9.refs_3_
  78.3 2.0 %spread_weights.1 = (bf16[512,512]{1,0:T(8,128)(2,1)}, bf16[512,512]{1,0:T(8,128)(2,1)}, bf16[512,512]{1,0:T(8,128)(2,1)}) custom-call(s32[3]{0:T(128)S(1)} %pad_add_fusion.place_ref, bf16[8,192,128]{2,1,0:T(8,128)(2,1)S(1)} %all_to_all.10.refs_0_, bf16[8,192,128]{2,1,0:T(8,128)(2,1)S(1)} %collective-permute-done.7.refs_1_, ...), custom_call_target="tpu_custom_call" | custom-call | flops 134217728 | bytes 2097152 | tf_op jit(solution)/shard_map/spread_weights/pallas_call | solution.py:370
Async XLA Ops:
  0.6 6.6 %collective-permute-start.1 = (bf16[8,512]{1,0:T(8,128)(2,1)}, bf16[8,512]{1,0:T(8,128)(2,1)S(1)}, u32[]{:S(2)}, u32[]{:S(2)}) collective-permute-start(bf16[8,512]{1,0:T(8,128)(2,1)} %bitcast.10), channel_id=1, source_target_pairs={{4,8},{12,16},{20,24},{8,4},{16,12},{24,20},{0,0},{28,28},{5,9},{1... | collective-permute-start | bytes 24584 | tf_op jit(solution)/shard_map/ppermute | solution.py:390
  2.0 7.0 %collective-permute-start = (bf16[8,512]{1,0:T(8,128)(2,1)}, bf16[8,512]{1,0:T(8,128)(2,1)S(1)}, u32[]{:S(2)}, u32[]{:S(2)}) collective-permute-start(bf16[8,512]{1,0:T(8,128)(2,1)} %bitcast.11), channel_id=1, source_target_pairs={{0,4},{4,0},{8,12},{12,8},{16,20},{20,16},{24,28},{28,24},{1,5},{5... | collective-permute-start | bytes 24584 | tf_op jit(solution)/shard_map/ppermute | solution.py:383
  21.2 2.4 %collective-permute-start.2 = (bf16[520,512]{1,0:T(8,128)(2,1)S(1)}, bf16[520,512]{1,0:T(8,128)(2,1)S(1)}, u32[]{:S(2)}, u32[]{:S(2)}) collective-permute-start(bf16[520,512]{1,0:T(8,128)(2,1)S(1)} %get-tuple-element.25), channel_id=1, source_target_pairs={{0,1},{1,0},{2,3},{3,2},{4,5},{5,4},{6,7},{7,6},{8,9},{9,8},{10,11... | collective-permute-start | bytes 1597448 | tf_op jit(solution)/shard_map/ppermute | solution.py:383
  21.3 2.3 %collective-permute-start.3 = (bf16[2,128,512]{2,1,0:T(8,128)(2,1)S(1)}, bf16[2,128,512]{2,1,0:T(8,128)(2,1)S(1)}, u32[]{:S(2)}, u32[]{:S(2)}) collective-permute-start(bf16[2,128,512]{2,1,0:T(8,128)(2,1)S(1)} %get-tuple-element.27), channel_id=1, source_target_pairs={{0,1},{1,0},{2,3},{3,2},{4,5},{5,4},{6,7},{7,6},{8,9},{9,8},{10,11... | collective-permute-start | bytes 786440 | tf_op jit(solution)/shard_map/ppermute | solution.py:383
  24.6 23.0 %copy-start = (bf16[512,512]{1,0:T(8,128)(2,1)S(1)}, bf16[512,512]{1,0:T(8,128)(2,1)}, u32[]{:S(2)}) copy-start(bf16[512,512]{1,0:T(8,128)(2,1)} %wsend_ref.1) | copy-start | bytes 1572868
  24.6 23.0 %copy-start.1 = (bf16[1,8,512]{2,1,0:T(8,128)(2,1)S(1)}, bf16[1,8,512]{2,1,0:T(8,128)(2,1)}, u32[]{:S(2)}) copy-start(bf16[1,8,512]{2,1,0:T(8,128)(2,1)} %param.12) | copy-start | bytes 24580
  24.6 23.0 %all-to-all-start = ((bf16[16,144,128]{2,1,0:T(8,128)(2,1)}), bf16[16,144,128]{2,1,0:T(8,128)(2,1)S(1)}, u32[]{:S(2)}, u32[]{:S(2)}) async-start(bf16[16,144,128]{2,1,0:T(8,128)(2,1)} %get-tuple-element.30), calls=%async_computation | async-start | bytes 1179648 | tf_op jit(solution)/shard_map/all_to_all | solution.py:435
  31.1 46.2 %copy-start.2 = (bf16[512,512]{1,0:T(8,128)(2,1)S(1)}, bf16[512,512]{1,0:T(8,128)(2,1)}, u32[]{:S(2)}) copy-start(bf16[512,512]{1,0:T(8,128)(2,1)} %refs_1_.1) | copy-start | bytes 1572868
  31.1 6.0 %collective-permute-start.5 = (f32[8,512]{1,0:T(8,128)S(1)}, f32[8,512]{1,0:T(8,128)S(1)}, u32[]{:S(2)}, u32[]{:S(2)}) collective-permute-start(f32[8,512]{1,0:T(8,128)S(1)} %get-tuple-element.32), channel_id=1, source_target_pairs={{0,4},{4,0},{8,12},{12,8},{16,20},{20,16},{24,28},{28,24},{1,5},{5... | collective-permute-start | bytes 49160 | tf_op jit(solution)/shard_map/ppermute | solution.py:383
  33.1 4.0 %collective-permute-start.6 = (f32[8,512]{1,0:T(8,128)S(1)}, f32[8,512]{1,0:T(8,128)S(1)}, u32[]{:S(2)}, u32[]{:S(2)}) collective-permute-start(f32[8,512]{1,0:T(8,128)S(1)} %get-tuple-element.33), channel_id=1, source_target_pairs={{4,8},{12,16},{20,24},{8,4},{16,12},{24,20},{0,0},{28,28},{5,9},{1... | collective-permute-start | bytes 49160 | tf_op jit(solution)/shard_map/ppermute | solution.py:390
  63.5 7.8 %collective-permute-start.8 = (bf16[8,192,128]{2,1,0:T(8,128)(2,1)S(1)}, bf16[8,192,128]{2,1,0:T(8,128)(2,1)S(1)}, u32[]{:S(2)}, u32[]{:S(2)}) collective-permute-start(bf16[8,192,128]{2,1,0:T(8,128)(2,1)S(1)} %all_to_all.10.refs_0_), channel_id=1, source_target_pairs={{0,2},{2,0},{1,3},{3,1},{4,6},{6,4},{5,7},{7,5},{8,10},{10,8},{9,1... | collective-permute-start | bytes 1179656 | tf_op jit(solution)/shard_map/ppermute | solution.py:383
  64.3 14.0 %collective-permute-start.7 = (bf16[8,192,128]{2,1,0:T(8,128)(2,1)S(1)}, bf16[8,192,128]{2,1,0:T(8,128)(2,1)S(1)}, u32[]{:S(2)}, u32[]{:S(2)}) collective-permute-start(bf16[8,192,128]{2,1,0:T(8,128)(2,1)S(1)} %all_to_all.10.refs_0_), channel_id=1, source_target_pairs={{0,1},{1,0},{2,3},{3,2},{4,5},{5,4},{6,7},{7,6},{8,9},{9,8},{10,11... | collective-permute-start | bytes 1179656 | tf_op jit(solution)/shard_map/ppermute | solution.py:383
  71.3 6.9 %collective-permute-start.9 = (bf16[8,192,128]{2,1,0:T(8,128)(2,1)S(1)}, bf16[8,192,128]{2,1,0:T(8,128)(2,1)S(1)}, u32[]{:S(2)}, u32[]{:S(2)}) collective-permute-start(bf16[8,192,128]{2,1,0:T(8,128)(2,1)S(1)} %collective-permute-done.8.refs_2_), channel_id=1, source_target_pairs={{0,1},{1,0},{2,3},{3,2},{4,5},{5,4},{6,7},{7,6},{8,9},{9,8},{10,11... | collective-permute-start | bytes 1179656 | tf_op jit(solution)/shard_map/ppermute | solution.py:383
  71.3 5.9 %collective-permute-start.4 = (bf16[128,512]{1,0:T(8,128)(2,1)S(1)}, bf16[128,512]{1,0:T(8,128)(2,1)S(1)}, u32[]{:S(2)}, u32[]{:S(2)}) collective-permute-start(bf16[128,512]{1,0:T(8,128)(2,1)S(1)} %get-tuple-element.29), channel_id=1, source_target_pairs={{0,2},{2,0},{1,3},{3,1},{4,6},{6,4},{5,7},{7,5},{8,10},{10,8},{9,1... | collective-permute-start | bytes 393224 | tf_op jit(solution)/shard_map/ppermute | solution.py:383

commit v5 on v4

--- a/solution.py
+++ b/solution.py
@@ -88,17 +88,51 @@
     return [rows[:, j : j + LANES] for j in range(0, rows.shape[1], LANES)]
 
 
-def edge_kernel(shards, mesh_rows, halved, fetched, place_ref, pair_ref, other_ref, *refs):
+def table_kernel(fetched, *refs):
+    sources, (rows_ref, cot_tab_ref) = refs[:fetched], refs[fetched : fetched + 2]
+    copies, sems = refs[fetched + 2 : -1], refs[-1]
+    grid_ref, w_ref, cot_ref, gain_ref = copies
+    moves = [pltpu.make_async_copy(sources[k], copies[k], sems.at[k]) for k in range(fetched)]
+    for move in moves:
+        move.start()
+    for move in moves[:2]:
+        move.wait()
+    proj = jnp.dot(grid_ref[...], w_ref[...], preferred_element_type=F32)
+    rows_ref[...] = (0.5 * proj).astype(BF16)
+    for move in moves[2:]:
+        move.wait()
+    cot_tab_ref[...] = (cot_ref[...].astype(F32) * gain_ref[...]).astype(BF16)
+
+
+def tables(*fetched):
+    out = jax.ShapeDtypeStruct(fetched[0].shape, BF16)
+    return pl.pallas_call(
+        functools.partial(table_kernel, len(fetched)),
+        in_specs=[pl.BlockSpec(memory_space=pltpu.HBM)] * len(fetched),
+        out_shape=[out, out],
+        scratch_shapes=[pltpu.VMEM(array.shape, array.dtype) for array in fetched]
+        + [pltpu.SemaphoreType.DMA((len(fetched),))],
+        compiler_params=pltpu.CompilerParams(vmem_limit_bytes=VMEM),
+        cost_estimate=cost(2 * out.size * out.shape[1], 4 * out.size),
+        name="tables",
+    )(*held(fetched))
+
+
+def held(arrays):
+    return [pltpu.with_memory_space_constraint(array, pltpu.HBM) for array in arrays]
+
+
+def edge_kernel(shards, mesh_rows, halved, fetched, place_ref, pair_ref, other_ref, rows_ref, cot_tab, *refs):
     sources, refs = refs[:fetched], refs[fetched:]
     dsend_ref, dkeep_ref, gsend_ref, gkeep_ref, own_ref, up_ref, down_ref = refs[:7]
     copies, refs = refs[7 : 7 + fetched], refs[7 + fetched :]
-    rows_tab, cot_tab, wsum, gacc, tacc, qacc, total, sems = refs
-    grid_ref, wrecv_ref, lat_ref, wsend_ref, bias_ref, gain_ref, cot_ref = copies[:7]
-    send_ref, recv_ref, live_ref, wout_ref = copies[7:]
+    rows_tab, wsum, acc, qacc, total, sems = refs
+    wsend_ref, lat_ref, bias_ref, send_ref, recv_ref, live_ref, wout_ref, gain_ref, grid_ref = copies
     step = pl.program_id(0)
     band, high, low = place_ref[0], place_ref[1], place_ref[2]
     even = lax.rem(band, 2) == 0
     height, width = grid_ref.shape
+    gacc, tacc = acc.at[:height, :], acc.at[height:, :]
     first_bias = 3 * mesh_rows
 
     def fetch(k):
@@ -115,12 +149,10 @@
 
     @pl.when(step == 0)
     def _():
-        for ref in (wsum, gacc, tacc, qacc):
+        for ref in (wsum, acc, qacc):
             ref[...] = jnp.zeros_like(ref)
-        arrived(0, 2)
-        proj = jnp.dot(grid_ref[...], wrecv_ref[...], preferred_element_type=F32)
-        rows_tab[:height, :] = (0.5 * proj).astype(BF16)
-        arrived(2, 5)
+        rows_tab[:height, :] = rows_ref[...]
+        arrived(0, 3)
         pair = pair_ref[...].astype(F32)
         other = other_ref[...].astype(F32)
         rows = [jnp.where(even, other, pair), lat_ref[...].astype(F32), jnp.where(even, pair, other)]
@@ -134,9 +166,7 @@
         rows_tab[height:, :] = jnp.concatenate(
             [sent, jnp.zeros((LANES - WINDOW_ROWS, width), F32)], axis=0
         ).astype(BF16)
-        arrived(5, 7)
-        cot_tab[...] = (cot_ref[...].astype(F32) * gain_ref[...]).astype(BF16)
-        arrived(7, fetched)
+        arrived(3, fetched)
 
     pieces = BLOCK // LANES
     each = SUB // LANES
@@ -185,10 +215,14 @@
             outer = jnp.dot(hidden, wout_ref[...], preferred_element_type=F32)
         if behind is not None:
             d_pre = (d_hidden * slope_b).astype(BF16)
-            hot = one_hot_cols([recv_lines[i] for i in span], height)
-            gacc[...] += jnp.dot(hot, d_pre, preferred_element_type=F32)
-            hot = one_hot_cols([near_lines[i] for i in span], WINDOW_ROWS)
-            tacc[...] += jnp.dot(hot, d_pre, preferred_element_type=F32)
+            hot = jnp.concatenate(
+                [
+                    one_hot_cols([recv_lines[i] for i in span], height),
+                    one_hot_cols([near_lines[i] for i in span], WINDOW_ROWS),
+                ],
+                axis=0,
+            )
+            acc[...] += jnp.dot(hot, d_pre, preferred_element_type=F32)
         if part < count:
             behind = (spans[part], hidden, slope, scaled, outer)
         if part + 1 < count:
@@ -227,8 +261,8 @@
             gsend_ref[k] = gacc[pl.ds(theirs, share), :].astype(BF16)
 
 
-def edges(shards, levels, place, pair, other, *fetched):
-    grid, send = fetched[0], fetched[7]
+def edges(shards, levels, place, pair, other, rows, cot, *fetched):
+    send, grid = fetched[3], fetched[-1]
     slots = send.shape[1]
     height, width = grid.shape
     mesh_rows = pair.shape[0]
@@ -246,17 +280,15 @@
     return pl.pallas_call(
         functools.partial(edge_kernel, shards, mesh_rows, halved, len(fetched)),
         grid=(slots // BLOCK,),
-        in_specs=[pl.BlockSpec(memory_space=pltpu.SMEM), full(pair), full(other)]
+        in_specs=[pl.BlockSpec(memory_space=pltpu.SMEM), full(pair), full(other), full(rows), full(cot)]
         + [pl.BlockSpec(memory_space=pltpu.HBM)] * len(fetched),
         out_specs=[full(out) for out in outs],
         out_shape=outs,
         scratch_shapes=[pltpu.VMEM(array.shape, array.dtype) for array in fetched]
         + [
             pltpu.VMEM((height + LANES, width), BF16),
-            pltpu.VMEM((height, width), BF16),
             pltpu.VMEM((width, width), F32),
-            pltpu.VMEM((height, width), F32),
-            pltpu.VMEM((WINDOW_ROWS, width), F32),
+            pltpu.VMEM((height + WINDOW_ROWS, width), F32),
             pltpu.VMEM((8, width), F32),
             pltpu.VMEM((width, width), F32),
             pltpu.SemaphoreType.DMA((len(fetched),)),
@@ -264,7 +296,7 @@
         compiler_params=pltpu.CompilerParams(vmem_limit_bytes=EDGE_VMEM),
         cost_estimate=cost(14 * slots * width * width, 16 * width * width),
         name="edges",
-    )(place, pair, other, *[pltpu.with_memory_space_constraint(x, pltpu.HBM) for x in fetched])
+    )(place, pair, other, rows, cot, *held(fetched))
 
 
 def combine_kernel(dkeep_ref, drecv_ref, gkeep_ref, grecv_ref, part_ref, gsend_ref, gown_ref):
@@ -276,9 +308,8 @@
         store_pieces(part_ref, k * slab, dkeep_ref[at, :] + drecv_ref[at, :].astype(F32))
     near = drecv_ref[2 * half :, :].astype(F32)
     vectors = dkeep_ref[2 * half : 2 * half + 2, :] + near[0:2] + near[2:4]
-    hi, lo = split(vectors)
-    extra = [v[k : k + 1] for v in (hi.astype(F32), lo.astype(F32)) for k in range(2)]
-    extra = jnp.concatenate([tile for v in extra for tile in tiles_of(v)], axis=0).astype(BF16)
+    extra = [tile for k in range(2) for tile in tiles_of(vectors[k : k + 1])]
+    extra = jnp.concatenate(extra, axis=0).astype(BF16)
     part_ref[:, 2 * slab :, :] = jnp.broadcast_to(extra[None], (part_ref.shape[0],) + extra.shape)
     gown_ref[...] = gkeep_ref[0] + grecv_ref[0].astype(F32)
     gsend_ref[...] = (gkeep_ref[1] + grecv_ref[1].astype(F32)).astype(BF16)
@@ -286,7 +317,7 @@
 
 def combine(parts, dkeep, drecv, gkeep, grecv):
     half, width = (dkeep.shape[0] - 8) // 2, dkeep.shape[1]
-    rows = (2 * half // parts + 4) * (width // LANES)
+    rows = (2 * half // parts + 2) * (width // LANES)
     return pl.pallas_call(
         combine_kernel,
         out_shape=[
@@ -305,11 +336,11 @@
     pay_ref, dmesh_ref, dbias_ref, dgain_ref,
 ):
     tiles = dbias_ref.shape[1] // LANES
-    slabs = part_ref.shape[1] - 4 * tiles
+    slabs = part_ref.shape[1] - 2 * tiles
     total = jnp.sum(part_ref[...].astype(F32), axis=0)
     for k, ref in enumerate((dbias_ref, dgain_ref)):
         base = slabs + k * tiles
-        both = total[base : base + tiles] + total[base + 2 * tiles : base + 3 * tiles]
+        both = total[base : base + tiles]
         for j in range(tiles):
             ref[:, j * LANES : (j + 1) * LANES] = both[j : j + 1]
     mesh = own_ref[...] + pair_ref[...] + other_ref[...]
@@ -322,7 +353,7 @@
 def sum_slabs(shards, part, lat, own, pair, other, wsend):
     mesh_rows, width = lat.shape
     tiles = width // LANES
-    rows = part.shape[1] - 4 * tiles + 2 * mesh_rows * tiles
+    rows = part.shape[1] - 2 * tiles + 2 * mesh_rows * tiles
     vector = jax.ShapeDtypeStruct((1, width), F32)
     return pl.pallas_call(
         sum_kernel,
@@ -404,10 +435,12 @@
 
     lat_pair = swap(lat, "space", 1)
     lat_other = swap_between(lat, "space")
+    gain = output_norm_gain[None]
+    rows, cot = tables(grid_latent, w_recv, grid_output_cotangent, gain)
     dsend, dkeep, gsend, gkeep, own, pair, other = edges(
-        shards, levels, place, lat_pair, lat_other,
-        grid_latent, w_recv, lat, w_send, hidden_layer_bias[None], output_norm_gain[None],
-        grid_output_cotangent, edge_sender, edge_receiver, edge_live, output_weight,
+        shards, levels, place, lat_pair, lat_other, rows, cot,
+        w_send, lat, hidden_layer_bias[None], edge_sender, edge_receiver, edge_live,
+        output_weight, gain, grid_latent,
     )
     pair = swap(pair, "space", 1)
     other = swap_between(other, "space")

time: 80.6 us -> 79.2 us (0.983)
  waiting for transfers between devices: 29.6 us -> 27.4 us
  Pallas kernels: 16.2 us -> 17.1 us
    pallas_call x0 -> x1, Pallas kernels: none -> 1.76 us  [tables(): pl.pallas_call(functools.partial(table_kernel, len(fetched)), in_specs=[p...]
    ppermute x8, waiting for transfers between devices: 19.1 us -> 17.4 us  [swap(): lax.ppermute(x, axis, [(i, i ^ bit) for i in range(lax.axis_size(axis))])]
  transfers between devices with their start and end apart: 11 -> 11, of which waited for: 6 -> 5; matrix products, arithmetic and copies ran while one was open for 1% -> 1% of each run, Pallas kernels for 0% -> 2%
where the time goes in v5:
time: 79.2 us; the launch traced here: 78.8 us
  waiting for transfers between devices  27.4 us (35%)
  starting transfers between devices  17.6 us (22%)
  Pallas kernels  17.1 us (22%)
  blocking collectives  15 us (19%)
  matrix products  1.02 us (1%)
    ppermute x8, waiting for transfers between devices, swap(): lax.ppermute(x, axis, [(i, i ^ bit) for i in range(lax.axis_size(axis))])  17.4 us
    all_to_all x1, blocking collectives, body(): received = {0: lax.all_to_all(payload, 'space', 0, 0, tiled=False)}  15 us
    pallas_call x1, Pallas kernels, edges(): pl.pallas_call(functools.partial(edge_kernel, shards, mesh_rows, halved,...  11.5 us
    all_to_all x1, waiting for transfers between devices, body(): part = lax.all_to_all(part, MOST, 0, 0, tiled=False)  10 us
    ppermute x8, starting transfers between devices, swap(): lax.ppermute(x, axis, [(i, i ^ bit) for i in range(lax.axis_size(axis))])  9.1 us
    all_to_all x1, starting transfers between devices, body(): part = lax.all_to_all(part, MOST, 0, 0, tiled=False)  6.45 us
    pallas_call x1, Pallas kernels, spread(): pl.pallas_call(functools.partial(spread_kernel, levels, mesh_rows), in_sp...  2.03 us
    ppermute x2, starting transfers between devices, swap_between(): return lax.ppermute(x, axis, pairs + [(j, i) for i, j in pairs] + ends)  2.01 us
  transfers between devices with their start and end apart: 11, of which 5 were waited for; matrix products, arithmetic and copies ran while one was open for 1% of the time, Pallas kernels for 2%

profile of v5, /device:TPU:0, one launch (start us, length us, event | category | flops | bytes accessed | tf_op | source)
XLA Modules:
  0.0 78.8 jit_solution(14654054037663723886)
XLA Ops:
  0.6 1.4 %collective-permute-start.1 = (bf16[8,512]{1,0:T(8,128)(2,1)}, bf16[8,512]{1,0:T(8,128)(2,1)S(1)}, u32[]{:S(2)}, u32[]{:S(2)}) collective-permute-start(bf16[8,512]{1,0:T(8,128)(2,1)} %bitcast.10), channel_id=1, source_target_pairs={{4,8},{12,16},{20,24},{8,4},{16,12},{24,20},{0,0},{28,28},{5,9},{1... | collective-permute-start | bytes 24584 | tf_op jit(solution)/shard_map/ppermute | solution.py:421
  2.0 5.1 %collective-permute-start = (bf16[8,512]{1,0:T(8,128)(2,1)}, bf16[8,512]{1,0:T(8,128)(2,1)S(1)}, u32[]{:S(2)}, u32[]{:S(2)}) collective-permute-start(bf16[8,512]{1,0:T(8,128)(2,1)} %bitcast.11), channel_id=1, source_target_pairs={{0,4},{4,0},{8,12},{12,8},{16,20},{20,16},{24,28},{28,24},{1,5},{5... | collective-permute-start | bytes 24584 | tf_op jit(solution)/shard_map/ppermute | solution.py:414
  7.1 0.1 pad_add_fusion.place_ref
  7.2 1.8 %tables.1 = (bf16[512,512]{1,0:T(8,128)(2,1)S(1)}, bf16[512,512]{1,0:T(8,128)(2,1)S(1)}) custom-call(bf16[512,512]{1,0:T(8,128)(2,1)} %refs_8_.1, bf16[512,512]{1,0:T(8,128)(2,1)} %refs_1_.1, bf16[512,512]{1,0:T(8,128)(2,1)} %refs_2_.1, f32[1,512]{1,0:T(1,128)} %bitcast.14), custom_call_target="tpu_custom_call" | custom-call | flops 268435456 | bytes 1048576 | tf_op jit(solution)/shard_map/tables/pallas_call | solution.py:109
  9.0 0.0 collective-permute-done.1.other_ref
  9.0 0.0 collective-permute-done.pair_ref
  9.0 11.5 %edges.1 = (bf16[520,512]{1,0:T(8,128)(2,1)S(1)}, f32[520,512]{1,0:T(8,128)S(1)}, bf16[2,128,512]{2,1,0:T(8,128)(2,1)S(1)}, f32[2,128,512]{2,1,0:T(8,128)S(1)}, ...) custom-call(s32[3]{0:T(128)S(1)} %pad_add_fusion.place_ref, ...), custom_call_target="tpu_custom_call" | custom-call | flops 7516192768 | bytes 4194304 | tf_op jit(solution)/shard_map/edges/pallas_call | solution.py:280
  20.5 0.1 collective-permute-start.2
  20.6 0.5 collective-permute-start.3
  21.1 1.8 %collective-permute-done.3.grecv_ref = bf16[2,128,512]{2,1,0:T(8,128)(2,1)S(1)} collective-permute-done((bf16[2,128,512]{2,1,0:T(8,128)(2,1)S(1)}, bf16[2,128,512]{2,1,0:T(8,128)(2,1)S(1)}, u32[]{:S(2)}, u32[]{:S(2)}) %collective-permute-start.3) | collective-permute-done | bytes 262176 | tf_op jit(solution)/shard_map/ppermute | solution.py:414
  22.9 0.0 collective-permute-done.2.drecv_ref
  22.9 1.0 %combine_halves.1 = (bf16[16,136,128]{2,1,0:T(8,128)(2,1)}, bf16[128,512]{1,0:T(8,128)(2,1)S(1)}, f32[128,512]{1,0:T(8,128)S(1)}) custom-call(f32[520,512]{1,0:T(8,128)S(1)} %get-tuple-element.28.dkeep_ref, bf16[520,512]{1,0:T(8,128)(2,1)S(1)} %collective-permute-done.2.drecv_ref, f32[2,128,512]{2,1,0:T(8,128)S(1)} %get-tuple-element.30.gkeep_ref, ...), custom_call_target="tpu_custom_call" | custom-call | flops 532480 | bytes 2129920 | tf_op jit(solution)/shard_map/combine_halves/pallas_call | solution.py:321
  23.8 0.0 copy-start
  23.8 0.0 copy-start.1
  23.8 6.4 %all-to-all-start = ((bf16[16,136,128]{2,1,0:T(8,128)(2,1)}), bf16[16,136,128]{2,1,0:T(8,128)(2,1)S(1)}, u32[]{:S(2)}, u32[]{:S(2)}) async-start(bf16[16,136,128]{2,1,0:T(8,128)(2,1)} %get-tuple-element.34), calls=%async_computation | async-start | bytes 1114112 | tf_op jit(solution)/shard_map/all_to_all | solution.py:468
  30.3 0.0 copy-start.2
  30.3 2.0 %collective-permute-start.5 = (f32[8,512]{1,0:T(8,128)S(1)}, f32[8,512]{1,0:T(8,128)S(1)}, u32[]{:S(2)}, u32[]{:S(2)}) collective-permute-start(f32[8,512]{1,0:T(8,128)S(1)} %get-tuple-element.36), channel_id=1, source_target_pairs={{0,4},{4,0},{8,12},{12,8},{16,20},{20,16},{24,28},{28,24},{1,5},{5... | collective-permute-start | bytes 49160 | tf_op jit(solution)/shard_map/ppermute | solution.py:414
  32.3 0.7 collective-permute-start.6
  32.9 3.3 %collective-permute-done.5.pair_ref = f32[8,512]{1,0:T(8,128)S(1)} collective-permute-done((f32[8,512]{1,0:T(8,128)S(1)}, f32[8,512]{1,0:T(8,128)S(1)}, u32[]{:S(2)}, u32[]{:S(2)}) %collective-permute-start.5) | collective-permute-done | bytes 16416 | tf_op jit(solution)/shard_map/ppermute | solution.py:414
  36.2 0.0 collective-permute-done.6.other_ref
  36.2 10.0 %all-to-all-done.part_ref = bf16[16,136,128]{2,1,0:T(8,128)(2,1)S(1)} async-done(((bf16[16,136,128]{2,1,0:T(8,128)(2,1)}), bf16[16,136,128]{2,1,0:T(8,128)(2,1)S(1)}, u32[]{:S(2)}, u32[]{:S(2)}) %all-to-all-start) | async-done | bytes 557088 | tf_op jit(solution)/shard_map/all_to_all | solution.py:468
  46.2 0.0 copy-done
  46.2 0.0 copy-done.1
  46.3 0.9 %sum_slabs.1 = (bf16[8,192,128]{2,1,0:T(8,128)(2,1)S(1)}, f32[8,512]{1,0:T(8,128)}, f32[1,512]{1,0:T(1,128)}, f32[1,512]{1,0:T(1,128)}) custom-call(bf16[16,136,128]{2,1,0:T(8,128)(2,1)S(1)} %all-to-all-done.part_ref, bf16[8,512]{1,0:T(8,128)(2,1)S(1)} %bitcast.13, f32[8,512]{1,0:T(8,128)S(1)} %get-tuple-element.35.own_ref, ...), custom_call_target="tpu_custom_call" | custom-call | flops 557056 | bytes 1114112 | tf_op jit(solution)/shard_map/sum_slabs/pallas_call | solution.py:358
  47.1 15.0 %all_to_all.10.refs_0_ = bf16[8,192,128]{2,1,0:T(8,128)(2,1)S(1)} all-to-all(bf16[8,192,128]{2,1,0:T(8,128)(2,1)S(1)} %get-tuple-element.39), channel_id=1, replica_groups=mesh['space'=8,'high'=2,'low'=2] {'space'}, dimensions={0} | all-to-all | bytes 786432 | tf_op jit(solution)/shard_map/all_to_all | solution.py:471
  62.1 0.7 collective-permute-start.8
  62.8 0.0 collective-permute-start.7
  62.8 7.1 %collective-permute-done.8.refs_2_ = bf16[8,192,128]{2,1,0:T(8,128)(2,1)S(1)} collective-permute-done((bf16[8,192,128]{2,1,0:T(8,128)(2,1)S(1)}, bf16[8,192,128]{2,1,0:T(8,128)(2,1)S(1)}, u32[]{:S(2)}, u32[]{:S(2)}) %collective-permute-start.8) | collective-permute-done | bytes 393248 | tf_op jit(solution)/shard_map/ppermute | solution.py:414
  69.9 0.0 collective-permute-start.9
  69.9 0.7 collective-permute-start.4
  70.6 5.2 %collective-permute-done.4 = bf16[128,512]{1,0:T(8,128)(2,1)S(1)} collective-permute-done((bf16[128,512]{1,0:T(8,128)(2,1)S(1)}, bf16[128,512]{1,0:T(8,128)(2,1)S(1)}, u32[]{:S(2)}, u32[]{:S(2)}) %collective-permute-start.4) | collective-permute-done | bytes 131104 | tf_op jit(solution)/shard_map/ppermute | solution.py:414
  75.8 0.0 copy-done.2
  75.8 1.0 %fusion = f32[128,512]{1,0:T(8,128)} fusion(bf16[512,512]{1,0:T(8,128)(2,1)S(1)} %copy-done.2, f32[128,512]{1,0:T(8,128)S(1)} %get-tuple-element.32, bf16[128,512]{1,0:T(8,128)(2,1)S(1)} %collective-permute-done.4), kind=kOutput, calls=%fused_computation.1 | convolution fusion | flops 67305472 | bytes 1179648 | tf_op jit(solution)/shard_map/dot_general | solution.py:33
  76.8 0.0 collective-permute-done.7.refs_1_
  76.8 0.0 collective-permute-done.9.refs_3_
  76.8 2.0 %spread_weights.1 = (bf16[512,512]{1,0:T(8,128)(2,1)}, bf16[512,512]{1,0:T(8,128)(2,1)}, bf16[512,512]{1,0:T(8,128)(2,1)}) custom-call(s32[3]{0:T(128)S(1)} %pad_add_fusion.place_ref, bf16[8,192,128]{2,1,0:T(8,128)(2,1)S(1)} %all_to_all.10.refs_0_, bf16[8,192,128]{2,1,0:T(8,128)(2,1)S(1)} %collective-permute-done.7.refs_1_, ...), custom_call_target="tpu_custom_call" | custom-call | flops 134217728 | bytes 2097152 | tf_op jit(solution)/shard_map/spread_weights/pallas_call | solution.py:401
Async XLA Ops:
  0.6 8.3 %collective-permute-start.1 = (bf16[8,512]{1,0:T(8,128)(2,1)}, bf16[8,512]{1,0:T(8,128)(2,1)S(1)}, u32[]{:S(2)}, u32[]{:S(2)}) collective-permute-start(bf16[8,512]{1,0:T(8,128)(2,1)} %bitcast.10), channel_id=1, source_target_pairs={{4,8},{12,16},{20,24},{8,4},{16,12},{24,20},{0,0},{28,28},{5,9},{1... | collective-permute-start | bytes 24584 | tf_op jit(solution)/shard_map/ppermute | solution.py:421
  2.0 7.0 %collective-permute-start = (bf16[8,512]{1,0:T(8,128)(2,1)}, bf16[8,512]{1,0:T(8,128)(2,1)S(1)}, u32[]{:S(2)}, u32[]{:S(2)}) collective-permute-start(bf16[8,512]{1,0:T(8,128)(2,1)} %bitcast.11), channel_id=1, source_target_pairs={{0,4},{4,0},{8,12},{12,8},{16,20},{20,16},{24,28},{28,24},{1,5},{5... | collective-permute-start | bytes 24584 | tf_op jit(solution)/shard_map/ppermute | solution.py:414
  20.5 2.4 %collective-permute-start.2 = (bf16[520,512]{1,0:T(8,128)(2,1)S(1)}, bf16[520,512]{1,0:T(8,128)(2,1)S(1)}, u32[]{:S(2)}, u32[]{:S(2)}) collective-permute-start(bf16[520,512]{1,0:T(8,128)(2,1)S(1)} %get-tuple-element.29), channel_id=1, source_target_pairs={{0,1},{1,0},{2,3},{3,2},{4,5},{5,4},{6,7},{7,6},{8,9},{9,8},{10,11... | collective-permute-start | bytes 1597448 | tf_op jit(solution)/shard_map/ppermute | solution.py:414
  20.6 2.3 %collective-permute-start.3 = (bf16[2,128,512]{2,1,0:T(8,128)(2,1)S(1)}, bf16[2,128,512]{2,1,0:T(8,128)(2,1)S(1)}, u32[]{:S(2)}, u32[]{:S(2)}) collective-permute-start(bf16[2,128,512]{2,1,0:T(8,128)(2,1)S(1)} %get-tuple-element.31), channel_id=1, source_target_pairs={{0,1},{1,0},{2,3},{3,2},{4,5},{5,4},{6,7},{7,6},{8,9},{9,8},{10,11... | collective-permute-start | bytes 786440 | tf_op jit(solution)/shard_map/ppermute | solution.py:414
  23.8 22.4 %copy-start = (bf16[512,512]{1,0:T(8,128)(2,1)S(1)}, bf16[512,512]{1,0:T(8,128)(2,1)}, u32[]{:S(2)}) copy-start(bf16[512,512]{1,0:T(8,128)(2,1)} %wsend_ref.1) | copy-start | bytes 1572868
  23.8 22.4 %copy-start.1 = (bf16[1,8,512]{2,1,0:T(8,128)(2,1)S(1)}, bf16[1,8,512]{2,1,0:T(8,128)(2,1)}, u32[]{:S(2)}) copy-start(bf16[1,8,512]{2,1,0:T(8,128)(2,1)} %param.12) | copy-start | bytes 24580
  23.8 22.4 %all-to-all-start = ((bf16[16,136,128]{2,1,0:T(8,128)(2,1)}), bf16[16,136,128]{2,1,0:T(8,128)(2,1)S(1)}, u32[]{:S(2)}, u32[]{:S(2)}) async-start(bf16[16,136,128]{2,1,0:T(8,128)(2,1)} %get-tuple-element.34), calls=%async_computation | async-start | bytes 1114112 | tf_op jit(solution)/shard_map/all_to_all | solution.py:468
  30.3 45.5 %copy-start.2 = (bf16[512,512]{1,0:T(8,128)(2,1)S(1)}, bf16[512,512]{1,0:T(8,128)(2,1)}, u32[]{:S(2)}) copy-start(bf16[512,512]{1,0:T(8,128)(2,1)} %refs_1_.1) | copy-start | bytes 1572868
  30.3 5.9 %collective-permute-start.5 = (f32[8,512]{1,0:T(8,128)S(1)}, f32[8,512]{1,0:T(8,128)S(1)}, u32[]{:S(2)}, u32[]{:S(2)}) collective-permute-start(f32[8,512]{1,0:T(8,128)S(1)} %get-tuple-element.36), channel_id=1, source_target_pairs={{0,4},{4,0},{8,12},{12,8},{16,20},{20,16},{24,28},{28,24},{1,5},{5... | collective-permute-start | bytes 49160 | tf_op jit(solution)/shard_map/ppermute | solution.py:414
  32.3 3.9 %collective-permute-start.6 = (f32[8,512]{1,0:T(8,128)S(1)}, f32[8,512]{1,0:T(8,128)S(1)}, u32[]{:S(2)}, u32[]{:S(2)}) collective-permute-start(f32[8,512]{1,0:T(8,128)S(1)} %get-tuple-element.37), channel_id=1, source_target_pairs={{4,8},{12,16},{20,24},{8,4},{16,12},{24,20},{0,0},{28,28},{5,9},{1... | collective-permute-start | bytes 49160 | tf_op jit(solution)/shard_map/ppermute | solution.py:421
  62.1 7.8 %collective-permute-start.8 = (bf16[8,192,128]{2,1,0:T(8,128)(2,1)S(1)}, bf16[8,192,128]{2,1,0:T(8,128)(2,1)S(1)}, u32[]{:S(2)}, u32[]{:S(2)}) collective-permute-start(bf16[8,192,128]{2,1,0:T(8,128)(2,1)S(1)} %all_to_all.10.refs_0_), channel_id=1, source_target_pairs={{0,2},{2,0},{1,3},{3,1},{4,6},{6,4},{5,7},{7,5},{8,10},{10,8},{9,1... | collective-permute-start | bytes 1179656 | tf_op jit(solution)/shard_map/ppermute | solution.py:414
  62.8 14.0 %collective-permute-start.7 = (bf16[8,192,128]{2,1,0:T(8,128)(2,1)S(1)}, bf16[8,192,128]{2,1,0:T(8,128)(2,1)S(1)}, u32[]{:S(2)}, u32[]{:S(2)}) collective-permute-start(bf16[8,192,128]{2,1,0:T(8,128)(2,1)S(1)} %all_to_all.10.refs_0_), channel_id=1, source_target_pairs={{0,1},{1,0},{2,3},{3,2},{4,5},{5,4},{6,7},{7,6},{8,9},{9,8},{10,11... | collective-permute-start | bytes 1179656 | tf_op jit(solution)/shard_map/ppermute | solution.py:414
  69.9 6.9 %collective-permute-start.9 = (bf16[8,192,128]{2,1,0:T(8,128)(2,1)S(1)}, bf16[8,192,128]{2,1,0:T(8,128)(2,1)S(1)}, u32[]{:S(2)}, u32[]{:S(2)}) collective-permute-start(bf16[8,192,128]{2,1,0:T(8,128)(2,1)S(1)} %collective-permute-done.8.refs_2_), channel_id=1, source_target_pairs={{0,1},{1,0},{2,3},{3,2},{4,5},{5,4},{6,7},{7,6},{8,9},{9,8},{10,11... | collective-permute-start | bytes 1179656 | tf_op jit(solution)/shard_map/ppermute | solution.py:414
  69.9 5.9 %collective-permute-start.4 = (bf16[128,512]{1,0:T(8,128)(2,1)S(1)}, bf16[128,512]{1,0:T(8,128)(2,1)S(1)}, u32[]{:S(2)}, u32[]{:S(2)}) collective-permute-start(bf16[128,512]{1,0:T(8,128)(2,1)S(1)} %get-tuple-element.33), channel_id=1, source_target_pairs={{0,2},{2,0},{1,3},{3,1},{4,6},{6,4},{5,7},{7,5},{8,10},{10,8},{9,1... | collective-permute-start | bytes 393224 | tf_op jit(solution)/shard_map/ppermute | solution.py:414

commit v6 on v5

--- a/solution.py
+++ b/solution.py
@@ -88,29 +88,35 @@
     return [rows[:, j : j + LANES] for j in range(0, rows.shape[1], LANES)]
 
 
-def table_kernel(fetched, *refs):
-    sources, (rows_ref, cot_tab_ref) = refs[:fetched], refs[fetched : fetched + 2]
-    copies, sems = refs[fetched + 2 : -1], refs[-1]
+def table_kernel(count, *refs):
+    sources, (rows_ref, cot_tab_ref) = refs[:count], refs[count : count + 2]
+    kept, copies, sems = refs[count + 2 : -5], refs[-5:-1], refs[-1]
     grid_ref, w_ref, cot_ref, gain_ref = copies
-    moves = [pltpu.make_async_copy(sources[k], copies[k], sems.at[k]) for k in range(fetched)]
+    targets = copies + kept
+    moves = [pltpu.make_async_copy(sources[k], targets[k], sems.at[k]) for k in range(count)]
     for move in moves:
         move.start()
     for move in moves[:2]:
         move.wait()
     proj = jnp.dot(grid_ref[...], w_ref[...], preferred_element_type=F32)
     rows_ref[...] = (0.5 * proj).astype(BF16)
-    for move in moves[2:]:
+    for move in moves[2:4]:
         move.wait()
     cot_tab_ref[...] = (cot_ref[...].astype(F32) * gain_ref[...]).astype(BF16)
-
-
-def tables(*fetched):
-    out = jax.ShapeDtypeStruct(fetched[0].shape, BF16)
+    for move in moves[4:]:
+        move.wait()
+
+
+def tables(grid, w, cot, gain, *kept):
+    fetched = (grid, w, cot, gain) + kept
+    out = jax.ShapeDtypeStruct(grid.shape, BF16)
+    outs = [out, out] + [jax.ShapeDtypeStruct(array.shape, array.dtype) for array in kept]
     return pl.pallas_call(
         functools.partial(table_kernel, len(fetched)),
         in_specs=[pl.BlockSpec(memory_space=pltpu.HBM)] * len(fetched),
-        out_shape=[out, out],
-        scratch_shapes=[pltpu.VMEM(array.shape, array.dtype) for array in fetched]
+        out_specs=[pl.BlockSpec(memory_space=pltpu.VMEM)] * len(outs),
+        out_shape=outs,
+        scratch_shapes=[pltpu.VMEM(array.shape, array.dtype) for array in fetched[:4]]
         + [pltpu.SemaphoreType.DMA((len(fetched),))],
         compiler_params=pltpu.CompilerParams(vmem_limit_bytes=VMEM),
         cost_estimate=cost(2 * out.size * out.shape[1], 4 * out.size),
@@ -123,11 +129,12 @@
 
 
 def edge_kernel(shards, mesh_rows, halved, fetched, place_ref, pair_ref, other_ref, rows_ref, cot_tab, *refs):
+    (wsend_ref, wout_ref), refs = refs[:2], refs[2:]
     sources, refs = refs[:fetched], refs[fetched:]
     dsend_ref, dkeep_ref, gsend_ref, gkeep_ref, own_ref, up_ref, down_ref = refs[:7]
     copies, refs = refs[7 : 7 + fetched], refs[7 + fetched :]
     rows_tab, wsum, acc, qacc, total, sems = refs
-    wsend_ref, lat_ref, bias_ref, send_ref, recv_ref, live_ref, wout_ref, gain_ref, grid_ref = copies
+    lat_ref, bias_ref, send_ref, recv_ref, live_ref, gain_ref, grid_ref = copies
     step = pl.program_id(0)
     band, high, low = place_ref[0], place_ref[1], place_ref[2]
     even = lax.rem(band, 2) == 0
@@ -152,7 +159,7 @@
         for ref in (wsum, acc, qacc):
             ref[...] = jnp.zeros_like(ref)
         rows_tab[:height, :] = rows_ref[...]
-        arrived(0, 3)
+        arrived(0, 2)
         pair = pair_ref[...].astype(F32)
         other = other_ref[...].astype(F32)
         rows = [jnp.where(even, other, pair), lat_ref[...].astype(F32), jnp.where(even, pair, other)]
@@ -166,7 +173,7 @@
         rows_tab[height:, :] = jnp.concatenate(
             [sent, jnp.zeros((LANES - WINDOW_ROWS, width), F32)], axis=0
         ).astype(BF16)
-        arrived(3, fetched)
+        arrived(2, fetched)
 
     pieces = BLOCK // LANES
     each = SUB // LANES
@@ -261,8 +268,9 @@
             gsend_ref[k] = gacc[pl.ds(theirs, share), :].astype(BF16)
 
 
-def edges(shards, levels, place, pair, other, rows, cot, *fetched):
-    send, grid = fetched[3], fetched[-1]
+def edges(shards, levels, place, pair, other, rows, cot, wsend, wout, *fetched):
+    send, grid = fetched[2], fetched[-1]
+    ready = (pair, other, rows, cot, wsend, wout)
     slots = send.shape[1]
     height, width = grid.shape
     mesh_rows = pair.shape[0]
@@ -280,7 +288,7 @@
     return pl.pallas_call(
         functools.partial(edge_kernel, shards, mesh_rows, halved, len(fetched)),
         grid=(slots // BLOCK,),
-        in_specs=[pl.BlockSpec(memory_space=pltpu.SMEM), full(pair), full(other), full(rows), full(cot)]
+        in_specs=[pl.BlockSpec(memory_space=pltpu.SMEM), *map(full, ready)]
         + [pl.BlockSpec(memory_space=pltpu.HBM)] * len(fetched),
         out_specs=[full(out) for out in outs],
         out_shape=outs,
@@ -296,7 +304,7 @@
         compiler_params=pltpu.CompilerParams(vmem_limit_bytes=EDGE_VMEM),
         cost_estimate=cost(14 * slots * width * width, 16 * width * width),
         name="edges",
-    )(place, pair, other, rows, cot, *held(fetched))
+    )(place, *ready, *held(fetched))
 
 
 def combine_kernel(dkeep_ref, drecv_ref, gkeep_ref, grecv_ref, part_ref, gsend_ref, gown_ref):
@@ -436,11 +444,13 @@
     lat_pair = swap(lat, "space", 1)
     lat_other = swap_between(lat, "space")
     gain = output_norm_gain[None]
-    rows, cot = tables(grid_latent, w_recv, grid_output_cotangent, gain)
+    ready = tables(
+        grid_latent, w_recv, grid_output_cotangent, gain, w_send, output_weight
+    )
     dsend, dkeep, gsend, gkeep, own, pair, other = edges(
-        shards, levels, place, lat_pair, lat_other, rows, cot,
-        w_send, lat, hidden_layer_bias[None], edge_sender, edge_receiver, edge_live,
-        output_weight, gain, grid_latent,
+        shards, levels, place, lat_pair, lat_other, *ready,
+        lat, hidden_layer_bias[None], edge_sender, edge_receiver, edge_live,
+        gain, grid_latent,
     )
     pair = swap(pair, "space", 1)
     other = swap_between(other, "space")

time: 79.2 us -> 78.9 us (level)
  no operation moved by 1% of the time
where the time goes in v6:
time: 78.9 us; the launch traced here: 78.5 us
  waiting for transfers between devices  27.4 us (35%)
  starting transfers between devices  17.5 us (22%)
  Pallas kernels  16.8 us (21%)
  blocking collectives  15 us (19%)
  matrix products  1.02 us (1%)
    ppermute x8, waiting for transfers between devices, swap(): lax.ppermute(x, axis, [(i, i ^ bit) for i in range(lax.axis_size(axis))])  17.4 us
    all_to_all x1, blocking collectives, body(): received = {0: lax.all_to_all(payload, 'space', 0, 0, tiled=False)}  15 us
    pallas_call x1, Pallas kernels, edges(): pl.pallas_call(functools.partial(edge_kernel, shards, mesh_rows, halved,...  11.2 us
    all_to_all x1, waiting for transfers between devices, body(): part = lax.all_to_all(part, MOST, 0, 0, tiled=False)  10 us
    ppermute x8, starting transfers between devices, swap(): lax.ppermute(x, axis, [(i, i ^ bit) for i in range(lax.axis_size(axis))])  9.1 us
    all_to_all x1, starting transfers between devices, body(): part = lax.all_to_all(part, MOST, 0, 0, tiled=False)  6.42 us
    pallas_call x1, Pallas kernels, spread(): pl.pallas_call(functools.partial(spread_kernel, levels, mesh_rows), in_sp...  2.03 us
    ppermute x2, starting transfers between devices, swap_between(): return lax.ppermute(x, axis, pairs + [(j, i) for i, j in pairs] + ends)  2.01 us
  transfers between devices with their start and end apart: 11, of which 5 were waited for; matrix products, arithmetic and copies ran while one was open for 1% of the time, Pallas kernels for 2%

profile of v6, /device:TPU:0, one launch (start us, length us, event | category | flops | bytes accessed | tf_op | source)
XLA Modules:
  0.0 78.5 jit_solution(12976820336958090566)
XLA Ops:
  0.6 1.4 %collective-permute-start.1 = (bf16[8,512]{1,0:T(8,128)(2,1)}, bf16[8,512]{1,0:T(8,128)(2,1)S(1)}, u32[]{:S(2)}, u32[]{:S(2)}) collective-permute-start(bf16[8,512]{1,0:T(8,128)(2,1)} %bitcast.10), channel_id=1, source_target_pairs={{4,8},{12,16},{20,24},{8,4},{16,12},{24,20},{0,0},{28,28},{5,9},{1... | collective-permute-start | bytes 24584 | tf_op jit(solution)/shard_map/ppermute | solution.py:429
  2.0 5.1 %collective-permute-start = (bf16[8,512]{1,0:T(8,128)(2,1)}, bf16[8,512]{1,0:T(8,128)(2,1)S(1)}, u32[]{:S(2)}, u32[]{:S(2)}) collective-permute-start(bf16[8,512]{1,0:T(8,128)(2,1)} %bitcast.11), channel_id=1, source_target_pairs={{0,4},{4,0},{8,12},{12,8},{16,20},{20,16},{24,28},{28,24},{1,5},{5... | collective-permute-start | bytes 24584 | tf_op jit(solution)/shard_map/ppermute | solution.py:422
  7.1 0.1 pad_add_fusion.place_ref
  7.2 1.8 %tables.1 = (bf16[512,512]{1,0:T(8,128)(2,1)S(1)}, bf16[512,512]{1,0:T(8,128)(2,1)S(1)}, bf16[512,512]{1,0:T(8,128)(2,1)S(1)}, bf16[512,512]{1,0:T(8,128)(2,1)S(1)}) custom-call(bf16[512,512]{1,0:T(8,128)(2,1)} %refs_8_.1, bf16[512,512]{1,0:T(8,128)(2,1)} %refs_1_.1, bf16[512,512]{1,0:T(8,128)(2,1)} %refs_2_.1, f32[1,512]{1,0:T(1,128)} %bitcast.14, ...), custom_call_target="tpu_custom_call" | custom-call | flops 268435456 | bytes 1048576 | tf_op jit(solution)/shard_map/tables/pallas_call | solution.py:114
  9.0 0.0 collective-permute-done.1.other_ref
  9.0 0.0 collective-permute-done.pair_ref
  9.0 11.2 %edges.1 = (bf16[520,512]{1,0:T(8,128)(2,1)S(1)}, f32[520,512]{1,0:T(8,128)S(1)}, bf16[2,128,512]{2,1,0:T(8,128)(2,1)S(1)}, f32[2,128,512]{2,1,0:T(8,128)S(1)}, ...) custom-call(s32[3]{0:T(128)S(1)} %pad_add_fusion.place_ref, ...), custom_call_target="tpu_custom_call" | custom-call | flops 7516192768 | bytes 4194304 | tf_op jit(solution)/shard_map/edges/pallas_call | solution.py:288
  20.2 0.1 collective-permute-start.2
  20.3 0.5 collective-permute-start.3
  20.8 1.8 %collective-permute-done.3.grecv_ref = bf16[2,128,512]{2,1,0:T(8,128)(2,1)S(1)} collective-permute-done((bf16[2,128,512]{2,1,0:T(8,128)(2,1)S(1)}, bf16[2,128,512]{2,1,0:T(8,128)(2,1)S(1)}, u32[]{:S(2)}, u32[]{:S(2)}) %collective-permute-start.3) | collective-permute-done | bytes 262176 | tf_op jit(solution)/shard_map/ppermute | solution.py:422
  22.6 0.0 collective-permute-done.2.drecv_ref
  22.6 1.0 %combine_halves.1 = (bf16[16,136,128]{2,1,0:T(8,128)(2,1)}, bf16[128,512]{1,0:T(8,128)(2,1)S(1)}, f32[128,512]{1,0:T(8,128)S(1)}) custom-call(f32[520,512]{1,0:T(8,128)S(1)} %get-tuple-element.32.dkeep_ref, bf16[520,512]{1,0:T(8,128)(2,1)S(1)} %collective-permute-done.2.drecv_ref, f32[2,128,512]{2,1,0:T(8,128)S(1)} %get-tuple-element.34.gkeep_ref, ...), custom_call_target="tpu_custom_call" | custom-call | flops 532480 | bytes 2129920 | tf_op jit(solution)/shard_map/combine_halves/pallas_call | solution.py:329
  23.5 0.0 copy-start
  23.5 0.0 copy-start.1
  23.5 6.4 %all-to-all-start = ((bf16[16,136,128]{2,1,0:T(8,128)(2,1)}), bf16[16,136,128]{2,1,0:T(8,128)(2,1)S(1)}, u32[]{:S(2)}, u32[]{:S(2)}) async-start(bf16[16,136,128]{2,1,0:T(8,128)(2,1)} %get-tuple-element.38), calls=%async_computation | async-start | bytes 1114112 | tf_op jit(solution)/shard_map/all_to_all | solution.py:478
  30.0 0.0 copy-start.2
  30.0 2.0 %collective-permute-start.5 = (f32[8,512]{1,0:T(8,128)S(1)}, f32[8,512]{1,0:T(8,128)S(1)}, u32[]{:S(2)}, u32[]{:S(2)}) collective-permute-start(f32[8,512]{1,0:T(8,128)S(1)} %get-tuple-element.40), channel_id=1, source_target_pairs={{0,4},{4,0},{8,12},{12,8},{16,20},{20,16},{24,28},{28,24},{1,5},{5... | collective-permute-start | bytes 49160 | tf_op jit(solution)/shard_map/ppermute | solution.py:422
  32.0 0.7 collective-permute-start.6
  32.6 3.3 %collective-permute-done.5.pair_ref = f32[8,512]{1,0:T(8,128)S(1)} collective-permute-done((f32[8,512]{1,0:T(8,128)S(1)}, f32[8,512]{1,0:T(8,128)S(1)}, u32[]{:S(2)}, u32[]{:S(2)}) %collective-permute-start.5) | collective-permute-done | bytes 16416 | tf_op jit(solution)/shard_map/ppermute | solution.py:422
  35.9 0.0 collective-permute-done.6.other_ref
  35.9 10.0 %all-to-all-done.part_ref = bf16[16,136,128]{2,1,0:T(8,128)(2,1)S(1)} async-done(((bf16[16,136,128]{2,1,0:T(8,128)(2,1)}), bf16[16,136,128]{2,1,0:T(8,128)(2,1)S(1)}, u32[]{:S(2)}, u32[]{:S(2)}) %all-to-all-start) | async-done | bytes 557088 | tf_op jit(solution)/shard_map/all_to_all | solution.py:478
  45.9 0.0 copy-done
  45.9 0.0 copy-done.1
  45.9 0.9 %sum_slabs.1 = (bf16[8,192,128]{2,1,0:T(8,128)(2,1)S(1)}, f32[8,512]{1,0:T(8,128)}, f32[1,512]{1,0:T(1,128)}, f32[1,512]{1,0:T(1,128)}) custom-call(bf16[16,136,128]{2,1,0:T(8,128)(2,1)S(1)} %all-to-all-done.part_ref, bf16[8,512]{1,0:T(8,128)(2,1)S(1)} %bitcast.13, f32[8,512]{1,0:T(8,128)S(1)} %get-tuple-element.39.own_ref, ...), custom_call_target="tpu_custom_call" | custom-call | flops 557056 | bytes 1114112 | tf_op jit(solution)/shard_map/sum_slabs/pallas_call | solution.py:366
  46.8 15.0 %all_to_all.10.refs_0_ = bf16[8,192,128]{2,1,0:T(8,128)(2,1)S(1)} all-to-all(bf16[8,192,128]{2,1,0:T(8,128)(2,1)S(1)} %get-tuple-element.43), channel_id=1, replica_groups=mesh['space'=8,'high'=2,'low'=2] {'space'}, dimensions={0} | all-to-all | bytes 786432 | tf_op jit(solution)/shard_map/all_to_all | solution.py:481
  61.8 0.7 collective-permute-start.8
  62.5 0.0 collective-permute-start.7
  62.5 7.1 %collective-permute-done.8.refs_2_ = bf16[8,192,128]{2,1,0:T(8,128)(2,1)S(1)} collective-permute-done((bf16[8,192,128]{2,1,0:T(8,128)(2,1)S(1)}, bf16[8,192,128]{2,1,0:T(8,128)(2,1)S(1)}, u32[]{:S(2)}, u32[]{:S(2)}) %collective-permute-start.8) | collective-permute-done | bytes 393248 | tf_op jit(solution)/shard_map/ppermute | solution.py:422
  69.5 0.0 collective-permute-start.9
  69.5 0.7 collective-permute-start.4
  70.2 5.2 %collective-permute-done.4 = bf16[128,512]{1,0:T(8,128)(2,1)S(1)} collective-permute-done((bf16[128,512]{1,0:T(8,128)(2,1)S(1)}, bf16[128,512]{1,0:T(8,128)(2,1)S(1)}, u32[]{:S(2)}, u32[]{:S(2)}) %collective-permute-start.4) | collective-permute-done | bytes 131104 | tf_op jit(solution)/shard_map/ppermute | solution.py:422
  75.5 0.0 copy-done.2
  75.5 1.0 %fusion = f32[128,512]{1,0:T(8,128)} fusion(bf16[512,512]{1,0:T(8,128)(2,1)S(1)} %copy-done.2, f32[128,512]{1,0:T(8,128)S(1)} %get-tuple-element.36, bf16[128,512]{1,0:T(8,128)(2,1)S(1)} %collective-permute-done.4), kind=kOutput, calls=%fused_computation.1 | convolution fusion | flops 67305472 | bytes 1179648 | tf_op jit(solution)/shard_map/dot_general | solution.py:33
  76.5 0.0 collective-permute-done.7.refs_1_
  76.5 0.0 collective-permute-done.9.refs_3_
  76.5 2.0 %spread_weights.1 = (bf16[512,512]{1,0:T(8,128)(2,1)}, bf16[512,512]{1,0:T(8,128)(2,1)}, bf16[512,512]{1,0:T(8,128)(2,1)}) custom-call(s32[3]{0:T(128)S(1)} %pad_add_fusion.place_ref, bf16[8,192,128]{2,1,0:T(8,128)(2,1)S(1)} %all_to_all.10.refs_0_, bf16[8,192,128]{2,1,0:T(8,128)(2,1)S(1)} %collective-permute-done.7.refs_1_, ...), custom_call_target="tpu_custom_call" | custom-call | flops 134217728 | bytes 2097152 | tf_op jit(solution)/shard_map/spread_weights/pallas_call | solution.py:409
Async XLA Ops:
  0.6 8.4 %collective-permute-start.1 = (bf16[8,512]{1,0:T(8,128)(2,1)}, bf16[8,512]{1,0:T(8,128)(2,1)S(1)}, u32[]{:S(2)}, u32[]{:S(2)}) collective-permute-start(bf16[8,512]{1,0:T(8,128)(2,1)} %bitcast.10), channel_id=1, source_target_pairs={{4,8},{12,16},{20,24},{8,4},{16,12},{24,20},{0,0},{28,28},{5,9},{1... | collective-permute-start | bytes 24584 | tf_op jit(solution)/shard_map/ppermute | solution.py:429
  2.0 7.0 %collective-permute-start = (bf16[8,512]{1,0:T(8,128)(2,1)}, bf16[8,512]{1,0:T(8,128)(2,1)S(1)}, u32[]{:S(2)}, u32[]{:S(2)}) collective-permute-start(bf16[8,512]{1,0:T(8,128)(2,1)} %bitcast.11), channel_id=1, source_target_pairs={{0,4},{4,0},{8,12},{12,8},{16,20},{20,16},{24,28},{28,24},{1,5},{5... | collective-permute-start | bytes 24584 | tf_op jit(solution)/shard_map/ppermute | solution.py:422
  20.2 2.4 %collective-permute-start.2 = (bf16[520,512]{1,0:T(8,128)(2,1)S(1)}, bf16[520,512]{1,0:T(8,128)(2,1)S(1)}, u32[]{:S(2)}, u32[]{:S(2)}) collective-permute-start(bf16[520,512]{1,0:T(8,128)(2,1)S(1)} %get-tuple-element.33), channel_id=1, source_target_pairs={{0,1},{1,0},{2,3},{3,2},{4,5},{5,4},{6,7},{7,6},{8,9},{9,8},{10,11... | collective-permute-start | bytes 1597448 | tf_op jit(solution)/shard_map/ppermute | solution.py:422
  20.3 2.3 %collective-permute-start.3 = (bf16[2,128,512]{2,1,0:T(8,128)(2,1)S(1)}, bf16[2,128,512]{2,1,0:T(8,128)(2,1)S(1)}, u32[]{:S(2)}, u32[]{:S(2)}) collective-permute-start(bf16[2,128,512]{2,1,0:T(8,128)(2,1)S(1)} %get-tuple-element.35), channel_id=1, source_target_pairs={{0,1},{1,0},{2,3},{3,2},{4,5},{5,4},{6,7},{7,6},{8,9},{9,8},{10,11... | collective-permute-start | bytes 786440 | tf_op jit(solution)/shard_map/ppermute | solution.py:422
  23.5 22.4 %copy-start = (bf16[512,512]{1,0:T(8,128)(2,1)S(1)}, bf16[512,512]{1,0:T(8,128)(2,1)}, u32[]{:S(2)}) copy-start(bf16[512,512]{1,0:T(8,128)(2,1)} %wsend_ref.1) | copy-start | bytes 1572868
  23.5 22.4 %copy-start.1 = (bf16[1,8,512]{2,1,0:T(8,128)(2,1)S(1)}, bf16[1,8,512]{2,1,0:T(8,128)(2,1)}, u32[]{:S(2)}) copy-start(bf16[1,8,512]{2,1,0:T(8,128)(2,1)} %param.12) | copy-start | bytes 24580
  23.5 22.4 %all-to-all-start = ((bf16[16,136,128]{2,1,0:T(8,128)(2,1)}), bf16[16,136,128]{2,1,0:T(8,128)(2,1)S(1)}, u32[]{:S(2)}, u32[]{:S(2)}) async-start(bf16[16,136,128]{2,1,0:T(8,128)(2,1)} %get-tuple-element.38), calls=%async_computation | async-start | bytes 1114112 | tf_op jit(solution)/shard_map/all_to_all | solution.py:478
  30.0 45.5 %copy-start.2 = (bf16[512,512]{1,0:T(8,128)(2,1)S(1)}, bf16[512,512]{1,0:T(8,128)(2,1)}, u32[]{:S(2)}) copy-start(bf16[512,512]{1,0:T(8,128)(2,1)} %refs_1_.1) | copy-start | bytes 1572868
  30.0 5.9 %collective-permute-start.5 = (f32[8,512]{1,0:T(8,128)S(1)}, f32[8,512]{1,0:T(8,128)S(1)}, u32[]{:S(2)}, u32[]{:S(2)}) collective-permute-start(f32[8,512]{1,0:T(8,128)S(1)} %get-tuple-element.40), channel_id=1, source_target_pairs={{0,4},{4,0},{8,12},{12,8},{16,20},{20,16},{24,28},{28,24},{1,5},{5... | collective-permute-start | bytes 49160 | tf_op jit(solution)/shard_map/ppermute | solution.py:422
  32.0 3.9 %collective-permute-start.6 = (f32[8,512]{1,0:T(8,128)S(1)}, f32[8,512]{1,0:T(8,128)S(1)}, u32[]{:S(2)}, u32[]{:S(2)}) collective-permute-start(f32[8,512]{1,0:T(8,128)S(1)} %get-tuple-element.41), channel_id=1, source_target_pairs={{4,8},{12,16},{20,24},{8,4},{16,12},{24,20},{0,0},{28,28},{5,9},{1... | collective-permute-start | bytes 49160 | tf_op jit(solution)/shard_map/ppermute | solution.py:429
  61.8 7.8 %collective-permute-start.8 = (bf16[8,192,128]{2,1,0:T(8,128)(2,1)S(1)}, bf16[8,192,128]{2,1,0:T(8,128)(2,1)S(1)}, u32[]{:S(2)}, u32[]{:S(2)}) collective-permute-start(bf16[8,192,128]{2,1,0:T(8,128)(2,1)S(1)} %all_to_all.10.refs_0_), channel_id=1, source_target_pairs={{0,2},{2,0},{1,3},{3,1},{4,6},{6,4},{5,7},{7,5},{8,10},{10,8},{9,1... | collective-permute-start | bytes 1179656 | tf_op jit(solution)/shard_map/ppermute | solution.py:422
  62.5 14.0 %collective-permute-start.7 = (bf16[8,192,128]{2,1,0:T(8,128)(2,1)S(1)}, bf16[8,192,128]{2,1,0:T(8,128)(2,1)S(1)}, u32[]{:S(2)}, u32[]{:S(2)}) collective-permute-start(bf16[8,192,128]{2,1,0:T(8,128)(2,1)S(1)} %all_to_all.10.refs_0_), channel_id=1, source_target_pairs={{0,1},{1,0},{2,3},{3,2},{4,5},{5,4},{6,7},{7,6},{8,9},{9,8},{10,11... | collective-permute-start | bytes 1179656 | tf_op jit(solution)/shard_map/ppermute | solution.py:422
  69.5 6.9 %collective-permute-start.9 = (bf16[8,192,128]{2,1,0:T(8,128)(2,1)S(1)}, bf16[8,192,128]{2,1,0:T(8,128)(2,1)S(1)}, u32[]{:S(2)}, u32[]{:S(2)}) collective-permute-start(bf16[8,192,128]{2,1,0:T(8,128)(2,1)S(1)} %collective-permute-done.8.refs_2_), channel_id=1, source_target_pairs={{0,1},{1,0},{2,3},{3,2},{4,5},{5,4},{6,7},{7,6},{8,9},{9,8},{10,11... | collective-permute-start | bytes 1179656 | tf_op jit(solution)/shard_map/ppermute | solution.py:422
  69.5 5.9 %collective-permute-start.4 = (bf16[128,512]{1,0:T(8,128)(2,1)S(1)}, bf16[128,512]{1,0:T(8,128)(2,1)S(1)}, u32[]{:S(2)}, u32[]{:S(2)}) collective-permute-start(bf16[128,512]{1,0:T(8,128)(2,1)S(1)} %get-tuple-element.37), channel_id=1, source_target_pairs={{0,2},{2,0},{1,3},{3,1},{4,6},{6,4},{5,7},{7,5},{8,10},{10,8},{9,1... | collective-permute-start | bytes 393224 | tf_op jit(solution)/shard_map/ppermute | solution.py:422
